TPU v7x, 256 devices: a whole 4x4x8 slice. The times are simulated.
256 devices in a mesh: row: 4 (over x), col: 16 (over z, core), depth: 4 (over y).
Axes of the slice: x: 4, y: 4, z: 8, core: 2. Of those that a mesh axis runs over, the one named last changes fastest.
Arguments:
- a_cols: float32 [32768, 1024], P(('row', 'col')), may hold values from -16 to 24, as said below
- past_panels: float32 [32768, 2048], P(('row', 'col'), 'depth'), may hold values from -1 to 1
Outputs:
- factor: float32 [32768, 1024], P(('row', 'col'))
Inputs may be any that keep to these rules, and one draw needn't show every extreme that they name: a_cols minus past_panels times the transpose of the top 1024 rows of past_panels is the first 1024 columns of a symmetric positive definite matrix whose top block has eigenvalues between 2 and 12.
All inputs are finite; a program needn't handle non-finite values.
Results may differ from a plain program's by a relative error of at most 0.0001.
Values sent between devices are 32-bit elements.
No kernel may reach another device: no remote copies, remote signals or barrier semaphores. Data moves between devices by JAX's collectives and lax.ppermute only.
A program may use at most 64 MiB of HBM per device.

v0:
```python
import jax
import jax.numpy as jnp
from jax import lax
from jax.sharding import Mesh
from jax.sharding import PartitionSpec as P

NB = 512
STEPS = 2
ROW_COL = ("row", "col_0", "col_1")


def spread(array, axis, root):
    mine = lax.axis_index(axis) == root
    return lax.psum(jnp.where(mine, array, jnp.zeros_like(array)), axis)


def rows_for(lines, size):
    spare = -lines.shape[0] % size
    if not spare:
        return lines
    return jnp.concatenate([lines, jnp.zeros((spare, *lines.shape[1:]), lines.dtype)])


def broadcast_by_parts(array, axis, root):
    lines = jnp.where(lax.axis_index(axis) == root, array, jnp.zeros_like(array)).reshape(
        -1, *array.shape[1:][-1:]
    )
    padded = rows_for(lines, lax.axis_size(axis))
    own = lax.psum_scatter(padded, axis, scatter_dimension=0, tiled=True)
    return lax.all_gather(own, axis, axis=0, tiled=True)[: len(lines)].reshape(array.shape)


def spread_2(array, axes, root):
    array = jnp.where(lax.axis_index(axes) == root, array, jnp.zeros_like(array))
    for axis in axes:
        array = lax.psum(array, axis)
    return array


def outer_rows(left, right):
    return lax.dot_general(
        left,
        right,
        (((1,), (1,)), ((), ())),
        precision=lax.Precision.HIGHEST,
        preferred_element_type=jnp.float32,
    )


def body(a_cols, past_panels):
    local_rows = a_cols.shape[0]
    position = lax.axis_index(ROW_COL)
    row_ids = position * local_rows + lax.broadcasted_iota(jnp.int32, (local_rows, NB), 0)
    col_ids = lax.broadcasted_iota(jnp.int32, (local_rows, NB), 1)
    result = jnp.zeros(a_cols.shape, jnp.float32)
    for section in range(STEPS):
        start = section * NB
        root = start // local_rows
        offset = start % local_rows
        above = spread(past_panels, ROW_COL, root)
        partial_value = outer_rows(past_panels, above)
        summed = lax.psum(partial_value, "depth")
        if section > 0:
            earlier = broadcast_by_parts(result[offset : offset + NB, :start], ROW_COL, root)
            summed = summed + outer_rows(result[:, :start], earlier)
        update = a_cols[:, start : start + NB] - summed
        block = spread_2(update, ROW_COL, root)
        diag_factor = jnp.linalg.cholesky(block)
        solved = jax.scipy.linalg.solve_triangular(diag_factor, update.T, lower=True).T
        new_panel = jnp.where(row_ids >= start + col_ids, solved, jnp.float32(0.0))
        result = result.at[:, start : start + NB].set(new_panel)
    return result


def solution(mesh):
    split = Mesh(
        mesh.devices.reshape(mesh.shape["row"], 8, 2, mesh.shape["depth"]),
        ("row", "col_0", "col_1", "depth"),
    )
    placed = (P(ROW_COL, None), P(ROW_COL, "depth"))
    return jax.shard_map(
        body, mesh=split, in_specs=placed, out_specs=P(ROW_COL, None), check_vma=False
    )
```

profile of v0, /device:TPU:1, one launch (start us, length us, event | category | flops | bytes accessed | tf_op | source)
XLA Modules:
  0.0 1128.0 jit_solution(7831291269363439358)
XLA Ops:
  6.5 1.6 copy.12
  8.1 1.7 broadcast_select_fusion.4
  9.9 193.3 %all-reduce.24.cloned.1.call-done = (f32[512,512]{0,1:T(8,128)}, f32[512,512]{0,1:T(8,128)}) async-done(((f32[512,512]{0,1:T(8,128)}, f32[512,512]{0,1:T(8,128)}), (f32[512,512]{0,1:T(8,128)}, f32[512,512]{0,1:T(8,128)})) %all-reduce.24.cloned.1.call-update) | async-done | bytes 2097168 | tf_op jit(solution)/shard_map/psum | solution.py:14
  203.2 5.8 convolution_bitcast_fusion
  209.0 4.5 convolution_bitcast_fusion.1
  213.6 1.2 fusion.67
  215.1 62.7 %all-reduce.26.cloned.1.call-done = (f32[512,512]{0,1:T(8,128)}, f32[512,512]{0,1:T(8,128)}) async-done(((f32[512,512]{0,1:T(8,128)}, f32[512,512]{0,1:T(8,128)}), (f32[512,512]{0,1:T(8,128)}, f32[512,512]{0,1:T(8,128)})) %all-reduce.26.cloned.1.call-update) | async-done | bytes 2097168 | tf_op jit(solution)/shard_map/psum | solution.py:62
  277.8 2.5 broadcast_select_fusion.3
  280.4 49.4 %all-reduce.12.cloned.1.call-done = f32[512,512]{0,1:T(8,128)} async-done(((f32[512,512]{0,1:T(8,128)}), f32[512,512]{0,1:T(8,128)}) %all-reduce.12.cloned.1.call-update) | async-done | bytes 1048592 | tf_op jit(solution)/shard_map/psum | solution.py:36
  329.8 76.5 %all-reduce.14.cloned.1.call-done = f32[512,512]{0,1:T(8,128)} async-done(((f32[512,512]{0,1:T(8,128)}), f32[512,512]{0,1:T(8,128)}) %all-reduce.14.cloned.1.call-update) | async-done | bytes 1048592 | tf_op jit(solution)/shard_map/psum | solution.py:36
  406.4 0.8 compare_reduce_fusion.8
  407.2 35.4 %all-reduce.16.cloned.1.call-done = f32[512,512]{0,1:T(8,128)} async-done(((f32[512,512]{0,1:T(8,128)}), f32[512,512]{0,1:T(8,128)}) %all-reduce.16.cloned.1.call-update) | async-done | bytes 1048592 | tf_op jit(solution)/shard_map/psum | solution.py:36
  442.6 1.6 copy.13
  444.5 1.0 copy-done.6
  445.5 11.7 %cholesky.286 = f32[128,128]{1,0:T(8,128)S(1)} custom-call(f32[128,128]{1,0:T(8,128)S(1)} %cholesky.426), custom_call_target="Cholesky" | custom-call | tf_op jit(solution)/shard_map/jit(cholesky)/cholesky | solution.py:68
  457.4 9.8 custom-call.27
  467.2 1.2 constant_dynamic-update-slice_fusion.5
  468.5 1.3 convolution_subtract_fusion.7
  469.7 11.7 %cholesky.305 = f32[128,128]{1,0:T(8,128)S(1)} custom-call(f32[128,128]{1,0:T(8,128)S(1)} %cholesky.430), custom_call_target="Cholesky" | custom-call | tf_op jit(solution)/shard_map/jit(cholesky)/cholesky | solution.py:68
  481.5 10.0 custom-call.28
  491.8 1.3 convolution_subtract_fusion.9
  493.1 11.7 %cholesky.326 = f32[128,128]{1,0:T(8,128)S(1)} custom-call(f32[128,128]{1,0:T(8,128)S(1)} %cholesky.435), custom_call_target="Cholesky" | custom-call | tf_op jit(solution)/shard_map/jit(cholesky)/cholesky | solution.py:68
  504.8 0.7 compare_reduce_fusion.5
  505.5 9.8 custom-call.29
  515.6 1.2 convolution_subtract_fusion.11
  516.8 11.7 %cholesky.343 = f32[128,128]{1,0:T(8,128)S(1)} custom-call(f32[128,128]{1,0:T(8,128)S(1)} %convolution_subtract_fusion.11), custom_call_target="Cholesky" | custom-call | tf_op jit(solution)/shard_map/jit(cholesky)/cholesky | solution.py:68
  532.9 8.2 while.6
  533.6 1.4 bitcast_dynamic-update-slice_fusion.4
  535.7 1.4 bitcast_dynamic-update-slice_fusion.4
  537.7 1.4 bitcast_dynamic-update-slice_fusion.4
  539.8 1.4 bitcast_dynamic-update-slice_fusion.4
  541.2 39.3 %custom-call.30 = f32[4,128,128]{1,2,0:T(8,128)S(1)} custom-call(f32[4,128,128]{2,1,0:T(8,128)S(1)} %get-tuple-element.45), custom_call_target="InvertDiagBlocksLowerTriangular" | custom-call | tf_op jit(solution)/shard_map/jit(_solve_triangular)/triangular_solve | solution.py:69
  583.6 0.9 broadcast_select_fusion.1
  584.5 1.4 copy.21
  586.0 135.8 %reduce-scatter.4.cloned.1.call-done = f32[8,512]{1,0:T(8,128)} async-done(((f32[512,512]{1,0:T(8,128)}), f32[8,512]{1,0:T(8,128)}) %reduce-scatter.4.cloned.1.call-update) | async-done | bytes 16400 | tf_op jit(solution)/shard_map/reduce_scatter | solution.py:29
  722.1 83.1 %all-gather.2.cloned.1.call-done = f32[512,512]{1,0:T(8,128)} async-done(((f32[8,512]{1,0:T(8,128)}), f32[512,512]{1,0:T(8,128)}) %all-gather.2.cloned.1.call-update) | async-done | bytes 1048592 | tf_op jit(solution)/shard_map/all_gather | solution.py:30
  805.2 4.8 broadcast_select_fusion
  810.1 46.9 %all-reduce.18.cloned.1.call-done = f32[512,512]{0,1:T(8,128)} async-done(((f32[512,512]{0,1:T(8,128)}), f32[512,512]{0,1:T(8,128)}) %all-reduce.18.cloned.1.call-update) | async-done | bytes 1048592 | tf_op jit(solution)/shard_map/psum | solution.py:36
  857.2 76.5 %all-reduce.20.cloned.1.call-done = f32[512,512]{0,1:T(8,128)} async-done(((f32[512,512]{0,1:T(8,128)}), f32[512,512]{0,1:T(8,128)}) %all-reduce.20.cloned.1.call-update) | async-done | bytes 1048592 | tf_op jit(solution)/shard_map/psum | solution.py:36
  933.7 36.2 %all-reduce.22.cloned.1.call-done = f32[512,512]{0,1:T(8,128)} async-done(((f32[512,512]{0,1:T(8,128)}), f32[512,512]{0,1:T(8,128)}) %all-reduce.22.cloned.1.call-update) | async-done | bytes 1048592 | tf_op jit(solution)/shard_map/psum | solution.py:36
  969.9 1.6 copy.18
  971.8 1.0 copy-done.5
  972.8 11.7 %cholesky.358 = f32[128,128]{1,0:T(8,128)S(1)} custom-call(f32[128,128]{1,0:T(8,128)S(1)} %cholesky.439), custom_call_target="Cholesky" | custom-call | tf_op jit(solution)/shard_map/jit(cholesky)/cholesky | solution.py:68
  984.7 9.8 custom-call.31
  994.5 1.2 constant_dynamic-update-slice_fusion.3
  995.7 1.3 convolution_subtract_fusion.6
  997.0 11.7 %cholesky.377 = f32[128,128]{1,0:T(8,128)S(1)} custom-call(f32[128,128]{1,0:T(8,128)S(1)} %cholesky.443), custom_call_target="Cholesky" | custom-call | tf_op jit(solution)/shard_map/jit(cholesky)/cholesky | solution.py:68
  1010.1 10.0 custom-call.32
  1020.4 1.3 convolution_subtract_fusion.8
  1021.7 11.7 %cholesky.398 = f32[128,128]{1,0:T(8,128)S(1)} custom-call(f32[128,128]{1,0:T(8,128)S(1)} %cholesky.448), custom_call_target="Cholesky" | custom-call | tf_op jit(solution)/shard_map/jit(cholesky)/cholesky | solution.py:68
  1034.1 9.8 custom-call.33
  1044.1 1.2 convolution_subtract_fusion.10
  1045.4 11.7 %cholesky.415 = f32[128,128]{1,0:T(8,128)S(1)} custom-call(f32[128,128]{1,0:T(8,128)S(1)} %convolution_subtract_fusion.10), custom_call_target="Cholesky" | custom-call | tf_op jit(solution)/shard_map/jit(cholesky)/cholesky | solution.py:68
  1060.3 1.4 select_select_fusion
  1061.7 11.7 %while.7 = (s32[]{:T(128)}, f32[512,512]{1,0:T(8,128)}, s32[4,2]{0,1:T(2,128)S(1)}, f32[4,128,128]{2,1,0:T(8,128)S(1)}, s32[]{:T(128)}) while((s32[]{:T(128)}, f32[512,512]{1,0:T(8,128)}, s32[4,2]{0,1:T(2,128)S(1)}, f32[4,128,128]{2,1,0:T(8,128)S(1)}, s32[]{:T(128)}) %tuple.92), condition=%wide.while_cond.2.clone, body=%wide.while_body.2.clone.sunk | while | flops 2 | bytes 131181 | solution.py:69
  1062.4 2.2 bitcast_dynamic-update-slice_fusion.5
  1065.3 2.2 bitcast_dynamic-update-slice_fusion.5
  1068.2 2.2 bitcast_dynamic-update-slice_fusion.5
  1071.2 2.2 bitcast_dynamic-update-slice_fusion.5
  1073.4 39.3 %custom-call.34 = f32[4,128,128]{1,2,0:T(8,128)S(1)} custom-call(f32[4,128,128]{2,1,0:T(8,128)S(1)} %get-tuple-element.46), custom_call_target="InvertDiagBlocksLowerTriangular" | custom-call | tf_op jit(solution)/shard_map/jit(_solve_triangular)/triangular_solve | solution.py:69
  1113.1 1.2 convolution_subtract_fusion.1
  1114.8 1.3 convolution_subtract_fusion
  1116.6 1.6 convolution_subtract_fusion.4
  1118.9 1.8 copy.19
  (102 shorter events, 18.4 us)
Async XLA Ops:
  6.5 196.7 %all-reduce.24.cloned.1.call-start = ((), (), s32[]{:S(2)}) async-start(), calls=%async_computation.9 | async-start | bytes 4194304 | tf_op jit(solution)/shard_map/psum | solution.py:14
  8.1 195.1 %copy-start = (f32[512,512]{1,0:T(8,128)S(1)}, f32[512,512]{1,0:T(8,128)}, u32[]{:S(2)}) copy-start(f32[512,512]{1,0:T(8,128)} %param.10) | copy-start | bytes 3145732
  9.8 268.0 %all-reduce.26.cloned.1.call-start = ((), (), s32[]{:S(2)}) async-start(), calls=%async_computation.10 | async-start | bytes 4194304 | tf_op jit(solution)/shard_map/psum | solution.py:62
  203.2 5.8 copy-start.8
  209.0 4.5 copy-start.7
  213.5 116.3 %all-reduce.12.cloned.1.call-start = ((), (), s32[]{:S(2)}) async-start(), calls=%async_computation.1 | async-start | bytes 2097152 | tf_op jit(solution)/shard_map/psum | solution.py:36
  280.3 126.0 %all-reduce.14.cloned.1.call-start = ((), (), s32[]{:S(2)}) async-start(), calls=%async_computation.2 | async-start | bytes 2097152 | tf_op jit(solution)/shard_map/psum | solution.py:36
  329.8 112.8 %all-reduce.16.cloned.1.call-start = ((), (), s32[]{:S(2)}) async-start(), calls=%async_computation.3 | async-start | bytes 2097152 | tf_op jit(solution)/shard_map/psum | solution.py:36
  406.4 315.3 %reduce-scatter.4.cloned.1.call-start = ((), (), s32[]{:S(2)}) async-start(), calls=%async_computation.8 | async-start | bytes 1064960 | tf_op jit(solution)/shard_map/reduce_scatter | solution.py:29
  442.6 1.7 copy-start.1
  444.5 1.0 copy-start.6
  584.5 137.3 %copy-start.4 = (f32[512,512]{1,0:T(8,128)S(1)}, f32[512,512]{1,0:T(8,128)}, u32[]{:S(2)}) copy-start(f32[512,512]{1,0:T(8,128)} %get-tuple-element.76) | copy-start | bytes 3145732
  585.9 219.3 %all-gather.2.cloned.1.call-start = ((), (), s32[]{:S(2)}) async-start(), calls=%async_computation.4 | async-start | bytes 1064960 | tf_op jit(solution)/shard_map/all_gather | solution.py:30
  721.7 135.2 %all-reduce.18.cloned.1.call-start = ((), (), s32[]{:S(2)}) async-start(), calls=%async_computation.5 | async-start | bytes 2097152 | tf_op jit(solution)/shard_map/psum | solution.py:36
  810.0 123.7 %all-reduce.20.cloned.1.call-start = ((), (), s32[]{:S(2)}) async-start(), calls=%async_computation.6 | async-start | bytes 2097152 | tf_op jit(solution)/shard_map/psum | solution.py:36
  857.0 113.0 %all-reduce.22.cloned.1.call-start = ((), (), s32[]{:S(2)}) async-start(), calls=%async_computation.7 | async-start | bytes 2097152 | tf_op jit(solution)/shard_map/psum | solution.py:36
  969.9 1.7 copy-start.2
  971.8 1.0 copy-start.5
  1021.7 91.0 %copy-start.3 = (f32[512,512]{0,1:T(8,128)S(1)}, f32[512,512]{0,1:T(8,128)}, u32[]{:S(2)}) copy-start(f32[512,512]{0,1:T(8,128)} %get-tuple-element.102) | copy-start | bytes 3145732
Sparse Core Ops, SparseCore 0:
  10.9 192.2 all-reduce.23
  213.6 64.1 all-reduce.25
  280.4 49.2 all-reduce.11
  332.0 74.3 all-reduce.13
  408.8 33.7 all-reduce.15
  586.0 135.6 reduce-scatter.3
  724.5 80.7 all-gather.1
  810.1 46.7 all-reduce.17
  859.3 74.3 all-reduce.19
  936.1 33.7 all-reduce.21
where the time goes:
time: 1130 us
  waiting for transfers between devices  796 us (70%)
  other arithmetic  245 us (22%)
  matrix products  34.8 us (3%)
  local copies, waits for them, and re-layouts  32 us (3%)
  between operations  19.5 us (2%)
    psum x6, waiting for transfers between devices, spread_2(): array = lax.psum(array, axis)  321 us
    psum x1, waiting for transfers between devices, spread(): return lax.psum(jnp.where(mine, array, jnp.zeros_like(array)), axis)  193 us
    another operation x29, other arithmetic, body(): diag_factor = jnp.linalg.cholesky(block)  158 us
    reduce_scatter x1, waiting for transfers between devices, broadcast_by_parts(): own = lax.psum_scatter(padded, axis, scatter_dimension=0, tiled=True)  136 us
    all_gather x1, waiting for transfers between devices, broadcast_by_parts(): lax.all_gather(own, axis, axis=0, tiled=True)[:len(lines)]  83.1 us
    another operation x5, other arithmetic, body(): jax.scipy.linalg.solve_triangular(diag_factor, update.T, lower=True)  80.5 us
    psum x1, waiting for transfers between devices, body(): summed = lax.psum(partial_value, 'depth')  62.7 us
  transfers between devices with their start and end apart: 10, of which 10 were waited for; matrix products, arithmetic and copies ran while one was open for 0% of the time, Pallas kernels for 0%

commit v1 on v0

v1 whole, which is shorter than its diff:
```python
import jax, jax.numpy as jnp
from jax import lax
from jax.experimental import pallas as pl
from jax.experimental.pallas import tpu as pltpu
NB=512
H=256
CENTRE, RADIUS = 7.0, 5.0
CHEB = 6
NEWTON = 2

def dims(ta, tb):
    return (((0 if ta else 1,), (1 if tb else 0,)), ((), ()))

def dot1(a, b, ta=False, tb=False):
    return lax.dot_general(a, b, dims(ta, tb), preferred_element_type=jnp.float32)

def split(a):
    hi = a.astype(jnp.bfloat16)
    return hi, (a - hi.astype(jnp.float32)).astype(jnp.bfloat16)

def dot3(a, b, ta=False, tb=False):
    (ah, al), (bh, bl) = a, b
    return dot1(ah, bh, ta, tb) + (dot1(ah, bl, ta, tb) + dot1(al, bh, ta, tb))

def tri(n, strict=False):
    r = lax.broadcasted_iota(jnp.int32, (n, n), 0)
    c = lax.broadcasted_iota(jnp.int32, (n, n), 1)
    return (r > c) if strict else (r >= c)

def eye(n):
    r = lax.broadcasted_iota(jnp.int32, (n, n), 0)
    c = lax.broadcasted_iota(jnp.int32, (n, n), 1)
    return (r == c)

def inverse_factor(a00, a10, a11):
    b = jnp.bfloat16
    low, ident = tri(H), eye(H).astype(jnp.float32)
    h00, h10, h11 = split(a00), split(a10), split(a11)
    b00, b10, b11 = h00[0], h10[0], h11[0]
    sigma = CENTRE / RADIUS
    rho = 1.0 / sigma
    d00 = ident * (1.0 / CENTRE); d11 = d00; d10 = jnp.zeros((H, H), jnp.float32)
    y00, y10, y11 = d00, d10, d11
    zero = jnp.zeros((H, H), jnp.float32)
    r00 = ident - jnp.where(low, a00, 0.0) * (1.0 / CENTRE)
    r10 = -a10 * (1.0 / CENTRE)
    r11 = ident - jnp.where(low, a11, 0.0) * (1.0 / CENTRE)
    for k in range(CHEB):
        nxt = 1.0 / (2.0 * sigma - rho)
        p, q = nxt * rho, 2.0 * nxt / RADIUS
        rho = nxt
        d00, d10, d11 = p * d00 + q * r00, p * d10 + q * r10, p * d11 + q * r11
        y00, y10, y11 = y00 + d00, y10 + d10, y11 + d11
        if k < CHEB - 1:
            v00, v10, v11 = y00.astype(b), y10.astype(b), y11.astype(b)
            r00 = ident - jnp.where(low, dot1(v00, b00), 0.0)
            r10 = -(dot1(v10, b00) + dot1(v11, b10))
            r11 = ident - jnp.where(low, dot1(v10, b10, False, True) + dot1(v11, b11), 0.0)
    s0 = lax.rsqrt(jnp.sum(y00 * ident, axis=1, keepdims=True))
    s1 = lax.rsqrt(jnp.sum(y11 * ident, axis=1, keepdims=True))
    x00, x10, x11 = y00 * s0, y10 * s1, y11 * s1
    half = jnp.where(tri(H, True), 1.0, 0.5 * ident)
    for k in range(NEWTON):
        t00, t10, t11 = split(x00), split(x10), split(x11)
        w00 = split(dot3(t00, h00))
        w10 = split(dot3(t10, h00) + dot3(t11, h10))
        w11 = split(dot3(t10, h10, False, True) + dot3(t11, h11))
        e00 = ((dot3(w00, t00, False, True) - ident) * half).astype(b)
        e10 = dot3(w10, t00, False, True).astype(b)
        e11 = ((dot3(w10, t10, False, True) + dot3(w11, t11, False, True) - ident) * half).astype(b)
        x10 = x10 - (dot1(e10, t00[0]) + dot1(e11, t10[0]))
        x00 = x00 - dot1(e00, t00[0])
        x11 = x11 - dot1(e11, t11[0])
    return x00, x10, x11

def factor_kernel(m0, m1, x_ref, l_ref):
    def put(i, x00, x10, x11):
        x_ref[i, :H, :H] = x00
        x_ref[i, :H, H:] = jnp.zeros((H, H), jnp.float32)
        x_ref[i, H:, :H] = x10
        x_ref[i, H:, H:] = x11
    x00, x10, x11 = inverse_factor(m0[:H, :H], m0[H:, :H], m0[H:, H:NB])
    put(0, x00, x10, x11)
    t00, t10, t11 = split(x00), split(x10), split(x11)
    for j, m in enumerate((m0, m1)):
        top, bot = split(m[:H, NB:]), split(m[H:, NB:])
        l_ref[:H, j * H:(j + 1) * H] = dot3(t00, top)
        l_ref[H:, j * H:(j + 1) * H] = dot3(t10, top) + dot3(t11, bot)
    p0, p1 = split(l_ref[:, :H]), split(l_ref[:, H:])
    c00 = m1[:H, :H] - dot3(p0, p0, True, False)
    c10 = m1[H:, :H] - dot3(p1, p0, True, False)
    c11 = m1[H:, H:NB] - dot3(p1, p1, True, False)
    put(1, *inverse_factor(c00, c10, c11))

def factor(m0, m1):
    return pl.pallas_call(
        factor_kernel,
        out_shape=(jax.ShapeDtypeStruct((2, NB, NB), jnp.float32), jax.ShapeDtypeStruct((NB, NB), jnp.float32)),
        in_specs=[pl.BlockSpec(memory_space=pltpu.VMEM)] * 2,
        out_specs=(pl.BlockSpec(memory_space=pltpu.VMEM),) * 2,
        cost_estimate=pl.CostEstimate(flops=2 * 10**10, bytes_accessed=2**23, transcendentals=0),
        name="factor",
    )(m0, m1)


from jax.sharding import Mesh
from jax.sharding import PartitionSpec as P

ROW_COL = ("row", "col_0", "col_1")
PLANE = ("row", "col_0")


def outer_rows(left, right):
    return lax.dot_general(
        left, right, (((1,), (1,)), ((), ())), precision=lax.Precision.HIGH, preferred_element_type=jnp.float32
    )


def swap_core(v):
    return lax.ppermute(v, "col_1", [(0, 1), (1, 0)])


def exchange(v, axis, size, bits):
    return lax.ppermute(v, axis, [(i, i ^ bits) for i in range(size)])


def in_order(pieces, me):
    low, high = (me & 1) == 1, (me >> 1) == 1
    p0, p1, p2, p3 = pieces
    p0, p1 = jnp.where(low, p1, p0), jnp.where(low, p0, p1)
    p2, p3 = jnp.where(low, p3, p2), jnp.where(low, p2, p3)
    p0, p2 = jnp.where(high, p2, p0), jnp.where(high, p0, p2)
    p1, p3 = jnp.where(high, p3, p1), jnp.where(high, p1, p3)
    return jnp.concatenate([p0, p1, p2, p3])


def gather_four(v, axis):
    return in_order([v] + [exchange(v, axis, 4, s) for s in (1, 2, 3)], lax.axis_index(axis))


def chunk_of(v, j):
    n = v.shape[0] // 4
    return lax.dynamic_slice_in_dim(v, j * n, n)


def scatter_sum(v, axis):
    me = lax.axis_index(axis)
    total = chunk_of(v, me)
    for s in (1, 2, 3):
        total = total + exchange(chunk_of(v, me ^ s), axis, 4, s)
    return total


def broadcast_plane(v):
    x, z = lax.axis_index("row"), lax.axis_index("col_0")
    n = v.shape[0] // 4
    mine = jnp.where((x == 0) & (z == 0), v[:n], 0.0)
    for p in (1, 2, 3):
        mine = mine + lax.ppermute(v[p * n : (p + 1) * n], PLANE, [(0, 8 * p)])
    got = jnp.where(z == 0, mine, 0.0)
    for p in (4, 2, 6):
        got = got + lax.ppermute(mine, "col_0", [(0, p)])
    odd = lax.ppermute(got, "col_0", [(0, 1), (2, 3), (4, 5), (6, 7)])
    got = jnp.where(z % 2 == 0, got, odd)
    return gather_four(got, "row")


def body(a_cols, past):
    core, y = lax.axis_index("col_1"), lax.axis_index("depth")
    first = core == 0

    other = swap_core(past)
    diag = outer_rows(past, past)
    side = outer_rows(jnp.where(first, past, other), jnp.where(first, other[:H], past[H:]))
    a_diag = jnp.where(first, a_cols[:, :NB], a_cols[:, NB:])
    a_side = jnp.where(first, a_cols[:, NB : NB + H], a_cols[H:, :NB].T)
    block = chunk_of(jnp.concatenate([a_diag, a_side], 1), y) - scatter_sum(
        jnp.concatenate([diag, side], 1), "depth"
    )

    top = broadcast_plane(past)
    top_other = swap_core(top)

    block = gather_four(broadcast_plane(block), "depth")
    block_other = swap_core(block)
    inverse, below = factor(
        jnp.where(first, block, block_other), jnp.where(first, block_other, block)
    )

    partial_value = jnp.concatenate([outer_rows(past, top), outer_rows(past, top_other)], 1)
    a_turned = jnp.concatenate([a_diag, jnp.where(first, a_cols[:, NB:], a_cols[:, :NB])], 1)
    update = gather_four(chunk_of(a_turned, y) - scatter_sum(partial_value, "depth"), "depth")
    update_1 = jnp.where(first, update[:, :NB], update[:, NB:])
    update_2 = jnp.where(first, update[:, NB:], update[:, :NB])
    out_1 = outer_rows(update_1, inverse[0])
    rest = update_2 - lax.dot_general(
        out_1, below, (((1,), (0,)), ((), ())), precision=lax.Precision.HIGH, preferred_element_type=jnp.float32
    )
    out_2 = outer_rows(rest, inverse[1])
    out = jnp.concatenate([out_1, out_2], 1)
    rows = lax.axis_index(ROW_COL) * out.shape[0] + lax.broadcasted_iota(jnp.int32, out.shape, 0)
    return jnp.where(rows >= lax.broadcasted_iota(jnp.int32, out.shape, 1), out, 0.0)


def solution(mesh):
    split_mesh = Mesh(
        mesh.devices.reshape(mesh.shape["row"], 8, 2, mesh.shape["depth"]),
        ("row", "col_0", "col_1", "depth"),
    )
    placed = (P(ROW_COL, None), P(ROW_COL, "depth"))
    return jax.shard_map(
        body, mesh=split_mesh, in_specs=placed, out_specs=P(ROW_COL, None), check_vma=False
    )
```

time: 1130 us -> 185 us (0.16)
  waiting for transfers between devices: 796 us -> 84.6 us
  other arithmetic: 245 us -> 9.86 us
  starting transfers between devices: 0.54 us -> 56.5 us
  local copies, waits for them, and re-layouts: 32 us -> 6.65 us
  matrix products: 34.8 us -> 11.9 us
  between operations: 19.5 us -> 0.58 us
  Pallas kernels: 0 us -> 12.8 us
    psum x8 -> x0, waiting for transfers between devices: 577 us -> none  [the longest x6 321 us: spread_2(): array = lax.psum(array, axis)]
    another operation x35 -> x0, other arithmetic: 239 us -> none  [the longest x29 158 us: body(): diag_factor = jnp.linalg.cholesky(block)]
    reduce_scatter x1 -> x0, waiting for transfers between devices: 136 us -> none  [broadcast_by_parts(): own = lax.psum_scatter(padded, axis, scatter_dimension=0, tiled=True)]
    ppermute x0 -> x35, waiting for transfers between devices: none -> 84.6 us  [the longest x18 70.1 us: exchange(): return lax.ppermute(v, axis, [(i, i ^ bits) for i in range(size)])]
    all_gather x1 -> x0, waiting for transfers between devices: 83.1 us -> none  [broadcast_by_parts(): lax.all_gather(own, axis, axis=0, tiled=True)[:len(lines)]]
    ppermute x0 -> x35, starting transfers between devices: none -> 56.5 us  [the longest x18 20.9 us: exchange(): return lax.ppermute(v, axis, [(i, i ^ bits) for i in range(size)])]
    another operation x35 -> x0, local copies, waits for them, and re-layouts: 20.1 us -> none  [the longest x27 19.8 us: body(): jax.scipy.linalg.solve_triangular(diag_factor, update.T, lower=True)]
    another operation x26 -> x0, matrix products: 19.8 us -> none  [the longest x12 10.9 us: body(): diag_factor = jnp.linalg.cholesky(block)]
  transfers between devices with their start and end apart: 10 -> 35, of which waited for: 10 -> 15; matrix products, arithmetic and copies ran while one was open for 0% -> 9% of each run, Pallas kernels for 0% -> 0%
where the time goes in v1:
time: 185 us; the launch traced here: 183 us
  waiting for transfers between devices  84.6 us (46%)
  starting transfers between devices  56.5 us (31%)
  Pallas kernels  12.8 us (7%)
  matrix products  11.9 us (6%)
  other arithmetic  9.86 us (5%)
  local copies, waits for them, and re-layouts  6.65 us (4%)
    ppermute x18, waiting for transfers between devices, exchange(): return lax.ppermute(v, axis, [(i, i ^ bits) for i in range(size)])  70.1 us
    ppermute x18, starting transfers between devices, exchange(): return lax.ppermute(v, axis, [(i, i ^ bits) for i in range(size)])  20.9 us
    pallas_call x1, Pallas kernels, factor(): pl.pallas_call(factor_kernel, out_shape=(jax.ShapeDtypeStruct((2, NB, NB)...  12.8 us
    ppermute x6, starting transfers between devices, broadcast_plane(): mine = mine + lax.ppermute(v[p * n:(p + 1) * n], PLANE, [(0, 8 * p)])  12.5 us
    ppermute x3, starting transfers between devices, swap_core(): return lax.ppermute(v, 'col_1', [(0, 1), (1, 0)])  12 us
    dot_general x6, matrix products, outer_rows(): lax.dot_general(left, right, (((1,), (1,)), ((), ())), precision=lax.Prec...  10.9 us
    ppermute x6, starting transfers between devices, broadcast_plane(): got = got + lax.ppermute(mine, 'col_0', [(0, p)])  7.8 us
    ppermute x6, waiting for transfers between devices, broadcast_plane(): got = got + lax.ppermute(mine, 'col_0', [(0, p)])  7.7 us
  transfers between devices with their start and end apart: 35, of which 15 were waited for; matrix products, arithmetic and copies ran while one was open for 9% of the time, Pallas kernels for 0%

profile of v1, /device:TPU:1, one launch (start us, length us, event | category | flops | bytes accessed | tf_op | source)
XLA Modules:
  0.0 182.9 jit_solution(5672188007933252968)
XLA Ops:
  0.0 3.2 %collective-permute-start.17 = (f32[512,512]{1,0:T(8,128)}, f32[512,512]{1,0:T(8,128)}, u32[]{:S(2)}, u32[]{:S(2)}) collective-permute-start(f32[512,512]{1,0:T(8,128)} %param.3), channel_id=1, source_target_pairs={{0,4},{4,0},{1,5},{5,1},{2,6},{6,2},{3,7},{7,3},{8,12},{12,8},{9,1... | collective-permute-start | bytes 3145736 | tf_op jit(solution)/shard_map/ppermute | solution.py:120
  3.2 1.2 fusion.41
  4.4 1.4 collective-permute-start
  5.8 2.2 %collective-permute-start.1 = (f32[128,512]{1,0:T(8,128)S(1)}, f32[128,512]{1,0:T(8,128)S(1)}, u32[]{:S(2)}, u32[]{:S(2)}) collective-permute-start(f32[128,512]{1,0:T(8,128)S(1)} %get-tuple-element.32), channel_id=1, source_target_pairs={{0,128},{1,129},{2,130},{3,131},{4,132},{5,133},{6,134},{7,135}} | collective-permute-start | bytes 786440 | tf_op jit(solution)/shard_map/ppermute | solution.py:159
  8.0 1.3 collective-permute-start.2
  9.4 1.1 slice.67
  10.5 1.0 copy.13
  11.5 1.0 fusion.43
  12.5 4.5 %collective-permute-done.1 = f32[128,512]{1,0:T(8,128)S(1)} collective-permute-done((f32[128,512]{1,0:T(8,128)S(1)}, f32[128,512]{1,0:T(8,128)S(1)}, u32[]{:S(2)}, u32[]{:S(2)}) %collective-permute-start.1) | collective-permute-done | bytes 262176 | tf_op jit(solution)/shard_map/ppermute | solution.py:159
  17.0 1.3 collective-permute-start.3
  18.4 1.3 collective-permute-start.4
  19.7 1.3 collective-permute-start.5
  21.0 0.2 slice_select_fusion
  21.3 2.1 %collective-permute-done.3 = f32[128,512]{1,0:T(8,128)S(1)} collective-permute-done((f32[128,512]{1,0:T(8,128)S(1)}, f32[128,512]{1,0:T(8,128)S(1)}, u32[]{:S(2)}, u32[]{:S(2)}) %collective-permute-start.3) | collective-permute-done | bytes 262176 | tf_op jit(solution)/shard_map/ppermute | solution.py:162
  23.3 5.6 %collective-permute-done.4 = f32[128,512]{1,0:T(8,128)S(1)} collective-permute-done((f32[128,512]{1,0:T(8,128)S(1)}, f32[128,512]{1,0:T(8,128)S(1)}, u32[]{:S(2)}, u32[]{:S(2)}) %collective-permute-start.4) | collective-permute-done | bytes 262176 | tf_op jit(solution)/shard_map/ppermute | solution.py:162
  29.0 1.3 collective-permute-start.6
  30.4 2.0 %fusion.8 = f32[512,256]{1,0:T(8,128)S(1)} fusion(f32[512,512]{1,0:T(8,128)S(1)} %copy-done, f32[512,512]{1,0:T(8,128)} %collective-permute-done.17, pred[]{:T(512)S(6)} %eq.36), kind=kOutput, calls=%fused_computation.35 | convolution fusion | flops 403046400 | bytes 3671040 | tf_op jit(solution)/shard_map/dot_general | solution.py:114
  32.5 1.4 collective-permute-start.18
  33.8 2.6 %collective-permute-start.19 = (f32[128,768]{1,0:T(8,128)S(1)}, f32[128,768]{1,0:T(8,128)S(1)}, u32[]{:S(2)}, u32[]{:S(2)}) collective-permute-start(f32[128,768]{1,0:T(8,128)S(1)} %get-tuple-element.24), channel_id=1, source_target_pairs={{0,2},{1,3},{2,0},{3,1},{4,6},{5,7},{6,4},{7,5},{8,10},{9,11},{10,... | collective-permute-start | bytes 1179656 | tf_op jit(solution)/shard_map/ppermute | solution.py:124
  36.6 1.4 collective-permute-start.7
  38.0 2.5 %collective-permute-start.8 = (f32[128,512]{1,0:T(8,128)S(1)}, f32[128,512]{1,0:T(8,128)S(1)}, u32[]{:S(2)}, u32[]{:S(2)}) collective-permute-start(f32[128,512]{1,0:T(8,128)S(1)} %broadcast_select_fusion.18), channel_id=1, source_target_pairs={{0,128},{64,192},{128,0},{192,64},{1,129},{65,193},{129,1},{193,65... | collective-permute-start | bytes 786440 | tf_op jit(solution)/shard_map/ppermute | solution.py:124
  40.5 1.5 collective-permute-done.18
  42.0 0.8 collective-permute-start.9
  42.8 10.1 %collective-permute-done.19 = f32[128,768]{1,0:T(8,128)S(1)} collective-permute-done((f32[128,768]{1,0:T(8,128)S(1)}, f32[128,768]{1,0:T(8,128)S(1)}, u32[]{:S(2)}, u32[]{:S(2)}) %collective-permute-start.19) | collective-permute-done | bytes 393248 | tf_op jit(solution)/shard_map/ppermute | solution.py:124
  52.9 2.1 %collective-permute-done.20 = f32[128,768]{1,0:T(8,128)S(1)} collective-permute-done((f32[128,768]{1,0:T(8,128)S(1)}, f32[128,768]{1,0:T(8,128)S(1)}, u32[]{:S(2)}, u32[]{:S(2)}) %collective-permute-start.20) | collective-permute-done | bytes 393248 | tf_op jit(solution)/shard_map/ppermute | solution.py:124
  55.2 2.7 %collective-permute-start.21 = (f32[32,768]{1,0:T(8,128)S(1)}, f32[32,768]{1,0:T(8,128)S(1)}, u32[]{:S(2)}, u32[]{:S(2)}) collective-permute-start(f32[32,768]{1,0:T(8,128)S(1)} %get-tuple-element.37), channel_id=1, source_target_pairs={{0,64},{1,65},{2,66},{3,67},{4,68},{5,69},{6,70},{7,71}} | collective-permute-start | bytes 294920 | tf_op jit(solution)/shard_map/ppermute | solution.py:159
  57.9 3.5 %collective-permute-start.22 = (f32[32,768]{1,0:T(8,128)S(1)}, f32[32,768]{1,0:T(8,128)S(1)}, u32[]{:S(2)}, u32[]{:S(2)}) collective-permute-start(f32[32,768]{1,0:T(8,128)S(1)} %get-tuple-element.39), channel_id=1, source_target_pairs={{0,128},{1,129},{2,130},{3,131},{4,132},{5,133},{6,134},{7,135}} | collective-permute-start | bytes 294920 | tf_op jit(solution)/shard_map/ppermute | solution.py:159
  61.5 1.3 collective-permute-start.23
  63.1 1.3 collective-permute-done.23
  64.4 1.3 collective-permute-start.24
  65.7 1.3 collective-permute-start.25
  67.0 1.3 collective-permute-start.26
  68.4 1.0 pad_maximum_fusion.2
  69.4 3.5 %collective-permute-start.10 = (f32[512,512]{1,0:T(8,128)}, f32[512,512]{1,0:T(8,128)}, u32[]{:S(2)}, u32[]{:S(2)}) collective-permute-start(f32[512,512]{1,0:T(8,128)} %pad_maximum_fusion.2), channel_id=1, source_target_pairs={{0,4},{4,0},{1,5},{5,1},{2,6},{6,2},{3,7},{7,3},{8,12},{12,8},{9,1... | collective-permute-start | bytes 3145736 | tf_op jit(solution)/shard_map/ppermute | solution.py:120
  72.9 1.9 %collective-permute-start.27 = (f32[32,768]{1,0:T(8,128)S(1)}, f32[32,768]{1,0:T(8,128)}, u32[]{:S(2)}, u32[]{:S(2)}) collective-permute-start(f32[32,768]{1,0:T(8,128)S(1)} %add_add_fusion.2), channel_id=1, source_target_pairs={{0,8},{16,24},{32,40},{48,56},{1,9},{17,25},{33,41},{49,57},{2,10}... | collective-permute-start | bytes 294920 | tf_op jit(solution)/shard_map/ppermute | solution.py:163
  74.9 1.0 collective-permute-done.27
  75.9 3.4 %collective-permute-start.28 = (f32[32,768]{1,0:T(8,128)S(1)}, f32[32,768]{1,0:T(8,128)S(1)}, u32[]{:S(2)}, u32[]{:S(2)}) collective-permute-start(f32[32,768]{1,0:T(8,128)S(1)} %broadcast_select_fusion.27), channel_id=1, source_target_pairs={{0,192},{64,128},{128,64},{192,0},{1,193},{65,129},{129,65},{193,1... | collective-permute-start | bytes 294920 | tf_op jit(solution)/shard_map/ppermute | solution.py:124
  79.3 0.7 collective-permute-start.30
  80.0 2.1 %convolution_bitcast_fusion.1 = f32[512,512]{1,0:T(8,128)S(1)} fusion(f32[512,512]{1,0:T(8,128)S(1)} %copy-done, f32[128,512]{1,0:T(8,128)} %copy-done.10, f32[128,512]{1,0:T(8,128)} %copy-done.9, f32[128,512]{1,0:T(8,128)} %copy-done.8, f32[128,512]{1,0:T(8,128)S(1)} %get-tuple-element.26), kind=kOutput, calls=%fused_computation.25 | convolution fusion | flops 806092800 | bytes 3145728 | tf_op jit(solution)/shard_map/dot_general | solution.py:114
  82.1 2.1 %collective-permute-done.29 = f32[32,768]{1,0:T(8,128)S(1)} collective-permute-done((f32[32,768]{1,0:T(8,128)S(1)}, f32[32,768]{1,0:T(8,128)S(1)}, u32[]{:S(2)}, u32[]{:S(2)}) %collective-permute-start.29) | collective-permute-done | bytes 98336 | tf_op jit(solution)/shard_map/ppermute | solution.py:124
  84.3 0.3 collective-permute-start.31
  84.6 0.4 collective-permute-start.32
  85.1 2.8 %collective-permute-start.33 = (f32[128,768]{1,0:T(8,128)S(1)}, f32[128,768]{1,0:T(8,128)S(1)}, u32[]{:S(2)}, u32[]{:S(2)}) collective-permute-start(f32[128,768]{1,0:T(8,128)S(1)} %pad_maximum_fusion.3), channel_id=1, source_target_pairs={{0,1},{1,0},{2,3},{3,2},{4,5},{5,4},{6,7},{7,6},{8,9},{9,8},{10,11... | collective-permute-start | bytes 1179656 | tf_op jit(solution)/shard_map/ppermute | solution.py:124
  87.9 2.2 %convolution_bitcast_fusion = f32[512,512]{1,0:T(8,128)S(1)} fusion(f32[512,512]{1,0:T(8,128)} %collective-permute-done.10, f32[512,512]{1,0:T(8,128)S(1)} %copy-done), kind=kOutput, calls=%fused_computation.24 | convolution fusion | flops 805306368 | bytes 3145728 | tf_op jit(solution)/shard_map/dot_general | solution.py:114
  90.4 1.3 collective-permute-start.12
  91.6 13.3 %collective-permute-done.31 = f32[128,768]{1,0:T(8,128)S(1)} collective-permute-done((f32[128,768]{1,0:T(8,128)S(1)}, f32[128,768]{1,0:T(8,128)S(1)}, u32[]{:S(2)}, u32[]{:S(2)}) %collective-permute-start.31) | collective-permute-done | bytes 393248 | tf_op jit(solution)/shard_map/ppermute | solution.py:124
  105.1 1.4 pad_maximum_fusion.1
  106.6 5.3 %collective-permute-start.34 = (f32[512,768]{1,0:T(8,128)}, f32[512,768]{1,0:T(8,128)}, u32[]{:S(2)}, u32[]{:S(2)}) collective-permute-start(f32[512,768]{1,0:T(8,128)} %pad_maximum_fusion.1), channel_id=1, source_target_pairs={{0,4},{4,0},{1,5},{5,1},{2,6},{6,2},{3,7},{7,3},{8,12},{12,8},{9,1... | collective-permute-start | bytes 4718600 | tf_op jit(solution)/shard_map/ppermute | solution.py:120
  111.9 1.6 collective-permute-done.11
  113.4 11.2 %collective-permute-done.12 = f32[128,1024]{1,0:T(8,128)S(1)} collective-permute-done((f32[128,1024]{1,0:T(8,128)S(1)}, f32[128,1024]{1,0:T(8,128)S(1)}, u32[]{:S(2)}, u32[]{:S(2)}) %collective-permute-start.12) | collective-permute-done | bytes 524320 | tf_op jit(solution)/shard_map/ppermute | solution.py:124
  124.6 5.3 %collective-permute-done.13 = f32[128,1024]{1,0:T(8,128)S(1)} collective-permute-done((f32[128,1024]{1,0:T(8,128)S(1)}, f32[128,1024]{1,0:T(8,128)S(1)}, u32[]{:S(2)}, u32[]{:S(2)}) %collective-permute-start.13) | collective-permute-done | bytes 524320 | tf_op jit(solution)/shard_map/ppermute | solution.py:124
  129.9 1.0 fusion.16
  131.0 3.2 %collective-permute-start.16 = (f32[128,1024]{1,0:T(8,128)}, f32[128,1024]{1,0:T(8,128)S(1)}, u32[]{:S(2)}, u32[]{:S(2)}) collective-permute-start(f32[128,1024]{1,0:T(8,128)} %fusion.16), channel_id=1, source_target_pairs={{0,1},{1,0},{2,3},{3,2},{4,5},{5,4},{6,7},{7,6},{8,9},{9,8},{10,11... | collective-permute-start | bytes 1572872 | tf_op jit(solution)/shard_map/ppermute | solution.py:124
  134.2 22.9 %collective-permute-done.14 = f32[128,1024]{1,0:T(8,128)S(1)} collective-permute-done((f32[128,1024]{1,0:T(8,128)}, f32[128,1024]{1,0:T(8,128)S(1)}, u32[]{:S(2)}, u32[]{:S(2)}) %collective-permute-start.14) | collective-permute-done | bytes 524320 | tf_op jit(solution)/shard_map/ppermute | solution.py:124
  157.2 1.3 broadcast_select_fusion.9
  158.6 0.8 copy-done.3
  159.7 3.3 %broadcast_select_fusion = (f32[512,768]{1,0:T(8,128)}, f32[512,768]{1,0:T(8,128)}) fusion(f32[512,768]{1,0:T(8,128)} %collective-permute-done.34, pred[]{:T(512)S(6)} %eq.36, f32[128,768]{1,0:T(8,128)S(1)} %copy-done.7, f32[128,768]{1,0:T(8,128)S(1)} %copy-done.5, f32[128,768]{1,0:T(8,128)S(1)} %copy-done.3, f32[128,768]{1,0:T(8,128)S(1)} %get-tuple-element.20), kind=kLoop, calls=%fused_computation.44 | loop fusion | flops 1966080 | bytes 6291457 | tf_op jit(solution)/shard_map/jit(_where)/select_n | solution.py:187
  163.0 12.8 %factor.1 = (f32[2,512,512]{2,1,0:T(8,128)}, f32[512,512]{1,0:T(8,128)}) custom-call(f32[512,768]{1,0:T(8,128)} %get-tuple-element.10.m0, f32[512,768]{1,0:T(8,128)} %get-tuple-element.9.m1), custom_call_target="tpu_custom_call" | custom-call | flops 20000000000 | bytes 8388608 | tf_op jit(solution)/shard_map/factor/pallas_call | solution.py:96
  175.8 2.3 %fusion.2 = f32[512,512]{0,1:T(8,128)S(1)} fusion(f32[2,512,512]{2,1,0:T(8,128)} %get-tuple-element.7, f32[512,1024]{1,0:T(8,128)S(1)} %pad_maximum_fusion, pred[]{:T(512)S(6)} %eq.36), kind=kOutput, calls=%fused_computation.29 | convolution fusion | flops 805568512 | bytes 4194305 | tf_op jit(solution)/shard_map/dot_general | solution.py:114
  178.1 1.1 fusion.44
  179.2 0.5 copy-done.11
  179.7 1.1 fusion
  180.8 0.3 maximum_select_fusion
  181.1 1.8 copy.8
  (71 shorter events, 1.9 us)
Async XLA Ops:
  0.0 11.5 %copy-start = (f32[512,512]{1,0:T(8,128)S(1)}, f32[512,512]{1,0:T(8,128)}, u32[]{:S(2)}) copy-start(f32[512,512]{1,0:T(8,128)} %param.3) | copy-start | bytes 3145732
  0.0 30.4 %collective-permute-start.17 = (f32[512,512]{1,0:T(8,128)}, f32[512,512]{1,0:T(8,128)}, u32[]{:S(2)}, u32[]{:S(2)}) collective-permute-start(f32[512,512]{1,0:T(8,128)} %param.3), channel_id=1, source_target_pairs={{0,4},{4,0},{1,5},{5,1},{2,6},{6,2},{3,7},{7,3},{8,12},{12,8},{9,1... | collective-permute-start | bytes 3145736 | tf_op jit(solution)/shard_map/ppermute | solution.py:120
  4.4 8.1 %collective-permute-start = (f32[128,512]{1,0:T(8,128)S(1)}, f32[128,512]{1,0:T(8,128)S(1)}, u32[]{:S(2)}, u32[]{:S(2)}) collective-permute-start(f32[128,512]{1,0:T(8,128)S(1)} %get-tuple-element.30), channel_id=1, source_target_pairs={{0,64},{1,65},{2,66},{3,67},{4,68},{5,69},{6,70},{7,71}} | collective-permute-start | bytes 786440 | tf_op jit(solution)/shard_map/ppermute | solution.py:159
  5.8 11.2 %collective-permute-start.1 = (f32[128,512]{1,0:T(8,128)S(1)}, f32[128,512]{1,0:T(8,128)S(1)}, u32[]{:S(2)}, u32[]{:S(2)}) collective-permute-start(f32[128,512]{1,0:T(8,128)S(1)} %get-tuple-element.32), channel_id=1, source_target_pairs={{0,128},{1,129},{2,130},{3,131},{4,132},{5,133},{6,134},{7,135}} | collective-permute-start | bytes 786440 | tf_op jit(solution)/shard_map/ppermute | solution.py:159
  8.0 8.9 %collective-permute-start.2 = (f32[128,512]{1,0:T(8,128)S(1)}, f32[128,512]{1,0:T(8,128)S(1)}, u32[]{:S(2)}, u32[]{:S(2)}) collective-permute-start(f32[128,512]{1,0:T(8,128)S(1)} %get-tuple-element.31), channel_id=1, source_target_pairs={{0,192},{1,193},{2,194},{3,195},{4,196},{5,197},{6,198},{7,199}} | collective-permute-start | bytes 786440 | tf_op jit(solution)/shard_map/ppermute | solution.py:159
  11.5 9.5 %copy-start.1 = (f32[512,1024]{1,0:T(8,128)S(1)}, f32[512,1024]{1,0:T(8,128)}, u32[]{:S(2)}) copy-start(f32[512,1024]{1,0:T(8,128)} %param.2) | copy-start | bytes 6291460
  17.0 6.3 %collective-permute-start.3 = (f32[128,512]{1,0:T(8,128)S(1)}, f32[128,512]{1,0:T(8,128)S(1)}, u32[]{:S(2)}, u32[]{:S(2)}) collective-permute-start(f32[128,512]{1,0:T(8,128)S(1)} %add_add_fusion.1), channel_id=1, source_target_pairs={{0,32},{1,33},{2,34},{3,35},{4,36},{5,37},{6,38},{7,39},{64,96},{6... | collective-permute-start | bytes 786440 | tf_op jit(solution)/shard_map/ppermute | solution.py:162
  18.4 10.6 %collective-permute-start.4 = (f32[128,512]{1,0:T(8,128)S(1)}, f32[128,512]{1,0:T(8,128)S(1)}, u32[]{:S(2)}, u32[]{:S(2)}) collective-permute-start(f32[128,512]{1,0:T(8,128)S(1)} %add_add_fusion.1), channel_id=1, source_target_pairs={{0,16},{1,17},{2,18},{3,19},{4,20},{5,21},{6,22},{7,23},{64,80},{6... | collective-permute-start | bytes 786440 | tf_op jit(solution)/shard_map/ppermute | solution.py:162
  19.7 9.3 %collective-permute-start.5 = (f32[128,512]{1,0:T(8,128)S(1)}, f32[128,512]{1,0:T(8,128)S(1)}, u32[]{:S(2)}, u32[]{:S(2)}) collective-permute-start(f32[128,512]{1,0:T(8,128)S(1)} %add_add_fusion.1), channel_id=1, source_target_pairs={{0,48},{1,49},{2,50},{3,51},{4,52},{5,53},{6,54},{7,55},{64,112},{... | collective-permute-start | bytes 786440 | tf_op jit(solution)/shard_map/ppermute | solution.py:162
  29.0 7.5 %collective-permute-start.6 = (f32[128,512]{1,0:T(8,128)S(1)}, f32[128,512]{1,0:T(8,128)S(1)}, u32[]{:S(2)}, u32[]{:S(2)}) collective-permute-start(f32[128,512]{1,0:T(8,128)S(1)} %add_add_fusion), channel_id=1, source_target_pairs={{0,8},{16,24},{32,40},{48,56},{1,9},{17,25},{33,41},{49,57},{2,10}... | collective-permute-start | bytes 786440 | tf_op jit(solution)/shard_map/ppermute | solution.py:163
  32.4 4.1 %copy-start.12 = (f32[256,512]{0,1:T(8,128)S(1)}, f32[256,512]{0,1:T(8,128)}, u32[]{:S(2)}) copy-start(f32[256,512]{0,1:T(8,128)} %copy.13) | copy-start | bytes 1572868
  32.5 9.6 %collective-permute-start.18 = (f32[128,768]{1,0:T(8,128)S(1)}, f32[128,768]{1,0:T(8,128)S(1)}, u32[]{:S(2)}, u32[]{:S(2)}) collective-permute-start(f32[128,768]{1,0:T(8,128)S(1)} %get-tuple-element.23), channel_id=1, source_target_pairs={{0,1},{1,0},{2,3},{3,2},{4,5},{5,4},{6,7},{7,6},{8,9},{9,8},{10,11... | collective-permute-start | bytes 1179656 | tf_op jit(solution)/shard_map/ppermute | solution.py:124
  33.8 19.1 %collective-permute-start.19 = (f32[128,768]{1,0:T(8,128)S(1)}, f32[128,768]{1,0:T(8,128)S(1)}, u32[]{:S(2)}, u32[]{:S(2)}) collective-permute-start(f32[128,768]{1,0:T(8,128)S(1)} %get-tuple-element.24), channel_id=1, source_target_pairs={{0,2},{1,3},{2,0},{3,1},{4,6},{5,7},{6,4},{7,5},{8,10},{9,11},{10,... | collective-permute-start | bytes 1179656 | tf_op jit(solution)/shard_map/ppermute | solution.py:124
  36.5 18.5 %collective-permute-start.20 = (f32[128,768]{1,0:T(8,128)S(1)}, f32[128,768]{1,0:T(8,128)S(1)}, u32[]{:S(2)}, u32[]{:S(2)}) collective-permute-start(f32[128,768]{1,0:T(8,128)S(1)} %get-tuple-element.25), channel_id=1, source_target_pairs={{0,3},{1,2},{2,1},{3,0},{4,7},{5,6},{6,5},{7,4},{8,11},{9,10},{10,... | collective-permute-start | bytes 1179656 | tf_op jit(solution)/shard_map/ppermute | solution.py:124
  36.6 24.9 %collective-permute-start.7 = (f32[128,512]{1,0:T(8,128)S(1)}, f32[128,512]{1,0:T(8,128)S(1)}, u32[]{:S(2)}, u32[]{:S(2)}) collective-permute-start(f32[128,512]{1,0:T(8,128)S(1)} %broadcast_select_fusion.18), channel_id=1, source_target_pairs={{0,192},{64,128},{128,64},{192,0},{1,193},{65,129},{129,65},{193,1... | collective-permute-start | bytes 786440 | tf_op jit(solution)/shard_map/ppermute | solution.py:124
  38.0 24.8 %collective-permute-start.8 = (f32[128,512]{1,0:T(8,128)S(1)}, f32[128,512]{1,0:T(8,128)S(1)}, u32[]{:S(2)}, u32[]{:S(2)}) collective-permute-start(f32[128,512]{1,0:T(8,128)S(1)} %broadcast_select_fusion.18), channel_id=1, source_target_pairs={{0,128},{64,192},{128,0},{192,64},{1,129},{65,193},{129,1},{193,65... | collective-permute-start | bytes 786440 | tf_op jit(solution)/shard_map/ppermute | solution.py:124
  42.0 20.8 %collective-permute-start.9 = (f32[128,512]{1,0:T(8,128)S(1)}, f32[128,512]{1,0:T(8,128)S(1)}, u32[]{:S(2)}, u32[]{:S(2)}) collective-permute-start(f32[128,512]{1,0:T(8,128)S(1)} %broadcast_select_fusion.18), channel_id=1, source_target_pairs={{0,64},{64,0},{128,192},{192,128},{1,65},{65,1},{129,193},{193,129... | collective-permute-start | bytes 786440 | tf_op jit(solution)/shard_map/ppermute | solution.py:124
  55.2 7.8 %collective-permute-start.21 = (f32[32,768]{1,0:T(8,128)S(1)}, f32[32,768]{1,0:T(8,128)S(1)}, u32[]{:S(2)}, u32[]{:S(2)}) collective-permute-start(f32[32,768]{1,0:T(8,128)S(1)} %get-tuple-element.37), channel_id=1, source_target_pairs={{0,64},{1,65},{2,66},{3,67},{4,68},{5,69},{6,70},{7,71}} | collective-permute-start | bytes 294920 | tf_op jit(solution)/shard_map/ppermute | solution.py:159
  57.9 5.2 %collective-permute-start.22 = (f32[32,768]{1,0:T(8,128)S(1)}, f32[32,768]{1,0:T(8,128)S(1)}, u32[]{:S(2)}, u32[]{:S(2)}) collective-permute-start(f32[32,768]{1,0:T(8,128)S(1)} %get-tuple-element.39), channel_id=1, source_target_pairs={{0,128},{1,129},{2,130},{3,131},{4,132},{5,133},{6,134},{7,135}} | collective-permute-start | bytes 294920 | tf_op jit(solution)/shard_map/ppermute | solution.py:159
  61.5 2.9 %collective-permute-start.23 = (f32[32,768]{1,0:T(8,128)S(1)}, f32[32,768]{1,0:T(8,128)S(1)}, u32[]{:S(2)}, u32[]{:S(2)}) collective-permute-start(f32[32,768]{1,0:T(8,128)S(1)} %get-tuple-element.38), channel_id=1, source_target_pairs={{0,192},{1,193},{2,194},{3,195},{4,196},{5,197},{6,198},{7,199}} | collective-permute-start | bytes 294920 | tf_op jit(solution)/shard_map/ppermute | solution.py:159
  63.0 5.4 %copy-start.8 = (f32[128,512]{1,0:T(8,128)}, f32[128,512]{1,0:T(8,128)S(1)}, u32[]{:S(2)}) copy-start(f32[128,512]{1,0:T(8,128)S(1)} %get-tuple-element.27) | copy-start | bytes 786436
  63.0 6.4 %copy-start.9 = (f32[128,512]{1,0:T(8,128)}, f32[128,512]{1,0:T(8,128)S(1)}, u32[]{:S(2)}) copy-start(f32[128,512]{1,0:T(8,128)S(1)} %get-tuple-element.28) | copy-start | bytes 786436
  63.0 9.9 %copy-start.10 = (f32[128,512]{1,0:T(8,128)}, f32[128,512]{1,0:T(8,128)S(1)}, u32[]{:S(2)}) copy-start(f32[128,512]{1,0:T(8,128)S(1)} %get-tuple-element.29) | copy-start | bytes 786436
  64.4 8.4 %collective-permute-start.24 = (f32[32,768]{1,0:T(8,128)S(1)}, f32[32,768]{1,0:T(8,128)S(1)}, u32[]{:S(2)}, u32[]{:S(2)}) collective-permute-start(f32[32,768]{1,0:T(8,128)S(1)} %fusion.40), channel_id=1, source_target_pairs={{0,32},{1,33},{2,34},{3,35},{4,36},{5,37},{6,38},{7,39},{64,96},{6... | collective-permute-start | bytes 294920 | tf_op jit(solution)/shard_map/ppermute | solution.py:162
  65.7 7.1 %collective-permute-start.25 = (f32[32,768]{1,0:T(8,128)S(1)}, f32[32,768]{1,0:T(8,128)S(1)}, u32[]{:S(2)}, u32[]{:S(2)}) collective-permute-start(f32[32,768]{1,0:T(8,128)S(1)} %fusion.40), channel_id=1, source_target_pairs={{0,16},{1,17},{2,18},{3,19},{4,20},{5,21},{6,22},{7,23},{64,80},{6... | collective-permute-start | bytes 294920 | tf_op jit(solution)/shard_map/ppermute | solution.py:162
  67.0 5.9 %collective-permute-start.26 = (f32[32,768]{1,0:T(8,128)S(1)}, f32[32,768]{1,0:T(8,128)S(1)}, u32[]{:S(2)}, u32[]{:S(2)}) collective-permute-start(f32[32,768]{1,0:T(8,128)S(1)} %fusion.40), channel_id=1, source_target_pairs={{0,48},{1,49},{2,50},{3,51},{4,52},{5,53},{6,54},{7,55},{64,112},{... | collective-permute-start | bytes 294920 | tf_op jit(solution)/shard_map/ppermute | solution.py:162
  69.4 18.5 %collective-permute-start.10 = (f32[512,512]{1,0:T(8,128)}, f32[512,512]{1,0:T(8,128)}, u32[]{:S(2)}, u32[]{:S(2)}) collective-permute-start(f32[512,512]{1,0:T(8,128)} %pad_maximum_fusion.2), channel_id=1, source_target_pairs={{0,4},{4,0},{1,5},{5,1},{2,6},{6,2},{3,7},{7,3},{8,12},{12,8},{9,1... | collective-permute-start | bytes 3145736 | tf_op jit(solution)/shard_map/ppermute | solution.py:120
  72.9 2.9 %collective-permute-start.27 = (f32[32,768]{1,0:T(8,128)S(1)}, f32[32,768]{1,0:T(8,128)}, u32[]{:S(2)}, u32[]{:S(2)}) collective-permute-start(f32[32,768]{1,0:T(8,128)S(1)} %add_add_fusion.2), channel_id=1, source_target_pairs={{0,8},{16,24},{32,40},{48,56},{1,9},{17,25},{33,41},{49,57},{2,10}... | collective-permute-start | bytes 294920 | tf_op jit(solution)/shard_map/ppermute | solution.py:163
  75.9 6.2 %collective-permute-start.28 = (f32[32,768]{1,0:T(8,128)S(1)}, f32[32,768]{1,0:T(8,128)S(1)}, u32[]{:S(2)}, u32[]{:S(2)}) collective-permute-start(f32[32,768]{1,0:T(8,128)S(1)} %broadcast_select_fusion.27), channel_id=1, source_target_pairs={{0,192},{64,128},{128,64},{192,0},{1,193},{65,129},{129,65},{193,1... | collective-permute-start | bytes 294920 | tf_op jit(solution)/shard_map/ppermute | solution.py:124
  79.3 5.0 %collective-permute-start.29 = (f32[32,768]{1,0:T(8,128)S(1)}, f32[32,768]{1,0:T(8,128)S(1)}, u32[]{:S(2)}, u32[]{:S(2)}) collective-permute-start(f32[32,768]{1,0:T(8,128)S(1)} %broadcast_select_fusion.27), channel_id=1, source_target_pairs={{0,128},{64,192},{128,0},{192,64},{1,129},{65,193},{129,1},{193,65... | collective-permute-start | bytes 294920 | tf_op jit(solution)/shard_map/ppermute | solution.py:124
  79.3 5.0 %collective-permute-start.30 = (f32[32,768]{1,0:T(8,128)S(1)}, f32[32,768]{1,0:T(8,128)S(1)}, u32[]{:S(2)}, u32[]{:S(2)}) collective-permute-start(f32[32,768]{1,0:T(8,128)S(1)} %broadcast_select_fusion.27), channel_id=1, source_target_pairs={{0,64},{64,0},{128,192},{192,128},{1,65},{65,1},{129,193},{193,129... | collective-permute-start | bytes 294920 | tf_op jit(solution)/shard_map/ppermute | solution.py:124
  84.3 20.5 %collective-permute-start.31 = (f32[128,768]{1,0:T(8,128)S(1)}, f32[128,768]{1,0:T(8,128)S(1)}, u32[]{:S(2)}, u32[]{:S(2)}) collective-permute-start(f32[128,768]{1,0:T(8,128)S(1)} %pad_maximum_fusion.3), channel_id=1, source_target_pairs={{0,3},{1,2},{2,1},{3,0},{4,7},{5,6},{6,5},{7,4},{8,11},{9,10},{10,... | collective-permute-start | bytes 1179656 | tf_op jit(solution)/shard_map/ppermute | solution.py:124
  84.6 20.3 %collective-permute-start.32 = (f32[128,768]{1,0:T(8,128)S(1)}, f32[128,768]{1,0:T(8,128)S(1)}, u32[]{:S(2)}, u32[]{:S(2)}) collective-permute-start(f32[128,768]{1,0:T(8,128)S(1)} %pad_maximum_fusion.3), channel_id=1, source_target_pairs={{0,2},{1,3},{2,0},{3,1},{4,6},{5,7},{6,4},{7,5},{8,10},{9,11},{10,... | collective-permute-start | bytes 1179656 | tf_op jit(solution)/shard_map/ppermute | solution.py:124
  85.1 19.9 %collective-permute-start.33 = (f32[128,768]{1,0:T(8,128)S(1)}, f32[128,768]{1,0:T(8,128)S(1)}, u32[]{:S(2)}, u32[]{:S(2)}) collective-permute-start(f32[128,768]{1,0:T(8,128)S(1)} %pad_maximum_fusion.3), channel_id=1, source_target_pairs={{0,1},{1,0},{2,3},{3,2},{4,5},{5,4},{6,7},{7,6},{8,9},{9,8},{10,11... | collective-permute-start | bytes 1179656 | tf_op jit(solution)/shard_map/ppermute | solution.py:124
  90.3 23.2 %collective-permute-start.11 = (f32[128,1024]{1,0:T(8,128)S(1)}, f32[128,1024]{1,0:T(8,128)S(1)}, u32[]{:S(2)}, u32[]{:S(2)}) collective-permute-start(f32[128,1024]{1,0:T(8,128)S(1)} %get-tuple-element.15), channel_id=1, source_target_pairs={{0,1},{1,0},{2,3},{3,2},{4,5},{5,4},{6,7},{7,6},{8,9},{9,8},{10,11... | collective-permute-start | bytes 1572872 | tf_op jit(solution)/shard_map/ppermute | solution.py:124
  90.4 34.3 %collective-permute-start.12 = (f32[128,1024]{1,0:T(8,128)S(1)}, f32[128,1024]{1,0:T(8,128)S(1)}, u32[]{:S(2)}, u32[]{:S(2)}) collective-permute-start(f32[128,1024]{1,0:T(8,128)S(1)} %get-tuple-element.16), channel_id=1, source_target_pairs={{0,2},{1,3},{2,0},{3,1},{4,6},{5,7},{6,4},{7,5},{8,10},{9,11},{10,... | collective-permute-start | bytes 1572872 | tf_op jit(solution)/shard_map/ppermute | solution.py:124
  104.9 25.0 %collective-permute-start.13 = (f32[128,1024]{1,0:T(8,128)S(1)}, f32[128,1024]{1,0:T(8,128)S(1)}, u32[]{:S(2)}, u32[]{:S(2)}) collective-permute-start(f32[128,1024]{1,0:T(8,128)S(1)} %get-tuple-element.17), channel_id=1, source_target_pairs={{0,3},{1,2},{2,1},{3,0},{4,7},{5,6},{6,5},{7,4},{8,11},{9,10},{10,... | collective-permute-start | bytes 1572872 | tf_op jit(solution)/shard_map/ppermute | solution.py:124
  105.0 1.5 copy-start.2
  105.0 1.5 copy-start.4
  105.1 25.8 %copy-start.6 = (f32[128,768]{1,0:T(8,128)}, f32[128,768]{1,0:T(8,128)S(1)}, u32[]{:S(2)}) copy-start(f32[128,768]{1,0:T(8,128)S(1)} %broadcast_select_fusion.14) | copy-start | bytes 1179652
  106.6 52.1 %collective-permute-start.34 = (f32[512,768]{1,0:T(8,128)}, f32[512,768]{1,0:T(8,128)}, u32[]{:S(2)}, u32[]{:S(2)}) collective-permute-start(f32[512,768]{1,0:T(8,128)} %pad_maximum_fusion.1), channel_id=1, source_target_pairs={{0,4},{4,0},{1,5},{5,1},{2,6},{6,2},{3,7},{7,3},{8,12},{12,8},{9,1... | collective-permute-start | bytes 4718600 | tf_op jit(solution)/shard_map/ppermute | solution.py:120
  130.9 26.2 %collective-permute-start.14 = (f32[128,1024]{1,0:T(8,128)}, f32[128,1024]{1,0:T(8,128)S(1)}, u32[]{:S(2)}, u32[]{:S(2)}) collective-permute-start(f32[128,1024]{1,0:T(8,128)} %fusion.16), channel_id=1, source_target_pairs={{0,3},{1,2},{2,1},{3,0},{4,7},{5,6},{6,5},{7,4},{8,11},{9,10},{10,... | collective-permute-start | bytes 1572872 | tf_op jit(solution)/shard_map/ppermute | solution.py:124
  130.9 26.2 %collective-permute-start.15 = (f32[128,1024]{1,0:T(8,128)}, f32[128,1024]{1,0:T(8,128)S(1)}, u32[]{:S(2)}, u32[]{:S(2)}) collective-permute-start(f32[128,1024]{1,0:T(8,128)} %fusion.16), channel_id=1, source_target_pairs={{0,2},{1,3},{2,0},{3,1},{4,6},{5,7},{6,4},{7,5},{8,10},{9,11},{10,... | collective-permute-start | bytes 1572872 | tf_op jit(solution)/shard_map/ppermute | solution.py:124
  131.0 26.2 %collective-permute-start.16 = (f32[128,1024]{1,0:T(8,128)}, f32[128,1024]{1,0:T(8,128)S(1)}, u32[]{:S(2)}, u32[]{:S(2)}) collective-permute-start(f32[128,1024]{1,0:T(8,128)} %fusion.16), channel_id=1, source_target_pairs={{0,1},{1,0},{2,3},{3,2},{4,5},{5,4},{6,7},{7,6},{8,9},{9,8},{10,11... | collective-permute-start | bytes 1572872 | tf_op jit(solution)/shard_map/ppermute | solution.py:124
  158.4 1.0 copy-start.3
  158.4 1.1 copy-start.5
  158.4 1.2 copy-start.7
  175.8 2.4 %copy-start.13 = (f32[512,512]{1,0:T(8,128)S(1)}, f32[512,512]{1,0:T(8,128)}, u32[]{:S(2)}) copy-start(f32[512,512]{1,0:T(8,128)} %get-tuple-element.8) | copy-start | bytes 3145732
  178.1 1.6 copy-start.11

commit v2 on v1

v2 whole, which is shorter than its diff:
```python
import jax, jax.numpy as jnp
from jax import lax
from jax.experimental import pallas as pl
from jax.experimental.pallas import tpu as pltpu
NB=512
H=256
CENTRE, RADIUS = 7.0, 5.0
CHEB = 6
NEWTON = 2


def dims(ta, tb):
    return (((0 if ta else 1,), (1 if tb else 0,)), ((), ()))


def dot1(a, b, ta=False, tb=False):
    return lax.dot_general(a, b, dims(ta, tb), preferred_element_type=jnp.float32)


def split(a):
    hi = a.astype(jnp.bfloat16)
    return hi, (a - hi.astype(jnp.float32)).astype(jnp.bfloat16)


def dot3(a, b, ta=False, tb=False):
    (ah, al), (bh, bl) = a, b
    return dot1(ah, bh, ta, tb) + (dot1(ah, bl, ta, tb) + dot1(al, bh, ta, tb))


def tri(n, strict=False):
    r = lax.broadcasted_iota(jnp.int32, (n, n), 0)
    c = lax.broadcasted_iota(jnp.int32, (n, n), 1)
    return (r > c) if strict else (r >= c)


def eye(n):
    r = lax.broadcasted_iota(jnp.int32, (n, n), 0)
    c = lax.broadcasted_iota(jnp.int32, (n, n), 1)
    return (r == c)


def inverse_factor(a00, a10, a11):
    b = jnp.bfloat16
    low, ident = tri(H), eye(H).astype(jnp.float32)
    h00, h10, h11 = split(a00), split(a10), split(a11)
    b00, b10, b11 = h00[0], h10[0], h11[0]
    sigma = CENTRE / RADIUS
    rho = 1.0 / sigma
    d00 = ident * (1.0 / CENTRE); d11 = d00; d10 = jnp.zeros((H, H), jnp.float32)
    y00, y10, y11 = d00, d10, d11
    zero = jnp.zeros((H, H), jnp.float32)
    r00 = ident - jnp.where(low, a00, 0.0) * (1.0 / CENTRE)
    r10 = -a10 * (1.0 / CENTRE)
    r11 = ident - jnp.where(low, a11, 0.0) * (1.0 / CENTRE)
    for k in range(CHEB):
        nxt = 1.0 / (2.0 * sigma - rho)
        p, q = nxt * rho, 2.0 * nxt / RADIUS
        rho = nxt
        d00, d10, d11 = p * d00 + q * r00, p * d10 + q * r10, p * d11 + q * r11
        y00, y10, y11 = y00 + d00, y10 + d10, y11 + d11
        if k < CHEB - 1:
            v00, v10, v11 = y00.astype(b), y10.astype(b), y11.astype(b)
            r00 = ident - jnp.where(low, dot1(v00, b00), 0.0)
            r10 = -(dot1(v10, b00) + dot1(v11, b10))
            r11 = ident - jnp.where(low, dot1(v10, b10, False, True) + dot1(v11, b11), 0.0)
    s0 = lax.rsqrt(jnp.sum(y00 * ident, axis=1, keepdims=True))
    s1 = lax.rsqrt(jnp.sum(y11 * ident, axis=1, keepdims=True))
    x00, x10, x11 = y00 * s0, y10 * s1, y11 * s1
    half = jnp.where(tri(H, True), 1.0, 0.5 * ident)
    for _ in range(NEWTON):
        t00, t10, t11 = split(x00), split(x10), split(x11)
        w00 = split(dot3(t00, h00))
        w10 = split(dot3(t10, h00) + dot3(t11, h10))
        w11 = split(dot3(t10, h10, False, True) + dot3(t11, h11))
        e00 = ((dot3(w00, t00, False, True) - ident) * half).astype(b)
        e10 = dot3(w10, t00, False, True).astype(b)
        e11 = ((dot3(w10, t10, False, True) + dot3(w11, t11, False, True) - ident) * half).astype(b)
        x10 = x10 - (dot1(e10, t00[0]) + dot1(e11, t10[0]))
        x00 = x00 - dot1(e00, t00[0])
        x11 = x11 - dot1(e11, t11[0])
    return x00, x10, x11


VMEM = pl.BlockSpec(memory_space=pltpu.VMEM)
SMEM = pl.BlockSpec(memory_space=pltpu.SMEM)
F32 = jnp.float32


def block_kernel(where_ref, own, other, a_ref, *refs):
    outs, part, a_part = refs[:4], refs[4], refs[5]
    first, y = where_ref[0] == 0, where_ref[1]
    t0, t1 = split(own[:H, :]), split(own[H:, :])
    part[:, :H] = -dot3(t0, t0, False, True)
    part[:, H : 2 * H] = -dot3(t1, t0, False, True)
    part[:, 2 * H : 3 * H] = -dot3(t1, t1, False, True)

    @pl.when(first)
    def _():
        q = split(other[:H, :])
        part[:, 3 * H : 4 * H] = -dot3(t0, q, False, True)
        part[:, 4 * H :] = -dot3(t1, q, False, True)
        a_part[:, :H] = a_ref[:H, :H]
        a_part[:, H : 2 * H] = a_ref[H:, :H]
        a_part[:, 2 * H : 3 * H] = a_ref[H:, H:NB]
        a_part[:, 3 * H : 4 * H] = a_ref[:H, NB : NB + H]
        a_part[:, 4 * H :] = a_ref[H:, NB : NB + H]

    @pl.when(jnp.logical_not(first))
    def _():
        part[:, 3 * H : 4 * H] = -dot3(split(other[:H, :]), t1, False, True)
        part[:, 4 * H :] = -dot3(split(other[H:, :]), t1, False, True)
        a_part[:, :H] = a_ref[:H, NB : NB + H]
        a_part[:, H : 2 * H] = a_ref[H:, NB : NB + H]
        a_part[:, 2 * H : 3 * H] = a_ref[H:, NB + H :]
        a_part[:, 3 * H : 4 * H] = a_ref[H:, :H].T
        a_part[:, 4 * H :] = a_ref[H:, H:NB].T

    n = H // 4
    outs[0][...] = part[pl.ds(y * n, n), :] + a_part[pl.ds(y * n, n), :]
    for s in (1, 2, 3):
        outs[s][...] = part[pl.ds((y ^ s) * n, n), :]


def block_parts(where, own, other, a_cols):
    return pl.pallas_call(
        block_kernel,
        out_shape=(jax.ShapeDtypeStruct((H // 4, 5 * H), F32),) * 4,
        in_specs=[SMEM, VMEM, VMEM, VMEM],
        out_specs=(VMEM,) * 4,
        scratch_shapes=[pltpu.VMEM((H, 5 * H), F32)] * 2,
        cost_estimate=pl.CostEstimate(flops=10**9, bytes_accessed=2**22, transcendentals=0),
        name="block_parts",
    )(where, own, other, a_cols)


def factor_kernel(where_ref, own, other, x_ref, l_ref, m0, m1):
    @pl.when(where_ref[0] == 0)
    def _():
        m0[...] = own[...]
        m1[...] = other[...]

    @pl.when(where_ref[0] != 0)
    def _():
        m0[...] = other[...]
        m1[...] = own[...]

    def tile(m, i):
        return m[:, i * H : (i + 1) * H]

    def put(i, x00, x10, x11):
        x_ref[i, :H, :H] = x00
        x_ref[i, :H, H:] = jnp.zeros((H, H), F32)
        x_ref[i, H:, :H] = x10
        x_ref[i, H:, H:] = x11

    x00, x10, x11 = inverse_factor(tile(m0, 0), tile(m0, 1), tile(m0, 2))
    put(0, x00, x10, x11)
    t00, t10, t11 = split(x00), split(x10), split(x11)
    for j, m in enumerate((m0, m1)):
        top, bot = split(tile(m, 3)), split(tile(m, 4))
        l_ref[:H, j * H : (j + 1) * H] = dot3(t00, top)
        l_ref[H:, j * H : (j + 1) * H] = dot3(t10, top) + dot3(t11, bot)
    p0, p1 = split(l_ref[:, :H]), split(l_ref[:, H:])
    c00 = tile(m1, 0) - dot3(p0, p0, True, False)
    c10 = tile(m1, 1) - dot3(p1, p0, True, False)
    c11 = tile(m1, 2) - dot3(p1, p1, True, False)
    put(1, *inverse_factor(c00, c10, c11))


def factor(where, own, other):
    return pl.pallas_call(
        factor_kernel,
        out_shape=(jax.ShapeDtypeStruct((2, NB, NB), F32), jax.ShapeDtypeStruct((NB, NB), F32)),
        in_specs=[SMEM] + [VMEM] * 2,
        out_specs=(VMEM,) * 2,
        scratch_shapes=[pltpu.VMEM((H, 5 * H), F32)] * 2,
        cost_estimate=pl.CostEstimate(flops=5 * 10**9, bytes_accessed=2**23, transcendentals=0),
        name="factor",
    )(where, own, other)


def update_kernel(where_ref, p0, p1, p2a, p2b, p3, own, other, a_ref, out, ph, pl_, th, tl):
    core, y = where_ref[0], where_ref[1]
    n = 128

    def put(hi, lo, rows, t, v):
        columns = slice(t * NB, (t + 1) * NB)
        hi[rows, columns], lo[rows, columns] = split(v)

    every = slice(0, NB)
    put(ph, pl_, every, 0, p0[...])
    put(ph, pl_, every, 1, p1[...])
    put(ph, pl_, slice(0, H), 2, p2a[...])
    put(ph, pl_, slice(H, NB), 2, p2b[...])
    put(ph, pl_, every, 3, p3[...])
    for t in range(4):
        put(th, tl, slice(0, n), t, own[t * n : (t + 1) * n, :])
        put(th, tl, slice(n, 2 * n), t, other[t * n : (t + 1) * n, :])
    total = dot3((ph[...], pl_[...]), (th[...], tl[...]), False, True)
    for i, half in enumerate((core, 1 - core)):
        columns = pl.ds(pl.multiple_of(half * NB + y * n, n), n)
        out[:, pl.ds(pl.multiple_of(half * n, n), n)] = a_ref[:, columns] - total[:, i * n : (i + 1) * n]


def update_part(where, past, own, other, a_cols):
    return pl.pallas_call(
        update_kernel,
        out_shape=jax.ShapeDtypeStruct((NB, 256), F32),
        in_specs=[SMEM] + [VMEM] * 8,
        out_specs=VMEM,
        scratch_shapes=[pltpu.VMEM((r, 4 * NB), jnp.bfloat16) for r in (NB, NB, H, H)],
        cost_estimate=pl.CostEstimate(flops=10**9, bytes_accessed=2**22, transcendentals=0),
        name="update_part",
    )(where, *past, own, other, a_cols)


def solve_kernel(where_ref, u0, u1, u2, u3, x_ref, l_ref, out, s1, s2):
    y, position = where_ref[1], where_ref[2]
    n = 128
    for u, piece in enumerate((u0, u1, u2, u3)):
        columns = pl.ds(pl.multiple_of((y ^ u) * n, n), n)
        s1[:, columns] = piece[:, :n]
        s2[:, columns] = piece[:, n:]

    def keep(v, start):
        rows = position * NB + lax.broadcasted_iota(jnp.int32, v.shape, 0)
        return jnp.where(rows >= start + lax.broadcasted_iota(jnp.int32, v.shape, 1), v, 0.0)

    def times_inverse(i, s, start):
        left, right = split(s[:, :H]), split(s[:, H:])
        a = dot3(left, split(x_ref[i, :H, :H]), False, True)
        b = dot3(left, split(x_ref[i, H:, :H]), False, True) + dot3(right, split(x_ref[i, H:, H:]), False, True)
        out[:, start : start + H] = keep(a, start)
        out[:, start + H : start + NB] = keep(b, start + H)
        return a, b

    a, b = times_inverse(0, s1, 0)
    a, b = split(a), split(b)
    s2[...] = s2[...] - (dot3(a, split(l_ref[:H, :])) + dot3(b, split(l_ref[H:, :])))
    times_inverse(1, s2, NB)


def solve(where, pieces, inverse, below):
    return pl.pallas_call(
        solve_kernel,
        out_shape=jax.ShapeDtypeStruct((NB, 2 * NB), F32),
        in_specs=[SMEM] + [VMEM] * 6,
        out_specs=VMEM,
        scratch_shapes=[pltpu.VMEM((NB, NB), F32)] * 2,
        cost_estimate=pl.CostEstimate(flops=10**9, bytes_accessed=2**22, transcendentals=0),
        name="solve",
    )(where, *pieces, inverse, below)


from jax.sharding import Mesh
from jax.sharding import PartitionSpec as P

ROW_COL = ("row", "col_0", "col_1")
PLANE = ("row", "col_0")
BOX = ("row", "col_0", "depth")
TRADE = False


def send(v, axis, pairs, one_way=False):
    if one_way and TRADE:
        pairs = pairs + [(b, a) for a, b in pairs]
    return lax.ppermute(v, axis, pairs)


def swap_core(v):
    return send(v, "col_1", [(0, 1), (1, 0)])


def exchange(v, axis, bits):
    return send(v, axis, [(i, i ^ bits) for i in range(4)])


def in_order(pieces, me):
    low, high = (me & 1) == 1, (me >> 1) == 1
    p0, p1, p2, p3 = pieces
    p0, p1 = jnp.where(low, p1, p0), jnp.where(low, p0, p1)
    p2, p3 = jnp.where(low, p3, p2), jnp.where(low, p2, p3)
    p0, p2 = jnp.where(high, p2, p0), jnp.where(high, p0, p2)
    p1, p3 = jnp.where(high, p3, p1), jnp.where(high, p1, p3)
    return jnp.concatenate([p0, p1, p2, p3])


def pieces_along(v, axis):
    return [v] + [exchange(v, axis, s) for s in (1, 2, 3)]


def chunk_of(v, j):
    n = v.shape[0] // 4
    return lax.dynamic_slice_in_dim(v, j * n, n)


def spread_z(v, z):
    a = send(v, "col_0", [(0, 3)], True) + send(v, "col_0", [(0, 5)], True)
    v = jnp.where(z == 0, v, a)
    b = send(v, "col_0", [(0, 1), (3, 4), (5, 6)], True) + send(v, "col_0", [(0, 7), (3, 2)], True)
    return jnp.where((z == 0) | (z == 3) | (z == 5), v, b)


def body(a_cols, past):
    x, z = lax.axis_index("row"), lax.axis_index("col_0")
    core, y = lax.axis_index("col_1"), lax.axis_index("depth")
    root = (x == 0) & (z == 0)
    where = jnp.stack([core, y, lax.axis_index(ROW_COL)]).astype(jnp.int32)

    other = swap_core(past)
    got = 0.0
    for s in (1, 2, 3):
        pairs = [(d, 32 * s + (d ^ s)) for d in range(4)]
        got = got + send(chunk_of(past, y ^ s), BOX, pairs, True)
    top = jnp.where(root, chunk_of(past, y), got)

    parts = block_parts(where, past, other, a_cols)
    block = parts[0]
    for s in (1, 2, 3):
        block = block + exchange(parts[s], "depth", s)

    near1, near3 = exchange(past, "depth", 1), exchange(past, "depth", 3)
    far = exchange(near3[:H], "depth", 1), exchange(near1[H:], "depth", 3)
    rows = past, near1, *far, near3

    top = in_order(pieces_along(spread_z(top, z), "row"), x)
    top_other = swap_core(top)

    n = block.shape[0] // 4
    got = 0.0
    for p in (1, 2, 3):
        got = got + send(block[p * n : (p + 1) * n], PLANE, [(0, 8 * p)], True)
    spread = spread_z(jnp.where(root, block[:n], got), z)
    spread = in_order(pieces_along(spread, "depth"), y).reshape(4, n, -1)
    spread = in_order(pieces_along(spread[None], "row"), x)
    block = spread.transpose(1, 0, 2, 3).reshape(H, -1)
    block_other = swap_core(block)

    update = update_part(where, rows, top, top_other, a_cols)
    pieces = pieces_along(update, "depth")
    inverse, below = factor(where, block, block_other)
    return solve(where, pieces, inverse, below)


def solution(mesh):
    split_mesh = Mesh(
        mesh.devices.reshape(mesh.shape["row"], 8, 2, mesh.shape["depth"]),
        ("row", "col_0", "col_1", "depth"),
    )

    placed = (P(ROW_COL, None), P(ROW_COL, "depth"))
    return jax.shard_map(
        body, mesh=split_mesh, in_specs=placed, out_specs=P(ROW_COL, None), check_vma=False
    )
```

time: 185 us -> 155 us (0.84)
  the two profiles are of different devices: /device:TPU:1 before, /device:TPU:70 now
where the time goes in v2:
time: 155 us
  waiting for transfers between devices  66.9 us (43%)
  starting transfers between devices  46.3 us (30%)
  Pallas kernels  31.5 us (20%)
  other arithmetic  5.53 us (4%)
  local copies, waits for them, and re-layouts  4.41 us (3%)
    ppermute x36, waiting for transfers between devices, send(): return lax.ppermute(v, axis, pairs)  66.9 us
    ppermute x36, starting transfers between devices, send(): return lax.ppermute(v, axis, pairs)  46.3 us
    pallas_call x1, Pallas kernels, factor(): pl.pallas_call(factor_kernel, out_shape=(jax.ShapeDtypeStruct((2, NB, NB)...  13 us
    pallas_call x1, Pallas kernels, solve(): pl.pallas_call(solve_kernel, out_shape=jax.ShapeDtypeStruct((NB, 2 * NB),...  7.36 us
    pallas_call x1, Pallas kernels, update_part(): pl.pallas_call(update_kernel, out_shape=jax.ShapeDtypeStruct((NB, 256), F...  6.17 us
    pallas_call x1, Pallas kernels, block_parts(): pl.pallas_call(block_kernel, out_shape=(jax.ShapeDtypeStruct((H // 4, 5 *...  4.89 us
    unnamed x20, local copies, waits for them, and re-layouts  4.26 us
  transfers between devices with their start and end apart: 36, of which 16 were waited for; matrix products, arithmetic and copies ran while one was open for 3% of the time, Pallas kernels for 12%

profile of v2, /device:TPU:70, one launch (start us, length us, event | category | flops | bytes accessed | tf_op | source)
XLA Modules:
  0.0 154.9 jit_solution(14780323952572144391)
XLA Ops:
  0.0 0.6 pad_add_fusion.where_ref
  0.6 2.3 %collective-permute-done.18.other = f32[512,512]{1,0:T(8,128)S(1)} collective-permute-done((f32[512,512]{1,0:T(8,128)}, f32[512,512]{1,0:T(8,128)S(1)}, u32[]{:S(2)}, u32[]{:S(2)}) %collective-permute-start.18) | collective-permute-done | bytes 1048608 | tf_op jit(solution)/shard_map/ppermute | solution.py:267
  2.9 1.0 copy-done.4
  3.8 4.9 %block_parts.1 = (f32[64,1280]{1,0:T(8,128)}, f32[64,1280]{1,0:T(8,128)}, f32[64,1280]{1,0:T(8,128)}, f32[64,1280]{1,0:T(8,128)}) custom-call(s32[3]{0:T(128)} %pad_add_fusion.where_ref, f32[512,512]{1,0:T(8,128)} %own.1, f32[512,512]{1,0:T(8,128)} %copy-done.4, f32[512,1024]{1,0:T(8,128)} %a_ref.3), custom_call_target="tpu_custom_call" | custom-call | flops 1000000000 | bytes 4194304 | tf_op jit(solution)/shard_map/block_parts/pallas_call | solution.py:125
  8.7 1.6 %collective-permute-start.19 = (f32[64,1280]{1,0:T(8,128)}, f32[64,1280]{1,0:T(8,128)S(1)}, u32[]{:S(2)}, u32[]{:S(2)}) collective-permute-start(f32[64,1280]{1,0:T(8,128)} %get-tuple-element.12), channel_id=1, source_target_pairs={{0,1},{1,0},{2,3},{3,2},{4,5},{5,4},{6,7},{7,6},{8,9},{9,8},{10,11... | collective-permute-start | bytes 983048 | tf_op jit(solution)/shard_map/ppermute | solution.py:267
  10.3 2.9 %collective-permute-start.20 = (f32[64,1280]{1,0:T(8,128)}, f32[64,1280]{1,0:T(8,128)S(1)}, u32[]{:S(2)}, u32[]{:S(2)}) collective-permute-start(f32[64,1280]{1,0:T(8,128)} %get-tuple-element.13), channel_id=1, source_target_pairs={{0,2},{1,3},{2,0},{3,1},{4,6},{5,7},{6,4},{7,5},{8,10},{9,11},{10,... | collective-permute-start | bytes 983048 | tf_op jit(solution)/shard_map/ppermute | solution.py:267
  13.2 0.2 collective-permute-start.21
  13.4 6.1 %collective-permute-done.19 = f32[64,1280]{1,0:T(8,128)S(1)} collective-permute-done((f32[64,1280]{1,0:T(8,128)}, f32[64,1280]{1,0:T(8,128)S(1)}, u32[]{:S(2)}, u32[]{:S(2)}) %collective-permute-start.19) | collective-permute-done | bytes 327712 | tf_op jit(solution)/shard_map/ppermute | solution.py:267
  19.5 8.7 %collective-permute-done.20 = f32[64,1280]{1,0:T(8,128)S(1)} collective-permute-done((f32[64,1280]{1,0:T(8,128)}, f32[64,1280]{1,0:T(8,128)S(1)}, u32[]{:S(2)}, u32[]{:S(2)}) %collective-permute-start.20) | collective-permute-done | bytes 327712 | tf_op jit(solution)/shard_map/ppermute | solution.py:267
  28.2 2.6 %collective-permute-done.21 = f32[64,1280]{1,0:T(8,128)S(1)} collective-permute-done((f32[64,1280]{1,0:T(8,128)}, f32[64,1280]{1,0:T(8,128)S(1)}, u32[]{:S(2)}, u32[]{:S(2)}) %collective-permute-start.21) | collective-permute-done | bytes 327712 | tf_op jit(solution)/shard_map/ppermute | solution.py:267
  30.8 1.0 add_add_fusion
  31.9 0.7 collective-permute-start.23
  32.6 0.7 collective-permute-start.24
  33.2 0.7 collective-permute-start.22
  34.0 0.7 collective-permute-start.5
  34.7 0.7 collective-permute-start.6
  35.4 0.7 collective-permute-start.4
  36.1 0.7 collective-permute-start.26
  36.8 0.7 collective-permute-start.25
  37.6 0.7 collective-permute-start.8
  38.3 0.7 collective-permute-start.7
  39.0 1.3 collective-permute-start.28
  40.3 0.7 collective-permute-start.27
  41.1 1.3 collective-permute-start.10
  42.4 0.7 collective-permute-start.9
  43.1 10.2 %collective-permute-done.28 = f32[16,1280]{1,0:T(8,128)S(1)} collective-permute-done((f32[16,1280]{1,0:T(8,128)S(1)}, f32[16,1280]{1,0:T(8,128)S(1)}, u32[]{:S(2)}, u32[]{:S(2)}) %collective-permute-start.28) | collective-permute-done | bytes 81952 | tf_op jit(solution)/shard_map/ppermute | solution.py:267
  53.4 1.7 %collective-permute-start.30 = (f32[16,1280]{1,0:T(8,128)S(1)}, f32[16,1280]{1,0:T(8,128)S(1)}, u32[]{:S(2)}, u32[]{:S(2)}) collective-permute-start(f32[16,1280]{1,0:T(8,128)S(1)} %add_select_fusion.3), channel_id=1, source_target_pairs={{0,2},{1,3},{2,0},{3,1},{4,6},{5,7},{6,4},{7,5},{8,10},{9,11},{10,... | collective-permute-start | bytes 245768 | tf_op jit(solution)/shard_map/ppermute | solution.py:267
  55.2 3.0 %collective-permute-start.29 = (f32[16,1280]{1,0:T(8,128)S(1)}, f32[16,1280]{1,0:T(8,128)S(1)}, u32[]{:S(2)}, u32[]{:S(2)}) collective-permute-start(f32[16,1280]{1,0:T(8,128)S(1)} %add_select_fusion.3), channel_id=1, source_target_pairs={{0,3},{1,2},{2,1},{3,0},{4,7},{5,6},{6,5},{7,4},{8,11},{9,10},{10,... | collective-permute-start | bytes 245768 | tf_op jit(solution)/shard_map/ppermute | solution.py:267
  58.1 4.5 %collective-permute-done.10 = f32[128,512]{1,0:T(8,128)S(1)} collective-permute-done((f32[128,512]{1,0:T(8,128)S(1)}, f32[128,512]{1,0:T(8,128)S(1)}, u32[]{:S(2)}, u32[]{:S(2)}) %collective-permute-start.10) | collective-permute-done | bytes 262176 | tf_op jit(solution)/shard_map/ppermute | solution.py:267
  62.7 3.7 %collective-permute-start.13 = (f32[128,512]{1,0:T(8,128)S(1)}, f32[128,512]{1,0:T(8,128)S(1)}, u32[]{:S(2)}, u32[]{:S(2)}) collective-permute-start(f32[128,512]{1,0:T(8,128)S(1)} %add_select_fusion), channel_id=1, source_target_pairs={{0,64},{64,0},{128,192},{192,128},{1,65},{65,1},{129,193},{193,129... | collective-permute-start | bytes 786440 | tf_op jit(solution)/shard_map/ppermute | solution.py:267
  66.4 2.7 %collective-permute-start.12 = (f32[128,512]{1,0:T(8,128)S(1)}, f32[128,512]{1,0:T(8,128)}, u32[]{:S(2)}, u32[]{:S(2)}) collective-permute-start(f32[128,512]{1,0:T(8,128)S(1)} %add_select_fusion), channel_id=1, source_target_pairs={{0,128},{64,192},{128,0},{192,64},{1,129},{65,193},{129,1},{193,65... | collective-permute-start | bytes 786440 | tf_op jit(solution)/shard_map/ppermute | solution.py:267
  69.3 1.0 collective-permute-start.34
  70.3 3.7 %collective-permute-start.33 = (f32[1,4,16,1280]{3,2,0,1:T(8,128)S(1)}, f32[1,4,16,1280]{3,2,0,1:T(8,128)S(1)}, u32[]{:S(2)}, u32[]{:S(2)}) collective-permute-start(f32[1,4,16,1280]{3,2,0,1:T(8,128)S(1)} %bitcast.10), channel_id=1, source_target_pairs={{0,128},{64,192},{128,0},{192,64},{1,129},{65,193},{129,1},{193,65... | collective-permute-start | bytes 983048 | tf_op jit(solution)/shard_map/ppermute | solution.py:267
  74.0 0.7 copy-done.9
  74.7 2.8 %collective-permute-start.32 = (f32[1,4,16,1280]{3,2,0,1:T(8,128)S(1)}, f32[1,4,16,1280]{3,2,0,1:T(8,128)}, u32[]{:S(2)}, u32[]{:S(2)}) collective-permute-start(f32[1,4,16,1280]{3,2,0,1:T(8,128)S(1)} %bitcast.11), channel_id=1, source_target_pairs={{0,192},{64,128},{128,64},{192,0},{1,193},{65,129},{129,65},{193,1... | collective-permute-start | bytes 983048 | tf_op jit(solution)/shard_map/ppermute | solution.py:267
  77.5 4.6 %collective-permute-done.12 = f32[128,512]{1,0:T(8,128)} collective-permute-done((f32[128,512]{1,0:T(8,128)S(1)}, f32[128,512]{1,0:T(8,128)}, u32[]{:S(2)}, u32[]{:S(2)}) %collective-permute-start.12) | collective-permute-done | bytes 262176 | tf_op jit(solution)/shard_map/ppermute | solution.py:267
  82.1 1.2 collective-permute-start.1
  83.3 1.6 %collective-permute-done.11 = f32[128,512]{1,0:T(8,128)} collective-permute-done((f32[128,512]{1,0:T(8,128)S(1)}, f32[128,512]{1,0:T(8,128)}, u32[]{:S(2)}, u32[]{:S(2)}) %collective-permute-start.11) | collective-permute-done | bytes 262176 | tf_op jit(solution)/shard_map/ppermute | solution.py:267
  84.9 2.1 %collective-permute-start = (f32[512,512]{1,0:T(8,128)S(1)}, f32[512,512]{1,0:T(8,128)S(1)}, u32[]{:S(2)}, u32[]{:S(2)}) collective-permute-start(f32[512,512]{1,0:T(8,128)S(1)} %copy-done), channel_id=1, source_target_pairs={{0,1},{1,0},{2,3},{3,2},{4,5},{5,4},{6,7},{7,6},{8,9},{9,8},{10,11... | collective-permute-start | bytes 3145736 | tf_op jit(solution)/shard_map/ppermute | solution.py:267
  87.1 1.2 broadcast_select_fusion.15
  88.3 3.1 %collective-permute-done.33 = f32[1,4,16,1280]{3,2,0,1:T(8,128)S(1)} collective-permute-done((f32[1,4,16,1280]{3,2,0,1:T(8,128)S(1)}, f32[1,4,16,1280]{3,2,0,1:T(8,128)S(1)}, u32[]{:S(2)}, u32[]{:S(2)}) %collective-permute-start.33) | collective-permute-done | bytes 327712 | tf_op jit(solution)/shard_map/ppermute | solution.py:267
  91.5 2.7 %collective-permute-done.32 = f32[1,4,16,1280]{3,2,0,1:T(8,128)} collective-permute-done((f32[1,4,16,1280]{3,2,0,1:T(8,128)S(1)}, f32[1,4,16,1280]{3,2,0,1:T(8,128)}, u32[]{:S(2)}, u32[]{:S(2)}) %collective-permute-start.32) | collective-permute-done | bytes 327712 | tf_op jit(solution)/shard_map/ppermute | solution.py:267
  94.2 1.1 broadcast_select_fusion.7
  95.3 1.2 pad_maximum_fusion
  96.5 0.6 collective-permute-start.14
  97.1 1.8 %collective-permute-done.1.p3 = f32[512,512]{1,0:T(8,128)S(1)} collective-permute-done((f32[512,512]{1,0:T(8,128)S(1)}, f32[512,512]{1,0:T(8,128)S(1)}, u32[]{:S(2)}, u32[]{:S(2)}) %collective-permute-start.1) | collective-permute-done | bytes 1048608 | tf_op jit(solution)/shard_map/ppermute | solution.py:267
  98.9 0.8 collective-permute-start.2
  99.7 0.8 collective-permute-done.p1
  100.5 1.0 copy-done.3
  101.5 3.3 %collective-permute-start.3 = (f32[256,512]{1,0:T(8,128)S(1)}, f32[256,512]{1,0:T(8,128)S(1)}, u32[]{:S(2)}, u32[]{:S(2)}) collective-permute-start(f32[256,512]{1,0:T(8,128)S(1)} %slice.25), channel_id=1, source_target_pairs={{0,3},{1,2},{2,1},{3,0},{4,7},{5,6},{6,5},{7,4},{8,11},{9,10},{10,... | collective-permute-start | bytes 1572872 | tf_op jit(solution)/shard_map/ppermute | solution.py:267
  104.8 6.8 %collective-permute-done.2.p2a = f32[256,512]{1,0:T(8,128)} collective-permute-done((f32[256,512]{1,0:T(8,128)S(1)}, f32[256,512]{1,0:T(8,128)}, u32[]{:S(2)}, u32[]{:S(2)}) %collective-permute-start.2) | collective-permute-done | bytes 524320 | tf_op jit(solution)/shard_map/ppermute | solution.py:267
  111.6 3.5 %collective-permute-done.3.p2b = f32[256,512]{1,0:T(8,128)S(1)} collective-permute-done((f32[256,512]{1,0:T(8,128)S(1)}, f32[256,512]{1,0:T(8,128)S(1)}, u32[]{:S(2)}, u32[]{:S(2)}) %collective-permute-start.3) | collective-permute-done | bytes 524320 | tf_op jit(solution)/shard_map/ppermute | solution.py:267
  115.1 0.8 copy-done.5
  115.9 6.2 %update_part.1.u0 = f32[512,256]{1,0:T(8,128)} custom-call(s32[3]{0:T(128)} %pad_add_fusion.where_ref, f32[512,512]{1,0:T(8,128)} %own.1, f32[512,512]{1,0:T(8,128)} %copy-done.3, f32[256,512]{1,0:T(8,128)} %collective-permute-done.2.p2a, f32[256,512]{1,0:T(8,128)} %copy-done.5, f32[512,512]{1,0:T(8,128)} %copy-done.2, f32[512,512]{1,0:T(8,128)} %copy-done.1, ...), custom_call_target="tpu_custom_call" | custom-call | flops 1000000000 | bytes 4194304 | tf_op jit(solution)/shard_map/update_part/pallas_call | solution.py:206
  122.0 0.3 collective-permute-start.17
  122.4 1.1 collective-permute-start.16
  123.4 2.7 %collective-permute-start.15 = (f32[512,256]{1,0:T(8,128)}, f32[512,256]{1,0:T(8,128)S(1)}, u32[]{:S(2)}, u32[]{:S(2)}) collective-permute-start(f32[512,256]{1,0:T(8,128)} %update_part.1.u0), channel_id=1, source_target_pairs={{0,1},{1,0},{2,3},{3,2},{4,5},{5,4},{6,7},{7,6},{8,9},{9,8},{10,11... | collective-permute-start | bytes 1572872 | tf_op jit(solution)/shard_map/ppermute | solution.py:267
  126.1 13.0 %factor.1 = (f32[2,512,512]{2,1,0:T(8,128)}, f32[512,512]{1,0:T(8,128)}) custom-call(s32[3]{0:T(128)} %pad_add_fusion.where_ref, f32[256,1280]{1,0:T(8,128)} %bitcast.7.own, f32[256,1280]{1,0:T(8,128)} %collective-permute-done.35.other), custom_call_target="tpu_custom_call" | custom-call | flops 5000000000 | bytes 8388608 | tf_op jit(solution)/shard_map/factor/pallas_call | solution.py:171
  139.2 6.9 %collective-permute-done.17.u3 = f32[512,256]{1,0:T(8,128)S(1)} collective-permute-done((f32[512,256]{1,0:T(8,128)}, f32[512,256]{1,0:T(8,128)S(1)}, u32[]{:S(2)}, u32[]{:S(2)}) %collective-permute-start.17) | collective-permute-done | bytes 524320 | tf_op jit(solution)/shard_map/ppermute | solution.py:267
  146.1 0.6 collective-permute-done.15.u1
  146.7 0.2 copy-done.6
  146.9 0.2 copy-done.7
  147.1 0.4 copy-done.8
  147.5 7.4 %solve.1 = f32[512,1024]{1,0:T(8,128)} custom-call(s32[3]{0:T(128)} %pad_add_fusion.where_ref, f32[512,256]{1,0:T(8,128)} %update_part.1.u0, f32[512,256]{1,0:T(8,128)} %copy-done.8, f32[512,256]{1,0:T(8,128)} %copy-done.7, f32[512,256]{1,0:T(8,128)} %copy-done.6, f32[2,512,512]{2,1,0:T(8,128)} %get-tuple-element.15.x_ref, f32[512,512]{1,0:T(8,128)} %get-tuple-element.16.l_ref), custom_call_target="tpu_custom_call" | custom-call | flops 1000000000 | bytes 4194304 | tf_op jit(solution)/shard_map/solve/pallas_call | solution.py:244
  (50 shorter events, 0.9 us)
Async XLA Ops:
  0.0 2.9 %collective-permute-start.18 = (f32[512,512]{1,0:T(8,128)}, f32[512,512]{1,0:T(8,128)S(1)}, u32[]{:S(2)}, u32[]{:S(2)}) collective-permute-start(f32[512,512]{1,0:T(8,128)} %own.1), channel_id=1, source_target_pairs={{0,4},{4,0},{1,5},{5,1},{2,6},{6,2},{3,7},{7,3},{8,12},{12,8},{9,1... | collective-permute-start | bytes 3145736 | tf_op jit(solution)/shard_map/ppermute | solution.py:267
  2.9 1.0 copy-start.4
  8.7 25.2 %copy-start = (f32[512,512]{1,0:T(8,128)S(1)}, f32[512,512]{1,0:T(8,128)}, u32[]{:S(2)}) copy-start(f32[512,512]{1,0:T(8,128)} %own.1) | copy-start | bytes 3145732
  8.7 10.8 %collective-permute-start.19 = (f32[64,1280]{1,0:T(8,128)}, f32[64,1280]{1,0:T(8,128)S(1)}, u32[]{:S(2)}, u32[]{:S(2)}) collective-permute-start(f32[64,1280]{1,0:T(8,128)} %get-tuple-element.12), channel_id=1, source_target_pairs={{0,1},{1,0},{2,3},{3,2},{4,5},{5,4},{6,7},{7,6},{8,9},{9,8},{10,11... | collective-permute-start | bytes 983048 | tf_op jit(solution)/shard_map/ppermute | solution.py:267
  10.3 17.9 %collective-permute-start.20 = (f32[64,1280]{1,0:T(8,128)}, f32[64,1280]{1,0:T(8,128)S(1)}, u32[]{:S(2)}, u32[]{:S(2)}) collective-permute-start(f32[64,1280]{1,0:T(8,128)} %get-tuple-element.13), channel_id=1, source_target_pairs={{0,2},{1,3},{2,0},{3,1},{4,6},{5,7},{6,4},{7,5},{8,10},{9,11},{10,... | collective-permute-start | bytes 983048 | tf_op jit(solution)/shard_map/ppermute | solution.py:267
  13.2 17.6 %collective-permute-start.21 = (f32[64,1280]{1,0:T(8,128)}, f32[64,1280]{1,0:T(8,128)S(1)}, u32[]{:S(2)}, u32[]{:S(2)}) collective-permute-start(f32[64,1280]{1,0:T(8,128)} %get-tuple-element.14), channel_id=1, source_target_pairs={{0,3},{1,2},{2,1},{3,0},{4,7},{5,6},{6,5},{7,4},{8,11},{9,10},{10,... | collective-permute-start | bytes 983048 | tf_op jit(solution)/shard_map/ppermute | solution.py:267
  31.9 3.5 %collective-permute-start.23 = (f32[16,1280]{1,0:T(8,128)S(1)}, f32[16,1280]{1,0:T(8,128)S(1)}, u32[]{:S(2)}, u32[]{:S(2)}) collective-permute-start(f32[16,1280]{1,0:T(8,128)S(1)} %get-tuple-element.32), channel_id=1, source_target_pairs={{0,128},{1,129},{2,130},{3,131},{4,132},{5,133},{6,134},{7,135}} | collective-permute-start | bytes 245768 | tf_op jit(solution)/shard_map/ppermute | solution.py:267
  32.6 3.5 %collective-permute-start.24 = (f32[16,1280]{1,0:T(8,128)S(1)}, f32[16,1280]{1,0:T(8,128)S(1)}, u32[]{:S(2)}, u32[]{:S(2)}) collective-permute-start(f32[16,1280]{1,0:T(8,128)S(1)} %get-tuple-element.33), channel_id=1, source_target_pairs={{0,192},{1,193},{2,194},{3,195},{4,196},{5,197},{6,198},{7,199}} | collective-permute-start | bytes 245768 | tf_op jit(solution)/shard_map/ppermute | solution.py:267
  33.2 2.9 %collective-permute-start.22 = (f32[16,1280]{1,0:T(8,128)S(1)}, f32[16,1280]{1,0:T(8,128)S(1)}, u32[]{:S(2)}, u32[]{:S(2)}) collective-permute-start(f32[16,1280]{1,0:T(8,128)S(1)} %get-tuple-element.34), channel_id=1, source_target_pairs={{0,64},{1,65},{2,66},{3,67},{4,68},{5,69},{6,70},{7,71}} | collective-permute-start | bytes 245768 | tf_op jit(solution)/shard_map/ppermute | solution.py:267
  34.0 3.5 %collective-permute-start.5 = (f32[128,512]{1,0:T(8,128)S(1)}, f32[128,512]{1,0:T(8,128)S(1)}, u32[]{:S(2)}, u32[]{:S(2)}) collective-permute-start(f32[128,512]{1,0:T(8,128)S(1)} %get-tuple-element.25), channel_id=1, source_target_pairs={{0,130},{1,131},{2,128},{3,129},{4,134},{5,135},{6,132},{7,133}} | collective-permute-start | bytes 786440 | tf_op jit(solution)/shard_map/ppermute | solution.py:267
  34.7 2.8 %collective-permute-start.6 = (f32[128,512]{1,0:T(8,128)S(1)}, f32[128,512]{1,0:T(8,128)S(1)}, u32[]{:S(2)}, u32[]{:S(2)}) collective-permute-start(f32[128,512]{1,0:T(8,128)S(1)} %get-tuple-element.26), channel_id=1, source_target_pairs={{0,195},{1,194},{2,193},{3,192},{4,199},{5,198},{6,197},{7,196}} | collective-permute-start | bytes 786440 | tf_op jit(solution)/shard_map/ppermute | solution.py:267
  35.4 2.1 %collective-permute-start.4 = (f32[128,512]{1,0:T(8,128)S(1)}, f32[128,512]{1,0:T(8,128)S(1)}, u32[]{:S(2)}, u32[]{:S(2)}) collective-permute-start(f32[128,512]{1,0:T(8,128)S(1)} %get-tuple-element.27), channel_id=1, source_target_pairs={{0,65},{1,64},{2,67},{3,66},{4,69},{5,68},{6,71},{7,70}} | collective-permute-start | bytes 786440 | tf_op jit(solution)/shard_map/ppermute | solution.py:267
  36.1 2.9 %collective-permute-start.26 = (f32[16,1280]{1,0:T(8,128)S(1)}, f32[16,1280]{1,0:T(8,128)S(1)}, u32[]{:S(2)}, u32[]{:S(2)}) collective-permute-start(f32[16,1280]{1,0:T(8,128)S(1)} %slice_select_fusion), channel_id=1, source_target_pairs={{0,40},{1,41},{2,42},{3,43},{4,44},{5,45},{6,46},{7,47},{64,104},{... | collective-permute-start | bytes 245768 | tf_op jit(solution)/shard_map/ppermute | solution.py:267
  36.8 2.2 %collective-permute-start.25 = (f32[16,1280]{1,0:T(8,128)S(1)}, f32[16,1280]{1,0:T(8,128)S(1)}, u32[]{:S(2)}, u32[]{:S(2)}) collective-permute-start(f32[16,1280]{1,0:T(8,128)S(1)} %slice_select_fusion), channel_id=1, source_target_pairs={{0,24},{1,25},{2,26},{3,27},{4,28},{5,29},{6,30},{7,31},{64,88},{6... | collective-permute-start | bytes 245768 | tf_op jit(solution)/shard_map/ppermute | solution.py:267
  37.6 3.4 %collective-permute-start.8 = (f32[128,512]{1,0:T(8,128)S(1)}, f32[128,512]{1,0:T(8,128)S(1)}, u32[]{:S(2)}, u32[]{:S(2)}) collective-permute-start(f32[128,512]{1,0:T(8,128)S(1)} %add_select_fusion.2), channel_id=1, source_target_pairs={{0,40},{1,41},{2,42},{3,43},{4,44},{5,45},{6,46},{7,47},{64,104},{... | collective-permute-start | bytes 786440 | tf_op jit(solution)/shard_map/ppermute | solution.py:267
  38.3 2.7 %collective-permute-start.7 = (f32[128,512]{1,0:T(8,128)S(1)}, f32[128,512]{1,0:T(8,128)S(1)}, u32[]{:S(2)}, u32[]{:S(2)}) collective-permute-start(f32[128,512]{1,0:T(8,128)S(1)} %add_select_fusion.2), channel_id=1, source_target_pairs={{0,24},{1,25},{2,26},{3,27},{4,28},{5,29},{6,30},{7,31},{64,88},{6... | collective-permute-start | bytes 786440 | tf_op jit(solution)/shard_map/ppermute | solution.py:267
  39.0 14.3 %collective-permute-start.28 = (f32[16,1280]{1,0:T(8,128)S(1)}, f32[16,1280]{1,0:T(8,128)S(1)}, u32[]{:S(2)}, u32[]{:S(2)}) collective-permute-start(f32[16,1280]{1,0:T(8,128)S(1)} %add_select_fusion.4), channel_id=1, source_target_pairs={{0,56},{24,16},{1,57},{25,17},{2,58},{26,18},{3,59},{27,19},{4,60}... | collective-permute-start | bytes 245768 | tf_op jit(solution)/shard_map/ppermute | solution.py:267
  40.3 13.0 %collective-permute-start.27 = (f32[16,1280]{1,0:T(8,128)S(1)}, f32[16,1280]{1,0:T(8,128)S(1)}, u32[]{:S(2)}, u32[]{:S(2)}) collective-permute-start(f32[16,1280]{1,0:T(8,128)S(1)} %add_select_fusion.4), channel_id=1, source_target_pairs={{0,8},{24,32},{40,48},{1,9},{25,33},{41,49},{2,10},{26,34},{42,50}... | collective-permute-start | bytes 245768 | tf_op jit(solution)/shard_map/ppermute | solution.py:267
  41.1 21.5 %collective-permute-start.10 = (f32[128,512]{1,0:T(8,128)S(1)}, f32[128,512]{1,0:T(8,128)S(1)}, u32[]{:S(2)}, u32[]{:S(2)}) collective-permute-start(f32[128,512]{1,0:T(8,128)S(1)} %add_select_fusion.1), channel_id=1, source_target_pairs={{0,56},{24,16},{1,57},{25,17},{2,58},{26,18},{3,59},{27,19},{4,60}... | collective-permute-start | bytes 786440 | tf_op jit(solution)/shard_map/ppermute | solution.py:267
  42.4 20.2 %collective-permute-start.9 = (f32[128,512]{1,0:T(8,128)S(1)}, f32[128,512]{1,0:T(8,128)S(1)}, u32[]{:S(2)}, u32[]{:S(2)}) collective-permute-start(f32[128,512]{1,0:T(8,128)S(1)} %add_select_fusion.1), channel_id=1, source_target_pairs={{0,8},{24,32},{40,48},{1,9},{25,33},{41,49},{2,10},{26,34},{42,50}... | collective-permute-start | bytes 786440 | tf_op jit(solution)/shard_map/ppermute | solution.py:267
  53.3 15.8 %collective-permute-start.31 = (f32[16,1280]{1,0:T(8,128)S(1)}, f32[16,1280]{1,0:T(8,128)S(1)}, u32[]{:S(2)}, u32[]{:S(2)}) collective-permute-start(f32[16,1280]{1,0:T(8,128)S(1)} %add_select_fusion.3), channel_id=1, source_target_pairs={{0,1},{1,0},{2,3},{3,2},{4,5},{5,4},{6,7},{7,6},{8,9},{9,8},{10,11... | collective-permute-start | bytes 245768 | tf_op jit(solution)/shard_map/ppermute | solution.py:267
  53.4 15.8 %collective-permute-start.30 = (f32[16,1280]{1,0:T(8,128)S(1)}, f32[16,1280]{1,0:T(8,128)S(1)}, u32[]{:S(2)}, u32[]{:S(2)}) collective-permute-start(f32[16,1280]{1,0:T(8,128)S(1)} %add_select_fusion.3), channel_id=1, source_target_pairs={{0,2},{1,3},{2,0},{3,1},{4,6},{5,7},{6,4},{7,5},{8,10},{9,11},{10,... | collective-permute-start | bytes 245768 | tf_op jit(solution)/shard_map/ppermute | solution.py:267
  55.2 14.1 %collective-permute-start.29 = (f32[16,1280]{1,0:T(8,128)S(1)}, f32[16,1280]{1,0:T(8,128)S(1)}, u32[]{:S(2)}, u32[]{:S(2)}) collective-permute-start(f32[16,1280]{1,0:T(8,128)S(1)} %add_select_fusion.3), channel_id=1, source_target_pairs={{0,3},{1,2},{2,1},{3,0},{4,7},{5,6},{6,5},{7,4},{8,11},{9,10},{10,... | collective-permute-start | bytes 245768 | tf_op jit(solution)/shard_map/ppermute | solution.py:267
  62.7 11.3 %collective-permute-start.13 = (f32[128,512]{1,0:T(8,128)S(1)}, f32[128,512]{1,0:T(8,128)S(1)}, u32[]{:S(2)}, u32[]{:S(2)}) collective-permute-start(f32[128,512]{1,0:T(8,128)S(1)} %add_select_fusion), channel_id=1, source_target_pairs={{0,64},{64,0},{128,192},{192,128},{1,65},{65,1},{129,193},{193,129... | collective-permute-start | bytes 786440 | tf_op jit(solution)/shard_map/ppermute | solution.py:267
  66.4 15.7 %collective-permute-start.12 = (f32[128,512]{1,0:T(8,128)S(1)}, f32[128,512]{1,0:T(8,128)}, u32[]{:S(2)}, u32[]{:S(2)}) collective-permute-start(f32[128,512]{1,0:T(8,128)S(1)} %add_select_fusion), channel_id=1, source_target_pairs={{0,128},{64,192},{128,0},{192,64},{1,129},{65,193},{129,1},{193,65... | collective-permute-start | bytes 786440 | tf_op jit(solution)/shard_map/ppermute | solution.py:267
  69.1 15.8 %collective-permute-start.11 = (f32[128,512]{1,0:T(8,128)S(1)}, f32[128,512]{1,0:T(8,128)}, u32[]{:S(2)}, u32[]{:S(2)}) collective-permute-start(f32[128,512]{1,0:T(8,128)S(1)} %add_select_fusion), channel_id=1, source_target_pairs={{0,192},{64,128},{128,64},{192,0},{1,193},{65,129},{129,65},{193,1... | collective-permute-start | bytes 786440 | tf_op jit(solution)/shard_map/ppermute | solution.py:267
  69.3 19.0 %collective-permute-start.34 = (f32[1,4,16,1280]{3,2,0,1:T(8,128)S(1)}, f32[1,4,16,1280]{3,2,0,1:T(8,128)S(1)}, u32[]{:S(2)}, u32[]{:S(2)}) collective-permute-start(f32[1,4,16,1280]{3,2,0,1:T(8,128)S(1)} %bitcast.9), channel_id=1, source_target_pairs={{0,64},{64,0},{128,192},{192,128},{1,65},{65,1},{129,193},{193,129... | collective-permute-start | bytes 983048 | tf_op jit(solution)/shard_map/ppermute | solution.py:267
  70.3 21.2 %collective-permute-start.33 = (f32[1,4,16,1280]{3,2,0,1:T(8,128)S(1)}, f32[1,4,16,1280]{3,2,0,1:T(8,128)S(1)}, u32[]{:S(2)}, u32[]{:S(2)}) collective-permute-start(f32[1,4,16,1280]{3,2,0,1:T(8,128)S(1)} %bitcast.10), channel_id=1, source_target_pairs={{0,128},{64,192},{128,0},{192,64},{1,129},{65,193},{129,1},{193,65... | collective-permute-start | bytes 983048 | tf_op jit(solution)/shard_map/ppermute | solution.py:267
  74.0 0.7 copy-start.9
  74.7 19.5 %collective-permute-start.32 = (f32[1,4,16,1280]{3,2,0,1:T(8,128)S(1)}, f32[1,4,16,1280]{3,2,0,1:T(8,128)}, u32[]{:S(2)}, u32[]{:S(2)}) collective-permute-start(f32[1,4,16,1280]{3,2,0,1:T(8,128)S(1)} %bitcast.11), channel_id=1, source_target_pairs={{0,192},{64,128},{128,64},{192,0},{1,193},{65,129},{129,65},{193,1... | collective-permute-start | bytes 983048 | tf_op jit(solution)/shard_map/ppermute | solution.py:267
  82.1 16.8 %collective-permute-start.1 = (f32[512,512]{1,0:T(8,128)S(1)}, f32[512,512]{1,0:T(8,128)S(1)}, u32[]{:S(2)}, u32[]{:S(2)}) collective-permute-start(f32[512,512]{1,0:T(8,128)S(1)} %copy-done), channel_id=1, source_target_pairs={{0,3},{1,2},{2,1},{3,0},{4,7},{5,6},{6,5},{7,4},{8,11},{9,10},{10,... | collective-permute-start | bytes 3145736 | tf_op jit(solution)/shard_map/ppermute | solution.py:267
  84.9 15.5 %collective-permute-start = (f32[512,512]{1,0:T(8,128)S(1)}, f32[512,512]{1,0:T(8,128)S(1)}, u32[]{:S(2)}, u32[]{:S(2)}) collective-permute-start(f32[512,512]{1,0:T(8,128)S(1)} %copy-done), channel_id=1, source_target_pairs={{0,1},{1,0},{2,3},{3,2},{4,5},{5,4},{6,7},{7,6},{8,9},{9,8},{10,11... | collective-permute-start | bytes 3145736 | tf_op jit(solution)/shard_map/ppermute | solution.py:267
  96.4 29.7 %collective-permute-start.35 = (f32[256,1280]{1,0:T(8,128)}, f32[256,1280]{1,0:T(8,128)}, u32[]{:S(2)}, u32[]{:S(2)}) collective-permute-start(f32[256,1280]{1,0:T(8,128)} %bitcast.7.own), channel_id=1, source_target_pairs={{0,4},{4,0},{1,5},{5,1},{2,6},{6,2},{3,7},{7,3},{8,12},{12,8},{9,1... | collective-permute-start | bytes 3932168 | tf_op jit(solution)/shard_map/ppermute | solution.py:267
  96.5 18.6 %copy-start.1 = (f32[512,512]{1,0:T(8,128)}, f32[512,512]{1,0:T(8,128)S(1)}, u32[]{:S(2)}) copy-start(f32[512,512]{1,0:T(8,128)S(1)} %pad_maximum_fusion.1.own) | copy-start | bytes 3145732
  96.5 18.6 %collective-permute-start.14 = (f32[512,512]{1,0:T(8,128)S(1)}, f32[512,512]{1,0:T(8,128)}, u32[]{:S(2)}, u32[]{:S(2)}) collective-permute-start(f32[512,512]{1,0:T(8,128)S(1)} %pad_maximum_fusion.1.own), channel_id=1, source_target_pairs={{0,4},{4,0},{1,5},{5,1},{2,6},{6,2},{3,7},{7,3},{8,12},{12,8},{9,1... | collective-permute-start | bytes 3145736 | tf_op jit(solution)/shard_map/ppermute | solution.py:267
  98.9 16.2 %copy-start.2 = (f32[512,512]{1,0:T(8,128)}, f32[512,512]{1,0:T(8,128)S(1)}, u32[]{:S(2)}) copy-start(f32[512,512]{1,0:T(8,128)S(1)} %collective-permute-done.1.p3) | copy-start | bytes 3145732
  98.9 12.7 %collective-permute-start.2 = (f32[256,512]{1,0:T(8,128)S(1)}, f32[256,512]{1,0:T(8,128)}, u32[]{:S(2)}, u32[]{:S(2)}) collective-permute-start(f32[256,512]{1,0:T(8,128)S(1)} %slice.24), channel_id=1, source_target_pairs={{0,1},{1,0},{2,3},{3,2},{4,5},{5,4},{6,7},{7,6},{8,9},{9,8},{10,11... | collective-permute-start | bytes 1572872 | tf_op jit(solution)/shard_map/ppermute | solution.py:267
  100.5 1.0 copy-start.3
  101.5 13.6 %collective-permute-start.3 = (f32[256,512]{1,0:T(8,128)S(1)}, f32[256,512]{1,0:T(8,128)S(1)}, u32[]{:S(2)}, u32[]{:S(2)}) collective-permute-start(f32[256,512]{1,0:T(8,128)S(1)} %slice.25), channel_id=1, source_target_pairs={{0,3},{1,2},{2,1},{3,0},{4,7},{5,6},{6,5},{7,4},{8,11},{9,10},{10,... | collective-permute-start | bytes 1572872 | tf_op jit(solution)/shard_map/ppermute | solution.py:267
  115.1 0.8 copy-start.5
  122.0 24.1 %collective-permute-start.17 = (f32[512,256]{1,0:T(8,128)}, f32[512,256]{1,0:T(8,128)S(1)}, u32[]{:S(2)}, u32[]{:S(2)}) collective-permute-start(f32[512,256]{1,0:T(8,128)} %update_part.1.u0), channel_id=1, source_target_pairs={{0,3},{1,2},{2,1},{3,0},{4,7},{5,6},{6,5},{7,4},{8,11},{9,10},{10,... | collective-permute-start | bytes 1572872 | tf_op jit(solution)/shard_map/ppermute | solution.py:267
  122.4 23.7 %collective-permute-start.16 = (f32[512,256]{1,0:T(8,128)}, f32[512,256]{1,0:T(8,128)S(1)}, u32[]{:S(2)}, u32[]{:S(2)}) collective-permute-start(f32[512,256]{1,0:T(8,128)} %update_part.1.u0), channel_id=1, source_target_pairs={{0,2},{1,3},{2,0},{3,1},{4,6},{5,7},{6,4},{7,5},{8,10},{9,11},{10,... | collective-permute-start | bytes 1572872 | tf_op jit(solution)/shard_map/ppermute | solution.py:267
  123.4 23.3 %collective-permute-start.15 = (f32[512,256]{1,0:T(8,128)}, f32[512,256]{1,0:T(8,128)S(1)}, u32[]{:S(2)}, u32[]{:S(2)}) collective-permute-start(f32[512,256]{1,0:T(8,128)} %update_part.1.u0), channel_id=1, source_target_pairs={{0,1},{1,0},{2,3},{3,2},{4,5},{5,4},{6,7},{7,6},{8,9},{9,8},{10,11... | collective-permute-start | bytes 1572872 | tf_op jit(solution)/shard_map/ppermute | solution.py:267
  146.1 0.8 copy-start.6
  146.1 1.0 copy-start.7
  146.7 0.8 copy-start.8

commit v3 on v2

--- a/solution.py
+++ b/solution.py
@@ -5,6 +5,7 @@
 NB=512
 H=256
 CENTRE, RADIUS = 7.0, 5.0
+GRANT = 24 * 2**20
 CHEB = 6
 NEWTON = 2
 
@@ -86,48 +87,87 @@
 F32 = jnp.float32
 
 
+CHUNK = 160
+PIECE = CHUNK // 4
+
+
 def block_kernel(where_ref, own, other, a_ref, *refs):
-    outs, part, a_part = refs[:4], refs[4], refs[5]
+    outs, part = refs[:4], refs[4]
     first, y = where_ref[0] == 0, where_ref[1]
+    n = H // 4
     t0, t1 = split(own[:H, :]), split(own[H:, :])
     part[:, :H] = -dot3(t0, t0, False, True)
     part[:, H : 2 * H] = -dot3(t1, t0, False, True)
     part[:, 2 * H : 3 * H] = -dot3(t1, t1, False, True)
+
+    def rows_of(start, size):
+        return pl.ds(pl.multiple_of(start + y * n, size), size)
+
+    above, below = rows_of(0, n), rows_of(H, n)
+    out = outs[0]
 
     @pl.when(first)
     def _():
         q = split(other[:H, :])
         part[:, 3 * H : 4 * H] = -dot3(t0, q, False, True)
         part[:, 4 * H :] = -dot3(t1, q, False, True)
-        a_part[:, :H] = a_ref[:H, :H]
-        a_part[:, H : 2 * H] = a_ref[H:, :H]
-        a_part[:, 2 * H : 3 * H] = a_ref[H:, H:NB]
-        a_part[:, 3 * H : 4 * H] = a_ref[:H, NB : NB + H]
-        a_part[:, 4 * H :] = a_ref[H:, NB : NB + H]
+        out[:n, :H] = a_ref[above, :H]
+        out[:n, H:] = a_ref[below, :H]
+        out[n : 2 * n, :H] = a_ref[below, H:NB]
+        out[n : 2 * n, H:] = a_ref[above, NB : NB + H]
+        out[2 * n :, :H] = a_ref[rows_of(H, n // 2), NB : NB + H]
+        out[2 * n :, H:] = a_ref[rows_of(H + n // 2, n // 2), NB : NB + H]
 
     @pl.when(jnp.logical_not(first))
     def _():
-        part[:, 3 * H : 4 * H] = -dot3(split(other[:H, :]), t1, False, True)
-        part[:, 4 * H :] = -dot3(split(other[H:, :]), t1, False, True)
-        a_part[:, :H] = a_ref[:H, NB : NB + H]
-        a_part[:, H : 2 * H] = a_ref[H:, NB : NB + H]
-        a_part[:, 2 * H : 3 * H] = a_ref[H:, NB + H :]
-        a_part[:, 3 * H : 4 * H] = a_ref[H:, :H].T
-        a_part[:, 4 * H :] = a_ref[H:, H:NB].T
-
+        part[:, 3 * H : 4 * H] = -dot3(t1, split(other[:H, :]), False, True)
+        part[:, 4 * H :] = -dot3(t1, split(other[H:, :]), False, True)
+        out[:n, :H] = a_ref[above, NB : NB + H]
+        out[:n, H:] = a_ref[below, NB : NB + H]
+        out[n : 2 * n, :H] = a_ref[below, NB + H :]
+        out[n : 2 * n, H:] = a_ref[below, :H]
+        out[2 * n :, :H] = a_ref[rows_of(H, n // 2), H:NB]
+        out[2 * n :, H:] = a_ref[rows_of(H + n // 2, n // 2), H:NB]
+
+    for s in range(4):
+        q = y ^ s
+        rows = pl.ds(pl.multiple_of(q * n, n), n)
+        top = pl.ds(pl.multiple_of(q * n, n // 2), n // 2)
+        bottom = pl.ds(pl.multiple_of(q * n + n // 2, n // 2), n // 2)
+        new = part[rows, :NB], part[rows, NB : 2 * NB], part[top, 4 * H :], part[bottom, 4 * H :]
+        to = (
+            (slice(0, n), slice(0, NB)),
+            (slice(n, 2 * n), slice(0, NB)),
+            (slice(2 * n, CHUNK), slice(0, H)),
+            (slice(2 * n, CHUNK), slice(H, NB)),
+        )
+        for place, value in zip(to, new):
+            outs[s][place] = value + out[place] if s == 0 else value
+
+
+def lay_out(m, got):
     n = H // 4
-    outs[0][...] = part[pl.ds(y * n, n), :] + a_part[pl.ds(y * n, n), :]
-    for s in (1, 2, 3):
-        outs[s][...] = part[pl.ds((y ^ s) * n, n), :]
+    for y in range(4):
+        for x in range(4):
+            for i in range(x * PIECE, (x + 1) * PIECE, 8):
+                v = got[x, y, i - x * PIECE : i - x * PIECE + 8, :]
+                if i < 2 * n:
+                    part, row = i // n, i % n
+                    m[y * n + row : y * n + row + 8, part * NB : (part + 1) * NB] = v
+                else:
+                    row = y * n + i - 2 * n
+                    m[row : row + 8, 4 * H :] = v[:, :H]
+                    m[row + n // 2 : row + n // 2 + 8, 4 * H :] = v[:, H:]
 
 
 def block_parts(where, own, other, a_cols):
     return pl.pallas_call(
         block_kernel,
-        out_shape=(jax.ShapeDtypeStruct((H // 4, 5 * H), F32),) * 4,
+        out_shape=(jax.ShapeDtypeStruct((CHUNK, NB), F32),) * 4,
         in_specs=[SMEM, VMEM, VMEM, VMEM],
         out_specs=(VMEM,) * 4,
-        scratch_shapes=[pltpu.VMEM((H, 5 * H), F32)] * 2,
+        scratch_shapes=[pltpu.VMEM((H, 5 * H), F32)],
+        compiler_params=pltpu.CompilerParams(vmem_limit_bytes=GRANT),
         cost_estimate=pl.CostEstimate(flops=10**9, bytes_accessed=2**22, transcendentals=0),
         name="block_parts",
     )(where, own, other, a_cols)
@@ -136,13 +176,13 @@
 def factor_kernel(where_ref, own, other, x_ref, l_ref, m0, m1):
     @pl.when(where_ref[0] == 0)
     def _():
-        m0[...] = own[...]
-        m1[...] = other[...]
+        lay_out(m0, own)
+        lay_out(m1, other)
 
     @pl.when(where_ref[0] != 0)
     def _():
-        m0[...] = other[...]
-        m1[...] = own[...]
+        lay_out(m0, other)
+        lay_out(m1, own)
 
     def tile(m, i):
         return m[:, i * H : (i + 1) * H]
@@ -158,8 +198,8 @@
     t00, t10, t11 = split(x00), split(x10), split(x11)
     for j, m in enumerate((m0, m1)):
         top, bot = split(tile(m, 3)), split(tile(m, 4))
-        l_ref[:H, j * H : (j + 1) * H] = dot3(t00, top)
-        l_ref[H:, j * H : (j + 1) * H] = dot3(t10, top) + dot3(t11, bot)
+        l_ref[:H, j * H : (j + 1) * H] = dot3(t00, top, False, j == 1)
+        l_ref[H:, j * H : (j + 1) * H] = dot3(t10, top, False, j == 1) + dot3(t11, bot, False, j == 1)
     p0, p1 = split(l_ref[:, :H]), split(l_ref[:, H:])
     c00 = tile(m1, 0) - dot3(p0, p0, True, False)
     c10 = tile(m1, 1) - dot3(p1, p0, True, False)
@@ -174,47 +214,66 @@
         in_specs=[SMEM] + [VMEM] * 2,
         out_specs=(VMEM,) * 2,
         scratch_shapes=[pltpu.VMEM((H, 5 * H), F32)] * 2,
+        compiler_params=pltpu.CompilerParams(vmem_limit_bytes=GRANT),
         cost_estimate=pl.CostEstimate(flops=5 * 10**9, bytes_accessed=2**23, transcendentals=0),
         name="factor",
     )(where, own, other)
 
 
-def update_kernel(where_ref, p0, p1, p2a, p2b, p3, own, other, a_ref, out, ph, pl_, th, tl):
+def put_split(hi, lo, row, column, src, low=0):
+    step = 32
+    for r in range(0, src.shape[0], step):
+        v = src[r : r + step, :]
+        columns = slice(column, column + src.shape[1])
+        hi[row + r : row + r + step, columns], lo[low + row + r : low + row + r + step, columns] = split(v)
+
+
+def rows_kernel(p0, p1a, p1b, p2a, p2b, p3a, p3b, hi, lo):
+    put_split(hi, lo, 0, 0, p0)
+    for t, (above, below) in enumerate(((p1b, p1a), (p2a, p2b), (p3a, p3b))):
+        put_split(hi, lo, 0, (t + 1) * NB, above)
+        put_split(hi, lo, H, (t + 1) * NB, below)
+
+
+def split_rows(*past):
+    return pl.pallas_call(
+        rows_kernel,
+        out_shape=(jax.ShapeDtypeStruct((NB, 4 * NB), jnp.bfloat16),) * 2,
+        in_specs=[VMEM] * 7,
+        out_specs=(VMEM,) * 2,
+        compiler_params=pltpu.CompilerParams(vmem_limit_bytes=GRANT),
+        cost_estimate=pl.CostEstimate(flops=10**8, bytes_accessed=2**23, transcendentals=0),
+        name="split_rows",
+    )(*past)
+
+
+def update_kernel(where_ref, ph, pl_, own, other, a_ref, out, th):
     core, y = where_ref[0], where_ref[1]
     n = 128
-
-    def put(hi, lo, rows, t, v):
-        columns = slice(t * NB, (t + 1) * NB)
-        hi[rows, columns], lo[rows, columns] = split(v)
-
-    every = slice(0, NB)
-    put(ph, pl_, every, 0, p0[...])
-    put(ph, pl_, every, 1, p1[...])
-    put(ph, pl_, slice(0, H), 2, p2a[...])
-    put(ph, pl_, slice(H, NB), 2, p2b[...])
-    put(ph, pl_, every, 3, p3[...])
     for t in range(4):
-        put(th, tl, slice(0, n), t, own[t * n : (t + 1) * n, :])
-        put(th, tl, slice(n, 2 * n), t, other[t * n : (t + 1) * n, :])
-    total = dot3((ph[...], pl_[...]), (th[...], tl[...]), False, True)
+        put_split(th, th, 0, t * NB, own.at[t * n : (t + 1) * n, :], H)
+        put_split(th, th, n, t * NB, other.at[t * n : (t + 1) * n, :], H)
+    both = dot1(ph[...], th[...], False, True)
+    total = both[:, :H] + (both[:, H:] + dot1(pl_[...], th[:H, :], False, True))
     for i, half in enumerate((core, 1 - core)):
         columns = pl.ds(pl.multiple_of(half * NB + y * n, n), n)
         out[:, pl.ds(pl.multiple_of(half * n, n), n)] = a_ref[:, columns] - total[:, i * n : (i + 1) * n]
 
 
-def update_part(where, past, own, other, a_cols):
+def update_part(where, rows, own, other, a_cols):
     return pl.pallas_call(
         update_kernel,
         out_shape=jax.ShapeDtypeStruct((NB, 256), F32),
-        in_specs=[SMEM] + [VMEM] * 8,
+        in_specs=[SMEM] + [VMEM] * 5,
         out_specs=VMEM,
-        scratch_shapes=[pltpu.VMEM((r, 4 * NB), jnp.bfloat16) for r in (NB, NB, H, H)],
+        scratch_shapes=[pltpu.VMEM((NB, 4 * NB), jnp.bfloat16)],
+        compiler_params=pltpu.CompilerParams(vmem_limit_bytes=GRANT),
         cost_estimate=pl.CostEstimate(flops=10**9, bytes_accessed=2**22, transcendentals=0),
         name="update_part",
-    )(where, *past, own, other, a_cols)
-
-
-def solve_kernel(where_ref, u0, u1, u2, u3, x_ref, l_ref, out, s1, s2):
+    )(where, *rows, own, other, a_cols)
+
+
+def solve_kernel(where_ref, u0, u1, u2, u3, x_ref, l_ref, out, s1, s2, h, lo, w, v):
     y, position = where_ref[1], where_ref[2]
     n = 128
     for u, piece in enumerate((u0, u1, u2, u3)):
@@ -222,22 +281,25 @@
         s1[:, columns] = piece[:, :n]
         s2[:, columns] = piece[:, n:]
 
-    def keep(v, start):
-        rows = position * NB + lax.broadcasted_iota(jnp.int32, v.shape, 0)
-        return jnp.where(rows >= start + lax.broadcasted_iota(jnp.int32, v.shape, 1), v, 0.0)
-
-    def times_inverse(i, s, start):
-        left, right = split(s[:, :H]), split(s[:, H:])
-        a = dot3(left, split(x_ref[i, :H, :H]), False, True)
-        b = dot3(left, split(x_ref[i, H:, :H]), False, True) + dot3(right, split(x_ref[i, H:, H:]), False, True)
-        out[:, start : start + H] = keep(a, start)
-        out[:, start + H : start + NB] = keep(b, start + H)
-        return a, b
-
-    a, b = times_inverse(0, s1, 0)
-    a, b = split(a), split(b)
-    s2[...] = s2[...] - (dot3(a, split(l_ref[:H, :])) + dot3(b, split(l_ref[H:, :])))
-    times_inverse(1, s2, NB)
+    def product(left, right, transposed):
+        put_split(h, lo, 0, 0, left)
+        put_split(w, v, 0, 0, right)
+        return dot3((h[...], lo[...]), (w[...], v[...]), False, transposed)
+
+    def keep(start):
+        rows = position * NB + lax.broadcasted_iota(jnp.int32, (NB, NB), 0)
+        columns = slice(start, start + NB)
+        kept = rows >= start + lax.broadcasted_iota(jnp.int32, (NB, NB), 1)
+        out[:, columns] = jnp.where(kept, out[:, columns], 0.0)
+
+    out[:, :NB] = product(s1, x_ref.at[0], True)
+    s2[...] = s2[...] - product(out.at[:, :NB], l_ref, False)
+    out[:, NB:] = product(s2, x_ref.at[1], True)
+
+    @pl.when(position < 2)
+    def _():
+        keep(0)
+        keep(NB)
 
 
 def solve(where, pieces, inverse, below):
@@ -246,7 +308,8 @@
         out_shape=jax.ShapeDtypeStruct((NB, 2 * NB), F32),
         in_specs=[SMEM] + [VMEM] * 6,
         out_specs=VMEM,
-        scratch_shapes=[pltpu.VMEM((NB, NB), F32)] * 2,
+        scratch_shapes=[pltpu.VMEM((NB, NB), F32)] * 2 + [pltpu.VMEM((NB, NB), jnp.bfloat16)] * 4,
+        compiler_params=pltpu.CompilerParams(vmem_limit_bytes=GRANT),
         cost_estimate=pl.CostEstimate(flops=10**9, bytes_accessed=2**22, transcendentals=0),
         name="solve",
     )(where, *pieces, inverse, below)
@@ -317,23 +380,23 @@
     parts = block_parts(where, past, other, a_cols)
     block = parts[0]
     for s in (1, 2, 3):
-        block = block + exchange(parts[s], "depth", s)
-
-    near1, near3 = exchange(past, "depth", 1), exchange(past, "depth", 3)
-    far = exchange(near3[:H], "depth", 1), exchange(near1[H:], "depth", 3)
-    rows = past, near1, *far, near3
-
-    top = in_order(pieces_along(spread_z(top, z), "row"), x)
-    top_other = swap_core(top)
-
-    n = block.shape[0] // 4
+        block = block + send(parts[s], BOX, [(d, d ^ s) for d in range(4)])
+
+    near1, near3 = exchange(past[H:], "depth", 1), exchange(past[:H], "depth", 3)
+    far1, far3 = exchange(near3, "depth", 1), exchange(near1, "depth", 3)
+    rest1, rest3 = exchange(past[:H], "depth", 1), exchange(past[H:], "depth", 3)
+    rows = split_rows(past, near1, rest1, far1, far3, near3, rest3)
+
     got = 0.0
     for p in (1, 2, 3):
-        got = got + send(block[p * n : (p + 1) * n], PLANE, [(0, 8 * p)], True)
-    spread = spread_z(jnp.where(root, block[:n], got), z)
-    spread = in_order(pieces_along(spread, "depth"), y).reshape(4, n, -1)
-    spread = in_order(pieces_along(spread[None], "row"), x)
-    block = spread.transpose(1, 0, 2, 3).reshape(H, -1)
+        got = got + send(block[p * PIECE : (p + 1) * PIECE], PLANE, [(0, 8 * p)], True)
+    both = spread_z(jnp.concatenate([top, jnp.where(root, block[:PIECE], got)]), z)
+
+    top = in_order(pieces_along(both[:128], "row"), x)
+    top_other = swap_core(top)
+
+    block = in_order(pieces_along(both[128:][None], "depth"), y)
+    block = in_order(pieces_along(block[None], "row"), x)
     block_other = swap_core(block)
 
     update = update_part(where, rows, top, top_other, a_cols)
@@ -349,6 +412,4 @@
     )
 
     placed = (P(ROW_COL, None), P(ROW_COL, "depth"))
-    return jax.shard_map(
-        body, mesh=split_mesh, in_specs=placed, out_specs=P(ROW_COL, None), check_vma=False
-    )
+    return jax.shard_map(body, mesh=split_mesh, in_specs=placed, out_specs=P(ROW_COL, None), check_vma=False)

time: 155 us -> 157 us (1.013)
  the two profiles are of different devices: /device:TPU:70 before, /device:TPU:94 now
where the time goes in v3:
time: 157 us
  waiting for transfers between devices  83.7 us (53%)
  starting transfers between devices  43.3 us (28%)
  Pallas kernels  20.3 us (13%)
  local copies, waits for them, and re-layouts  4.75 us (3%)
  other arithmetic  4.33 us (3%)
    ppermute x34, waiting for transfers between devices, send(): return lax.ppermute(v, axis, pairs)  83.7 us
    ppermute x34, starting transfers between devices, send(): return lax.ppermute(v, axis, pairs)  43.3 us
    pallas_call x1, Pallas kernels, factor(): pl.pallas_call(factor_kernel, out_shape=(jax.ShapeDtypeStruct((2, NB, NB)...  10.5 us
    pallas_call x1, Pallas kernels, solve(): pl.pallas_call(solve_kernel, out_shape=jax.ShapeDtypeStruct((NB, 2 * NB),...  4.82 us
  transfers between devices with their start and end apart: 34, of which 12 were waited for; matrix products, arithmetic and copies ran while one was open for 4% of the time, Pallas kernels for 9%

profile of v3, /device:TPU:94, one launch (start us, length us, event | category | flops | bytes accessed | tf_op | source)
XLA Modules:
  0.0 156.7 jit_solution(6149288394444224980)
XLA Ops:
  0.0 0.0 collective-permute-start.9
  0.0 0.1 pad_add_fusion.where_ref
  0.1 2.8 %collective-permute-done.9.other = f32[512,512]{1,0:T(8,128)S(1)} collective-permute-done((f32[512,512]{1,0:T(8,128)}, f32[512,512]{1,0:T(8,128)S(1)}, u32[]{:S(2)}, u32[]{:S(2)}) %collective-permute-start.9) | collective-permute-done | bytes 1048608 | tf_op jit(solution)/shard_map/ppermute | solution.py:330
  2.9 1.2 copy-done
  4.1 1.6 %copy-done.2 = f32[512,1024]{1,0:T(8,128)S(1)} copy-done((f32[512,1024]{1,0:T(8,128)S(1)}, f32[512,1024]{1,0:T(8,128)}, u32[]{:S(2)}) %copy-start.2) | copy-done | bytes 2097176
  5.7 2.1 %block_parts.1 = (f32[160,512]{1,0:T(8,128)S(1)}, f32[160,512]{1,0:T(8,128)S(1)}, f32[160,512]{1,0:T(8,128)S(1)}, f32[160,512]{1,0:T(8,128)S(1)}) custom-call(s32[3]{0:T(128)S(1)} %pad_add_fusion.where_ref, f32[512,512]{1,0:T(8,128)S(1)} %copy-done, f32[512,512]{1,0:T(8,128)S(1)} %collective-permute-done.9.other, f32[512,1024]{1,0:T(8,128)S(1)} %copy-done.2), custom_call_target="tpu_custom_call" | custom-call | flops 1000000000 | bytes 4194304 | tf_op jit(solution)/shard_map/block_parts/pallas_call | solution.py:164
  7.8 0.7 collective-permute-start.12
  8.4 1.4 collective-permute-start.11
  9.8 1.4 collective-permute-start.10
  11.2 0.8 constant_dynamic-slice_fusion.1
  12.1 1.3 collective-permute-start.8
  13.4 1.4 collective-permute-start.6
  14.8 0.7 collective-permute-start.7
  15.5 1.2 add_add_fusion
  16.7 0.7 collective-permute-start.15
  17.4 0.7 collective-permute-start.13
  18.0 0.7 collective-permute-start.14
  18.7 1.1 add_select_fusion.2
  20.0 0.7 collective-permute-start.16
  20.7 0.7 collective-permute-start.17
  21.4 0.1 add_select_fusion.1
  21.5 0.7 collective-permute-start.18
  22.1 1.3 collective-permute-start.19
  23.5 29.6 %collective-permute-done.19 = f32[168,512]{1,0:T(8,128)S(1)} collective-permute-done((f32[168,512]{1,0:T(8,128)S(1)}, f32[168,512]{1,0:T(8,128)S(1)}, u32[]{:S(2)}, u32[]{:S(2)}) %collective-permute-start.19) | collective-permute-done | bytes 344096 | tf_op jit(solution)/shard_map/ppermute | solution.py:330
  53.1 0.1 add_select_fusion
  53.2 2.0 %collective-permute-start.27 = (f32[1,40,512]{2,1,0:T(8,128)S(1)}, f32[1,40,512]{2,1,0:T(8,128)S(1)}, u32[]{:S(2)}, u32[]{:S(2)}) collective-permute-start(f32[1,40,512]{2,1,0:T(8,128)S(1)} %slice_bitcast_fusion), channel_id=1, source_target_pairs={{0,3},{1,2},{2,1},{3,0},{4,7},{5,6},{6,5},{7,4},{8,11},{9,10},{10,... | collective-permute-start | bytes 245768 | tf_op jit(solution)/shard_map/ppermute | solution.py:330
  55.2 0.9 collective-permute-start.28
  56.1 1.3 collective-permute-start.29
  57.4 4.5 %collective-permute-start.20 = (f32[128,512]{1,0:T(8,128)S(1)}, f32[128,512]{1,0:T(8,128)}, u32[]{:S(2)}, u32[]{:S(2)}) collective-permute-start(f32[128,512]{1,0:T(8,128)S(1)} %slice.38), channel_id=1, source_target_pairs={{0,192},{64,128},{128,64},{192,0},{1,193},{65,129},{129,65},{193,1... | collective-permute-start | bytes 786440 | tf_op jit(solution)/shard_map/ppermute | solution.py:330
  61.9 2.8 %collective-permute-start.21 = (f32[128,512]{1,0:T(8,128)S(1)}, f32[128,512]{1,0:T(8,128)}, u32[]{:S(2)}, u32[]{:S(2)}) collective-permute-start(f32[128,512]{1,0:T(8,128)S(1)} %slice.38), channel_id=1, source_target_pairs={{0,128},{64,192},{128,0},{192,64},{1,129},{65,193},{129,1},{193,65... | collective-permute-start | bytes 786440 | tf_op jit(solution)/shard_map/ppermute | solution.py:330
  64.8 2.2 %collective-permute-start.31 = (f32[1,4,40,512]{3,2,1,0:T(8,128)S(1)}, f32[1,4,40,512]{3,2,1,0:T(8,128)S(1)}, u32[]{:S(2)}, u32[]{:S(2)}) collective-permute-start(f32[1,4,40,512]{3,2,1,0:T(8,128)S(1)} %maximum_bitcast_fusion), channel_id=1, source_target_pairs={{0,128},{64,192},{128,0},{192,64},{1,129},{65,193},{129,1},{193,65... | collective-permute-start | bytes 983048 | tf_op jit(solution)/shard_map/ppermute | solution.py:330
  67.0 2.5 %collective-permute-start.30 = (f32[1,4,40,512]{3,2,1,0:T(8,128)S(1)}, f32[1,4,40,512]{3,2,1,0:T(8,128)S(1)}, u32[]{:S(2)}, u32[]{:S(2)}) collective-permute-start(f32[1,4,40,512]{3,2,1,0:T(8,128)S(1)} %maximum_bitcast_fusion), channel_id=1, source_target_pairs={{0,192},{64,128},{128,64},{192,0},{1,193},{65,129},{129,65},{193,1... | collective-permute-start | bytes 983048 | tf_op jit(solution)/shard_map/ppermute | solution.py:330
  69.6 6.3 %collective-permute-done.20 = f32[128,512]{1,0:T(8,128)} collective-permute-done((f32[128,512]{1,0:T(8,128)S(1)}, f32[128,512]{1,0:T(8,128)}, u32[]{:S(2)}, u32[]{:S(2)}) %collective-permute-start.20) | collective-permute-done | bytes 262176 | tf_op jit(solution)/shard_map/ppermute | solution.py:330
  75.8 2.8 %collective-permute-start.32 = (f32[1,4,40,512]{3,2,1,0:T(8,128)S(1)}, f32[1,4,40,512]{3,2,1,0:T(8,128)S(1)}, u32[]{:S(2)}, u32[]{:S(2)}) collective-permute-start(f32[1,4,40,512]{3,2,1,0:T(8,128)S(1)} %maximum_bitcast_fusion), channel_id=1, source_target_pairs={{0,64},{64,0},{128,192},{192,128},{1,65},{65,1},{129,193},{193,129... | collective-permute-start | bytes 983048 | tf_op jit(solution)/shard_map/ppermute | solution.py:330
  78.6 1.0 fusion
  79.7 0.6 collective-permute-start.1
  80.3 1.6 %collective-permute-start.2 = (f32[256,512]{1,0:T(8,128)}, f32[256,512]{1,0:T(8,128)S(1)}, u32[]{:S(2)}, u32[]{:S(2)}) collective-permute-start(f32[256,512]{1,0:T(8,128)} %get-tuple-element.31), channel_id=1, source_target_pairs={{0,3},{1,2},{2,1},{3,0},{4,7},{5,6},{6,5},{7,4},{8,11},{9,10},{10,... | collective-permute-start | bytes 1572872 | tf_op jit(solution)/shard_map/ppermute | solution.py:330
  81.9 1.2 broadcast_select_fusion.15
  83.1 1.6 %collective-permute-done.31 = f32[1,4,40,512]{3,2,1,0:T(8,128)S(1)} collective-permute-done((f32[1,4,40,512]{3,2,1,0:T(8,128)S(1)}, f32[1,4,40,512]{3,2,1,0:T(8,128)S(1)}, u32[]{:S(2)}, u32[]{:S(2)}) %collective-permute-start.31) | collective-permute-done | bytes 327712 | tf_op jit(solution)/shard_map/ppermute | solution.py:330
  84.7 0.2 collective-permute-start
  85.0 0.4 collective-permute-done.30
  85.3 1.4 collective-permute-done.32
  86.7 0.1 broadcast_select_fusion.4
  86.9 0.2 broadcast_select_fusion.7
  87.0 0.1 pad_maximum_fusion.own
  87.2 0.1 collective-permute-start.33
  87.3 0.1 pad_maximum_fusion.1.own
  87.3 0.0 copy-start.3
  87.3 0.8 collective-permute-start.23
  88.1 13.4 %collective-permute-done.p1a = f32[256,512]{1,0:T(8,128)S(1)} collective-permute-done((f32[256,512]{1,0:T(8,128)}, f32[256,512]{1,0:T(8,128)S(1)}, u32[]{:S(2)}, u32[]{:S(2)}) %collective-permute-start) | collective-permute-done | bytes 524320 | tf_op jit(solution)/shard_map/ppermute | solution.py:330
  101.5 2.6 %collective-permute-start.5 = (f32[256,512]{1,0:T(8,128)}, f32[256,512]{1,0:T(8,128)S(1)}, u32[]{:S(2)}, u32[]{:S(2)}) collective-permute-start(f32[256,512]{1,0:T(8,128)} %get-tuple-element.32), channel_id=1, source_target_pairs={{0,3},{1,2},{2,1},{3,0},{4,7},{5,6},{6,5},{7,4},{8,11},{9,10},{10,... | collective-permute-start | bytes 1572872 | tf_op jit(solution)/shard_map/ppermute | solution.py:330
  104.2 0.2 collective-permute-start.3
  104.4 0.6 collective-permute-start.4
  105.0 7.1 %collective-permute-done.5.p3b = f32[256,512]{1,0:T(8,128)S(1)} collective-permute-done((f32[256,512]{1,0:T(8,128)}, f32[256,512]{1,0:T(8,128)S(1)}, u32[]{:S(2)}, u32[]{:S(2)}) %collective-permute-start.5) | collective-permute-done | bytes 524320 | tf_op jit(solution)/shard_map/ppermute | solution.py:330
  112.1 4.9 %collective-permute-done.3.p2a = f32[256,512]{1,0:T(8,128)S(1)} collective-permute-done((f32[256,512]{1,0:T(8,128)S(1)}, f32[256,512]{1,0:T(8,128)S(1)}, u32[]{:S(2)}, u32[]{:S(2)}) %collective-permute-start.3) | collective-permute-done | bytes 524320 | tf_op jit(solution)/shard_map/ppermute | solution.py:330
  117.0 10.6 %collective-permute-done.4.p2b = f32[256,512]{1,0:T(8,128)S(1)} collective-permute-done((f32[256,512]{1,0:T(8,128)S(1)}, f32[256,512]{1,0:T(8,128)S(1)}, u32[]{:S(2)}, u32[]{:S(2)}) %collective-permute-start.4) | collective-permute-done | bytes 524320 | tf_op jit(solution)/shard_map/ppermute | solution.py:330
  127.7 0.5 split_rows.1
  128.2 2.4 %update_part.1.u0 = f32[512,256]{1,0:T(8,128)S(1)} custom-call(s32[3]{0:T(128)S(1)} %pad_add_fusion.where_ref, bf16[512,2048]{1,0:T(8,128)(2,1)S(1)} %get-tuple-element.13.ph, bf16[512,2048]{1,0:T(8,128)(2,1)S(1)} %get-tuple-element.14.pl_, f32[512,512]{1,0:T(8,128)S(1)} %pad_maximum_fusion.1.own, f32[512,512]{1,0:T(8,128)S(1)} %collective-permute-done.23.other, ...), custom_call_target="tpu_custom_call" | custom-call | flops 1000000000 | bytes 4194304 | tf_op jit(solution)/shard_map/update_part/pallas_call | solution.py:264
  130.6 0.6 collective-permute-start.24
  131.2 4.7 %collective-permute-start.25 = (f32[512,256]{1,0:T(8,128)S(1)}, f32[512,256]{1,0:T(8,128)S(1)}, u32[]{:S(2)}, u32[]{:S(2)}) collective-permute-start(f32[512,256]{1,0:T(8,128)S(1)} %update_part.1.u0), channel_id=1, source_target_pairs={{0,2},{1,3},{2,0},{3,1},{4,6},{5,7},{6,4},{7,5},{8,10},{9,11},{10,... | collective-permute-start | bytes 1572872 | tf_op jit(solution)/shard_map/ppermute | solution.py:330
  135.9 10.5 %factor.1 = (f32[2,512,512]{2,1,0:T(8,128)S(1)}, f32[512,512]{1,0:T(8,128)S(1)}) custom-call(s32[3]{0:T(128)S(1)} %pad_add_fusion.where_ref, f32[4,4,40,512]{3,2,1,0:T(8,128)S(1)} %pad_maximum_fusion.own, f32[4,4,40,512]{3,2,1,0:T(8,128)S(1)} %collective-permute-done.33.other), custom_call_target="tpu_custom_call" | custom-call | flops 5000000000 | bytes 8388608 | tf_op jit(solution)/shard_map/factor/pallas_call | solution.py:211
  146.4 2.3 %collective-permute-done.25.u2 = f32[512,256]{1,0:T(8,128)S(1)} collective-permute-done((f32[512,256]{1,0:T(8,128)S(1)}, f32[512,256]{1,0:T(8,128)S(1)}, u32[]{:S(2)}, u32[]{:S(2)}) %collective-permute-start.25) | collective-permute-done | bytes 524320 | tf_op jit(solution)/shard_map/ppermute | solution.py:330
  148.7 3.1 %collective-permute-done.26.u3 = f32[512,256]{1,0:T(8,128)S(1)} collective-permute-done((f32[512,256]{1,0:T(8,128)S(1)}, f32[512,256]{1,0:T(8,128)S(1)}, u32[]{:S(2)}, u32[]{:S(2)}) %collective-permute-start.26) | collective-permute-done | bytes 524320 | tf_op jit(solution)/shard_map/ppermute | solution.py:330
  151.9 4.8 %solve.1 = f32[512,1024]{1,0:T(8,128)} custom-call(s32[3]{0:T(128)S(1)} %pad_add_fusion.where_ref, f32[512,256]{1,0:T(8,128)S(1)} %update_part.1.u0, f32[512,256]{1,0:T(8,128)S(1)} %collective-permute-done.24.u1, f32[512,256]{1,0:T(8,128)S(1)} %collective-permute-done.25.u2, f32[512,256]{1,0:T(8,128)S(1)} %collective-permute-done.26.u3, ...), custom_call_target="tpu_custom_call" | custom-call | flops 1000000000 | bytes 4194304 | tf_op jit(solution)/shard_map/solve/pallas_call | solution.py:306
  (36 shorter events, 0.2 us)
Async XLA Ops:
  0.0 2.9 %collective-permute-start.9 = (f32[512,512]{1,0:T(8,128)}, f32[512,512]{1,0:T(8,128)S(1)}, u32[]{:S(2)}, u32[]{:S(2)}) collective-permute-start(f32[512,512]{1,0:T(8,128)} %own.1), channel_id=1, source_target_pairs={{0,4},{4,0},{1,5},{5,1},{2,6},{6,2},{3,7},{7,3},{8,12},{12,8},{9,1... | collective-permute-start | bytes 3145736 | tf_op jit(solution)/shard_map/ppermute | solution.py:330
  2.9 1.2 copy-start
  4.1 1.6 %copy-start.2 = (f32[512,1024]{1,0:T(8,128)S(1)}, f32[512,1024]{1,0:T(8,128)}, u32[]{:S(2)}) copy-start(f32[512,1024]{1,0:T(8,128)} %a_ref.3) | copy-start | bytes 6291460
  5.7 5.5 %copy-start.1 = (f32[512,512]{1,0:T(8,128)S(1)}, f32[512,512]{1,0:T(8,128)}, u32[]{:S(2)}) copy-start(f32[512,512]{1,0:T(8,128)} %own.1) | copy-start | bytes 3145732
  7.8 7.0 %collective-permute-start.12 = (f32[160,512]{1,0:T(8,128)S(1)}, f32[160,512]{1,0:T(8,128)S(1)}, u32[]{:S(2)}, u32[]{:S(2)}) collective-permute-start(f32[160,512]{1,0:T(8,128)S(1)} %get-tuple-element.18), channel_id=1, source_target_pairs={{0,3},{1,2},{2,1},{3,0},{4,7},{5,6},{6,5},{7,4}} | collective-permute-start | bytes 983048 | tf_op jit(solution)/shard_map/ppermute | solution.py:330
  8.4 7.0 %collective-permute-start.11 = (f32[160,512]{1,0:T(8,128)S(1)}, f32[160,512]{1,0:T(8,128)}, u32[]{:S(2)}, u32[]{:S(2)}) collective-permute-start(f32[160,512]{1,0:T(8,128)S(1)} %get-tuple-element.17), channel_id=1, source_target_pairs={{0,2},{1,3},{2,0},{3,1},{4,6},{5,7},{6,4},{7,5}} | collective-permute-start | bytes 983048 | tf_op jit(solution)/shard_map/ppermute | solution.py:330
  9.8 5.6 %collective-permute-start.10 = (f32[160,512]{1,0:T(8,128)S(1)}, f32[160,512]{1,0:T(8,128)}, u32[]{:S(2)}, u32[]{:S(2)}) collective-permute-start(f32[160,512]{1,0:T(8,128)S(1)} %get-tuple-element.16), channel_id=1, source_target_pairs={{0,1},{1,0},{2,3},{3,2},{4,5},{5,4},{6,7},{7,6}} | collective-permute-start | bytes 983048 | tf_op jit(solution)/shard_map/ppermute | solution.py:330
  12.1 6.0 %collective-permute-start.8 = (f32[128,512]{1,0:T(8,128)}, f32[128,512]{1,0:T(8,128)}, u32[]{:S(2)}, u32[]{:S(2)}) collective-permute-start(f32[128,512]{1,0:T(8,128)} %get-tuple-element.29), channel_id=1, source_target_pairs={{0,195},{1,194},{2,193},{3,192},{4,199},{5,198},{6,197},{7,196}} | collective-permute-start | bytes 786440 | tf_op jit(solution)/shard_map/ppermute | solution.py:330
  13.4 5.3 %collective-permute-start.6 = (f32[128,512]{1,0:T(8,128)}, f32[128,512]{1,0:T(8,128)}, u32[]{:S(2)}, u32[]{:S(2)}) collective-permute-start(f32[128,512]{1,0:T(8,128)} %get-tuple-element.30), channel_id=1, source_target_pairs={{0,65},{1,64},{2,67},{3,66},{4,69},{5,68},{6,71},{7,70}} | collective-permute-start | bytes 786440 | tf_op jit(solution)/shard_map/ppermute | solution.py:330
  14.8 4.0 %collective-permute-start.7 = (f32[128,512]{1,0:T(8,128)S(1)}, f32[128,512]{1,0:T(8,128)S(1)}, u32[]{:S(2)}, u32[]{:S(2)}) collective-permute-start(f32[128,512]{1,0:T(8,128)S(1)} %get-tuple-element.28), channel_id=1, source_target_pairs={{0,130},{1,131},{2,128},{3,129},{4,134},{5,135},{6,132},{7,133}} | collective-permute-start | bytes 786440 | tf_op jit(solution)/shard_map/ppermute | solution.py:330
  16.7 3.2 %collective-permute-start.15 = (f32[40,512]{1,0:T(8,128)S(1)}, f32[40,512]{1,0:T(8,128)S(1)}, u32[]{:S(2)}, u32[]{:S(2)}) collective-permute-start(f32[40,512]{1,0:T(8,128)S(1)} %get-tuple-element.38), channel_id=1, source_target_pairs={{0,192},{1,193},{2,194},{3,195},{4,196},{5,197},{6,198},{7,199}} | collective-permute-start | bytes 245768 | tf_op jit(solution)/shard_map/ppermute | solution.py:330
  17.4 2.5 %collective-permute-start.13 = (f32[40,512]{1,0:T(8,128)S(1)}, f32[40,512]{1,0:T(8,128)S(1)}, u32[]{:S(2)}, u32[]{:S(2)}) collective-permute-start(f32[40,512]{1,0:T(8,128)S(1)} %get-tuple-element.39), channel_id=1, source_target_pairs={{0,64},{1,65},{2,66},{3,67},{4,68},{5,69},{6,70},{7,71}} | collective-permute-start | bytes 245768 | tf_op jit(solution)/shard_map/ppermute | solution.py:330
  18.0 1.8 %collective-permute-start.14 = (f32[40,512]{1,0:T(8,128)S(1)}, f32[40,512]{1,0:T(8,128)S(1)}, u32[]{:S(2)}, u32[]{:S(2)}) collective-permute-start(f32[40,512]{1,0:T(8,128)S(1)} %get-tuple-element.37), channel_id=1, source_target_pairs={{0,128},{1,129},{2,130},{3,131},{4,132},{5,133},{6,134},{7,135}} | collective-permute-start | bytes 245768 | tf_op jit(solution)/shard_map/ppermute | solution.py:330
  20.0 1.4 collective-permute-start.16
  20.7 0.7 collective-permute-start.17
  21.5 2.0 %collective-permute-start.18 = (f32[168,512]{1,0:T(8,128)S(1)}, f32[168,512]{1,0:T(8,128)S(1)}, u32[]{:S(2)}, u32[]{:S(2)}) collective-permute-start(f32[168,512]{1,0:T(8,128)S(1)} %add_select_fusion.1), channel_id=1, source_target_pairs={{0,8},{24,32},{40,48},{1,9},{25,33},{41,49},{2,10},{26,34},{42,50}... | collective-permute-start | bytes 1032200 | tf_op jit(solution)/shard_map/ppermute | solution.py:330
  22.1 30.9 %collective-permute-start.19 = (f32[168,512]{1,0:T(8,128)S(1)}, f32[168,512]{1,0:T(8,128)S(1)}, u32[]{:S(2)}, u32[]{:S(2)}) collective-permute-start(f32[168,512]{1,0:T(8,128)S(1)} %add_select_fusion.1), channel_id=1, source_target_pairs={{0,56},{24,16},{1,57},{25,17},{2,58},{26,18},{3,59},{27,19},{4,60}... | collective-permute-start | bytes 1032200 | tf_op jit(solution)/shard_map/ppermute | solution.py:330
  53.2 11.5 %collective-permute-start.27 = (f32[1,40,512]{2,1,0:T(8,128)S(1)}, f32[1,40,512]{2,1,0:T(8,128)S(1)}, u32[]{:S(2)}, u32[]{:S(2)}) collective-permute-start(f32[1,40,512]{2,1,0:T(8,128)S(1)} %slice_bitcast_fusion), channel_id=1, source_target_pairs={{0,3},{1,2},{2,1},{3,0},{4,7},{5,6},{6,5},{7,4},{8,11},{9,10},{10,... | collective-permute-start | bytes 245768 | tf_op jit(solution)/shard_map/ppermute | solution.py:330
  55.2 9.5 %collective-permute-start.28 = (f32[1,40,512]{2,1,0:T(8,128)S(1)}, f32[1,40,512]{2,1,0:T(8,128)S(1)}, u32[]{:S(2)}, u32[]{:S(2)}) collective-permute-start(f32[1,40,512]{2,1,0:T(8,128)S(1)} %slice_bitcast_fusion), channel_id=1, source_target_pairs={{0,2},{1,3},{2,0},{3,1},{4,6},{5,7},{6,4},{7,5},{8,10},{9,11},{10,... | collective-permute-start | bytes 245768 | tf_op jit(solution)/shard_map/ppermute | solution.py:330
  56.1 8.6 %collective-permute-start.29 = (f32[1,40,512]{2,1,0:T(8,128)S(1)}, f32[1,40,512]{2,1,0:T(8,128)S(1)}, u32[]{:S(2)}, u32[]{:S(2)}) collective-permute-start(f32[1,40,512]{2,1,0:T(8,128)S(1)} %slice_bitcast_fusion), channel_id=1, source_target_pairs={{0,1},{1,0},{2,3},{3,2},{4,5},{5,4},{6,7},{7,6},{8,9},{9,8},{10,11... | collective-permute-start | bytes 245768 | tf_op jit(solution)/shard_map/ppermute | solution.py:330
  57.4 18.5 %collective-permute-start.20 = (f32[128,512]{1,0:T(8,128)S(1)}, f32[128,512]{1,0:T(8,128)}, u32[]{:S(2)}, u32[]{:S(2)}) collective-permute-start(f32[128,512]{1,0:T(8,128)S(1)} %slice.38), channel_id=1, source_target_pairs={{0,192},{64,128},{128,64},{192,0},{1,193},{65,129},{129,65},{193,1... | collective-permute-start | bytes 786440 | tf_op jit(solution)/shard_map/ppermute | solution.py:330
  61.9 17.8 %collective-permute-start.21 = (f32[128,512]{1,0:T(8,128)S(1)}, f32[128,512]{1,0:T(8,128)}, u32[]{:S(2)}, u32[]{:S(2)}) collective-permute-start(f32[128,512]{1,0:T(8,128)S(1)} %slice.38), channel_id=1, source_target_pairs={{0,128},{64,192},{128,0},{192,64},{1,129},{65,193},{129,1},{193,65... | collective-permute-start | bytes 786440 | tf_op jit(solution)/shard_map/ppermute | solution.py:330
  64.7 15.6 %collective-permute-start.22 = (f32[128,512]{1,0:T(8,128)S(1)}, f32[128,512]{1,0:T(8,128)}, u32[]{:S(2)}, u32[]{:S(2)}) collective-permute-start(f32[128,512]{1,0:T(8,128)S(1)} %slice.38), channel_id=1, source_target_pairs={{0,64},{64,0},{128,192},{192,128},{1,65},{65,1},{129,193},{193,129... | collective-permute-start | bytes 786440 | tf_op jit(solution)/shard_map/ppermute | solution.py:330
  64.8 19.9 %collective-permute-start.31 = (f32[1,4,40,512]{3,2,1,0:T(8,128)S(1)}, f32[1,4,40,512]{3,2,1,0:T(8,128)S(1)}, u32[]{:S(2)}, u32[]{:S(2)}) collective-permute-start(f32[1,4,40,512]{3,2,1,0:T(8,128)S(1)} %maximum_bitcast_fusion), channel_id=1, source_target_pairs={{0,128},{64,192},{128,0},{192,64},{1,129},{65,193},{129,1},{193,65... | collective-permute-start | bytes 983048 | tf_op jit(solution)/shard_map/ppermute | solution.py:330
  67.0 18.3 %collective-permute-start.30 = (f32[1,4,40,512]{3,2,1,0:T(8,128)S(1)}, f32[1,4,40,512]{3,2,1,0:T(8,128)S(1)}, u32[]{:S(2)}, u32[]{:S(2)}) collective-permute-start(f32[1,4,40,512]{3,2,1,0:T(8,128)S(1)} %maximum_bitcast_fusion), channel_id=1, source_target_pairs={{0,192},{64,128},{128,64},{192,0},{1,193},{65,129},{129,65},{193,1... | collective-permute-start | bytes 983048 | tf_op jit(solution)/shard_map/ppermute | solution.py:330
  75.8 10.9 %collective-permute-start.32 = (f32[1,4,40,512]{3,2,1,0:T(8,128)S(1)}, f32[1,4,40,512]{3,2,1,0:T(8,128)S(1)}, u32[]{:S(2)}, u32[]{:S(2)}) collective-permute-start(f32[1,4,40,512]{3,2,1,0:T(8,128)S(1)} %maximum_bitcast_fusion), channel_id=1, source_target_pairs={{0,64},{64,0},{128,192},{192,128},{1,65},{65,1},{129,193},{193,129... | collective-permute-start | bytes 983048 | tf_op jit(solution)/shard_map/ppermute | solution.py:330
  79.7 24.7 %collective-permute-start.1 = (f32[256,512]{1,0:T(8,128)}, f32[256,512]{1,0:T(8,128)S(1)}, u32[]{:S(2)}, u32[]{:S(2)}) collective-permute-start(f32[256,512]{1,0:T(8,128)} %get-tuple-element.31), channel_id=1, source_target_pairs={{0,1},{1,0},{2,3},{3,2},{4,5},{5,4},{6,7},{7,6},{8,9},{9,8},{10,11... | collective-permute-start | bytes 1572872 | tf_op jit(solution)/shard_map/ppermute | solution.py:330
  80.3 23.9 %collective-permute-start.2 = (f32[256,512]{1,0:T(8,128)}, f32[256,512]{1,0:T(8,128)S(1)}, u32[]{:S(2)}, u32[]{:S(2)}) collective-permute-start(f32[256,512]{1,0:T(8,128)} %get-tuple-element.31), channel_id=1, source_target_pairs={{0,3},{1,2},{2,1},{3,0},{4,7},{5,6},{6,5},{7,4},{8,11},{9,10},{10,... | collective-permute-start | bytes 1572872 | tf_op jit(solution)/shard_map/ppermute | solution.py:330
  84.7 16.8 %collective-permute-start = (f32[256,512]{1,0:T(8,128)}, f32[256,512]{1,0:T(8,128)S(1)}, u32[]{:S(2)}, u32[]{:S(2)}) collective-permute-start(f32[256,512]{1,0:T(8,128)} %get-tuple-element.32), channel_id=1, source_target_pairs={{0,1},{1,0},{2,3},{3,2},{4,5},{5,4},{6,7},{7,6},{8,9},{9,8},{10,11... | collective-permute-start | bytes 1572872 | tf_op jit(solution)/shard_map/ppermute | solution.py:330
  87.2 48.7 %collective-permute-start.33 = (f32[4,4,40,512]{3,2,1,0:T(8,128)S(1)}, f32[4,4,40,512]{3,2,1,0:T(8,128)S(1)}, u32[]{:S(2)}, u32[]{:S(2)}) collective-permute-start(f32[4,4,40,512]{3,2,1,0:T(8,128)S(1)} %pad_maximum_fusion.own), channel_id=1, source_target_pairs={{0,4},{4,0},{1,5},{5,1},{2,6},{6,2},{3,7},{7,3},{8,12},{12,8},{9,1... | collective-permute-start | bytes 3932168 | tf_op jit(solution)/shard_map/ppermute | solution.py:330
  87.3 40.8 %copy-start.3 = (f32[512,1024]{1,0:T(8,128)S(1)}, f32[512,1024]{1,0:T(8,128)}, u32[]{:S(2)}) copy-start(f32[512,1024]{1,0:T(8,128)} %a_ref.3) | copy-start | bytes 6291460
  87.3 40.8 %collective-permute-start.23 = (f32[512,512]{1,0:T(8,128)S(1)}, f32[512,512]{1,0:T(8,128)S(1)}, u32[]{:S(2)}, u32[]{:S(2)}) collective-permute-start(f32[512,512]{1,0:T(8,128)S(1)} %pad_maximum_fusion.1.own), channel_id=1, source_target_pairs={{0,4},{4,0},{1,5},{5,1},{2,6},{6,2},{3,7},{7,3},{8,12},{12,8},{9,1... | collective-permute-start | bytes 3145736 | tf_op jit(solution)/shard_map/ppermute | solution.py:330
  101.5 10.6 %collective-permute-start.5 = (f32[256,512]{1,0:T(8,128)}, f32[256,512]{1,0:T(8,128)S(1)}, u32[]{:S(2)}, u32[]{:S(2)}) collective-permute-start(f32[256,512]{1,0:T(8,128)} %get-tuple-element.32), channel_id=1, source_target_pairs={{0,3},{1,2},{2,1},{3,0},{4,7},{5,6},{6,5},{7,4},{8,11},{9,10},{10,... | collective-permute-start | bytes 1572872 | tf_op jit(solution)/shard_map/ppermute | solution.py:330
  104.2 12.9 %collective-permute-start.3 = (f32[256,512]{1,0:T(8,128)S(1)}, f32[256,512]{1,0:T(8,128)S(1)}, u32[]{:S(2)}, u32[]{:S(2)}) collective-permute-start(f32[256,512]{1,0:T(8,128)S(1)} %collective-permute-done.2.p3a), channel_id=1, source_target_pairs={{0,1},{1,0},{2,3},{3,2},{4,5},{5,4},{6,7},{7,6},{8,9},{9,8},{10,11... | collective-permute-start | bytes 1572872 | tf_op jit(solution)/shard_map/ppermute | solution.py:330
  104.4 23.3 %collective-permute-start.4 = (f32[256,512]{1,0:T(8,128)S(1)}, f32[256,512]{1,0:T(8,128)S(1)}, u32[]{:S(2)}, u32[]{:S(2)}) collective-permute-start(f32[256,512]{1,0:T(8,128)S(1)} %collective-permute-done.p1a), channel_id=1, source_target_pairs={{0,3},{1,2},{2,1},{3,0},{4,7},{5,6},{6,5},{7,4},{8,11},{9,10},{10,... | collective-permute-start | bytes 1572872 | tf_op jit(solution)/shard_map/ppermute | solution.py:330
  130.6 15.8 %collective-permute-start.24 = (f32[512,256]{1,0:T(8,128)S(1)}, f32[512,256]{1,0:T(8,128)S(1)}, u32[]{:S(2)}, u32[]{:S(2)}) collective-permute-start(f32[512,256]{1,0:T(8,128)S(1)} %update_part.1.u0), channel_id=1, source_target_pairs={{0,1},{1,0},{2,3},{3,2},{4,5},{5,4},{6,7},{7,6},{8,9},{9,8},{10,11... | collective-permute-start | bytes 1572872 | tf_op jit(solution)/shard_map/ppermute | solution.py:330
  131.2 17.6 %collective-permute-start.25 = (f32[512,256]{1,0:T(8,128)S(1)}, f32[512,256]{1,0:T(8,128)S(1)}, u32[]{:S(2)}, u32[]{:S(2)}) collective-permute-start(f32[512,256]{1,0:T(8,128)S(1)} %update_part.1.u0), channel_id=1, source_target_pairs={{0,2},{1,3},{2,0},{3,1},{4,6},{5,7},{6,4},{7,5},{8,10},{9,11},{10,... | collective-permute-start | bytes 1572872 | tf_op jit(solution)/shard_map/ppermute | solution.py:330
  135.9 16.0 %collective-permute-start.26 = (f32[512,256]{1,0:T(8,128)S(1)}, f32[512,256]{1,0:T(8,128)S(1)}, u32[]{:S(2)}, u32[]{:S(2)}) collective-permute-start(f32[512,256]{1,0:T(8,128)S(1)} %update_part.1.u0), channel_id=1, source_target_pairs={{0,3},{1,2},{2,1},{3,0},{4,7},{5,6},{6,5},{7,4},{8,11},{9,10},{10,... | collective-permute-start | bytes 1572872 | tf_op jit(solution)/shard_map/ppermute | solution.py:330

commit v4 on v3

--- a/solution.py
+++ b/solution.py
@@ -84,6 +84,7 @@
 
 VMEM = pl.BlockSpec(memory_space=pltpu.VMEM)
 SMEM = pl.BlockSpec(memory_space=pltpu.SMEM)
+HBM = pl.BlockSpec(memory_space=pltpu.HBM)
 F32 = jnp.float32
 
 
@@ -92,42 +93,58 @@
 
 
 def block_kernel(where_ref, own, other, a_ref, *refs):
-    outs, part = refs[:4], refs[4]
+    outs, part, a_rows, sems = refs[:4], refs[4], refs[5], refs[6]
     first, y = where_ref[0] == 0, where_ref[1]
     n = H // 4
+
+    def rows_of(start, size):
+        return pl.ds(pl.multiple_of(start + y * n, size), size)
+
+    def copies(places):
+        to = ((0, n, 0), (0, n, H), (n, n, 0), (n, n, H), (2 * n, n // 2, 0), (2 * n, n // 2, H))
+        return [
+            pltpu.make_async_copy(
+                a_ref.at[rows_of(start, size), column : column + H],
+                a_rows.at[row : row + size, side : side + H],
+                sems.at[i],
+            )
+            for i, ((row, size, side), (start, column)) in enumerate(zip(to, places))
+        ]
+
+    places = (
+        ((0, 0), (H, 0), (H, H), (0, NB), (H, NB), (H + n // 2, NB)),
+        ((0, NB), (H, NB), (H, NB + H), (H, 0), (H, H), (H + n // 2, H)),
+    )
+
+    @pl.when(first)
+    def _():
+        for copy in copies(places[0]):
+            copy.start()
+
+    @pl.when(jnp.logical_not(first))
+    def _():
+        for copy in copies(places[1]):
+            copy.start()
+
     t0, t1 = split(own[:H, :]), split(own[H:, :])
     part[:, :H] = -dot3(t0, t0, False, True)
     part[:, H : 2 * H] = -dot3(t1, t0, False, True)
     part[:, 2 * H : 3 * H] = -dot3(t1, t1, False, True)
 
-    def rows_of(start, size):
-        return pl.ds(pl.multiple_of(start + y * n, size), size)
-
-    above, below = rows_of(0, n), rows_of(H, n)
-    out = outs[0]
-
     @pl.when(first)
     def _():
         q = split(other[:H, :])
         part[:, 3 * H : 4 * H] = -dot3(t0, q, False, True)
         part[:, 4 * H :] = -dot3(t1, q, False, True)
-        out[:n, :H] = a_ref[above, :H]
-        out[:n, H:] = a_ref[below, :H]
-        out[n : 2 * n, :H] = a_ref[below, H:NB]
-        out[n : 2 * n, H:] = a_ref[above, NB : NB + H]
-        out[2 * n :, :H] = a_ref[rows_of(H, n // 2), NB : NB + H]
-        out[2 * n :, H:] = a_ref[rows_of(H + n // 2, n // 2), NB : NB + H]
+        for copy in copies(places[0]):
+            copy.wait()
 
     @pl.when(jnp.logical_not(first))
     def _():
         part[:, 3 * H : 4 * H] = -dot3(t1, split(other[:H, :]), False, True)
         part[:, 4 * H :] = -dot3(t1, split(other[H:, :]), False, True)
-        out[:n, :H] = a_ref[above, NB : NB + H]
-        out[:n, H:] = a_ref[below, NB : NB + H]
-        out[n : 2 * n, :H] = a_ref[below, NB + H :]
-        out[n : 2 * n, H:] = a_ref[below, :H]
-        out[2 * n :, :H] = a_ref[rows_of(H, n // 2), H:NB]
-        out[2 * n :, H:] = a_ref[rows_of(H + n // 2, n // 2), H:NB]
+        for copy in copies(places[1]):
+            copy.wait()
 
     for s in range(4):
         q = y ^ s
@@ -142,7 +159,7 @@
             (slice(2 * n, CHUNK), slice(H, NB)),
         )
         for place, value in zip(to, new):
-            outs[s][place] = value + out[place] if s == 0 else value
+            outs[s][place] = value + a_rows[place] if s == 0 else value
 
 
 def lay_out(m, got):
@@ -164,9 +181,13 @@
     return pl.pallas_call(
         block_kernel,
         out_shape=(jax.ShapeDtypeStruct((CHUNK, NB), F32),) * 4,
-        in_specs=[SMEM, VMEM, VMEM, VMEM],
+        in_specs=[SMEM, VMEM, VMEM, HBM],
         out_specs=(VMEM,) * 4,
-        scratch_shapes=[pltpu.VMEM((H, 5 * H), F32)],
+        scratch_shapes=[
+            pltpu.VMEM((H, 5 * H), F32),
+            pltpu.VMEM((CHUNK, NB), F32),
+            pltpu.SemaphoreType.DMA((6,)),
+        ],
         compiler_params=pltpu.CompilerParams(vmem_limit_bytes=GRANT),
         cost_estimate=pl.CostEstimate(flops=10**9, bytes_accessed=2**22, transcendentals=0),
         name="block_parts",
@@ -228,9 +249,9 @@
         hi[row + r : row + r + step, columns], lo[low + row + r : low + row + r + step, columns] = split(v)
 
 
-def rows_kernel(p0, p1a, p1b, p2a, p2b, p3a, p3b, hi, lo):
+def rows_kernel(p0, p1a, p1b, p3a, p3b, hi, lo):
     put_split(hi, lo, 0, 0, p0)
-    for t, (above, below) in enumerate(((p1b, p1a), (p2a, p2b), (p3a, p3b))):
+    for t, (above, below) in enumerate(((p1b, p1a), (p3a, p3b))):
         put_split(hi, lo, 0, (t + 1) * NB, above)
         put_split(hi, lo, H, (t + 1) * NB, below)
 
@@ -238,8 +259,8 @@
 def split_rows(*past):
     return pl.pallas_call(
         rows_kernel,
-        out_shape=(jax.ShapeDtypeStruct((NB, 4 * NB), jnp.bfloat16),) * 2,
-        in_specs=[VMEM] * 7,
+        out_shape=(jax.ShapeDtypeStruct((NB, 3 * NB), jnp.bfloat16),) * 2,
+        in_specs=[VMEM] * 5,
         out_specs=(VMEM,) * 2,
         compiler_params=pltpu.CompilerParams(vmem_limit_bytes=GRANT),
         cost_estimate=pl.CostEstimate(flops=10**8, bytes_accessed=2**23, transcendentals=0),
@@ -247,30 +268,36 @@
     )(*past)
 
 
-def update_kernel(where_ref, ph, pl_, own, other, a_ref, out, th):
+def update_kernel(where_ref, ph, pl_, far1, far3, own, other, a_ref, out, th, fh, fl):
     core, y = where_ref[0], where_ref[1]
     n = 128
-    for t in range(4):
-        put_split(th, th, 0, t * NB, own.at[t * n : (t + 1) * n, :], H)
-        put_split(th, th, n, t * NB, other.at[t * n : (t + 1) * n, :], H)
-    both = dot1(ph[...], th[...], False, True)
-    total = both[:, :H] + (both[:, H:] + dot1(pl_[...], th[:H, :], False, True))
+    for place, t in enumerate((0, 1, 3, 2)):
+        put_split(th, th, 0, place * NB, own.at[t * n : (t + 1) * n, :], H)
+        put_split(th, th, n, place * NB, other.at[t * n : (t + 1) * n, :], H)
+    put_split(fh, fl, 0, 0, far1)
+    put_split(fh, fl, H, 0, far3)
+
+    def product(hi, lo, columns):
+        both = dot1(hi[...], th[:, columns], False, True)
+        return both[:, :H] + (both[:, H:] + dot1(lo[...], th[:H, columns], False, True))
+
+    total = product(ph, pl_, slice(0, 3 * NB)) + product(fh, fl, slice(3 * NB, 4 * NB))
     for i, half in enumerate((core, 1 - core)):
         columns = pl.ds(pl.multiple_of(half * NB + y * n, n), n)
         out[:, pl.ds(pl.multiple_of(half * n, n), n)] = a_ref[:, columns] - total[:, i * n : (i + 1) * n]
 
 
-def update_part(where, rows, own, other, a_cols):
+def update_part(where, rows, far, own, other, a_cols):
     return pl.pallas_call(
         update_kernel,
         out_shape=jax.ShapeDtypeStruct((NB, 256), F32),
-        in_specs=[SMEM] + [VMEM] * 5,
+        in_specs=[SMEM] + [VMEM] * 7,
         out_specs=VMEM,
-        scratch_shapes=[pltpu.VMEM((NB, 4 * NB), jnp.bfloat16)],
+        scratch_shapes=[pltpu.VMEM((NB, c * NB), jnp.bfloat16) for c in (4, 1, 1)],
         compiler_params=pltpu.CompilerParams(vmem_limit_bytes=GRANT),
         cost_estimate=pl.CostEstimate(flops=10**9, bytes_accessed=2**22, transcendentals=0),
         name="update_part",
-    )(where, *rows, own, other, a_cols)
+    )(where, *rows, *far, own, other, a_cols)
 
 
 def solve_kernel(where_ref, u0, u1, u2, u3, x_ref, l_ref, out, s1, s2, h, lo, w, v):
@@ -385,7 +412,7 @@
     near1, near3 = exchange(past[H:], "depth", 1), exchange(past[:H], "depth", 3)
     far1, far3 = exchange(near3, "depth", 1), exchange(near1, "depth", 3)
     rest1, rest3 = exchange(past[:H], "depth", 1), exchange(past[H:], "depth", 3)
-    rows = split_rows(past, near1, rest1, far1, far3, near3, rest3)
+    rows = split_rows(past, near1, rest1, near3, rest3)
 
     got = 0.0
     for p in (1, 2, 3):
@@ -399,7 +426,7 @@
     block = in_order(pieces_along(block[None], "row"), x)
     block_other = swap_core(block)
 
-    update = update_part(where, rows, top, top_other, a_cols)
+    update = update_part(where, rows, (far1, far3), top, top_other, a_cols)
     pieces = pieces_along(update, "depth")
     inverse, below = factor(where, block, block_other)
     return solve(where, pieces, inverse, below)

time: 157 us -> 157 us (level)
  no operation moved by 1% of the time
where the time goes in v4:
time: 157 us
  waiting for transfers between devices  83.5 us (53%)
  starting transfers between devices  43.3 us (28%)
  Pallas kernels  20.4 us (13%)
  local copies, waits for them, and re-layouts  4.75 us (3%)
  other arithmetic  4.36 us (3%)
    ppermute x34, waiting for transfers between devices, send(): return lax.ppermute(v, axis, pairs)  83.5 us
    ppermute x34, starting transfers between devices, send(): return lax.ppermute(v, axis, pairs)  43.3 us
    pallas_call x1, Pallas kernels, factor(): pl.pallas_call(factor_kernel, out_shape=(jax.ShapeDtypeStruct((2, NB, NB)...  10.5 us
    pallas_call x1, Pallas kernels, solve(): pl.pallas_call(solve_kernel, out_shape=jax.ShapeDtypeStruct((NB, 2 * NB),...  4.82 us
  transfers between devices with their start and end apart: 34, of which 12 were waited for; matrix products, arithmetic and copies ran while one was open for 4% of the time, Pallas kernels for 9%

profile of v4, /device:TPU:94, one launch (start us, length us, event | category | flops | bytes accessed | tf_op | source)
XLA Modules:
  0.0 156.6 jit_solution(1818906346400913924)
XLA Ops:
  0.0 0.0 collective-permute-start.9
  0.0 0.1 pad_add_fusion.where_ref
  0.1 2.8 %collective-permute-done.9.other = f32[512,512]{1,0:T(8,128)S(1)} collective-permute-done((f32[512,512]{1,0:T(8,128)}, f32[512,512]{1,0:T(8,128)S(1)}, u32[]{:S(2)}, u32[]{:S(2)}) %collective-permute-start.9) | collective-permute-done | bytes 1048608 | tf_op jit(solution)/shard_map/ppermute | solution.py:357
  2.9 1.2 copy-done
  4.1 1.6 %copy-done.2 = f32[512,1024]{1,0:T(8,128)S(1)} copy-done((f32[512,1024]{1,0:T(8,128)S(1)}, f32[512,1024]{1,0:T(8,128)}, u32[]{:S(2)}) %copy-start.2) | copy-done | bytes 2097176
  5.7 2.2 %block_parts.1 = (f32[160,512]{1,0:T(8,128)S(1)}, f32[160,512]{1,0:T(8,128)S(1)}, f32[160,512]{1,0:T(8,128)S(1)}, f32[160,512]{1,0:T(8,128)S(1)}) custom-call(s32[3]{0:T(128)S(1)} %pad_add_fusion.where_ref, f32[512,512]{1,0:T(8,128)S(1)} %copy-done, f32[512,512]{1,0:T(8,128)S(1)} %collective-permute-done.9.other, f32[512,1024]{1,0:T(8,128)S(1)} %copy-done.2), custom_call_target="tpu_custom_call" | custom-call | flops 1000000000 | bytes 4194304 | tf_op jit(solution)/shard_map/block_parts/pallas_call | solution.py:181
  7.9 0.7 collective-permute-start.12
  8.6 1.4 collective-permute-start.11
  10.0 1.4 collective-permute-start.10
  11.4 0.8 constant_dynamic-slice_fusion.1
  12.2 1.3 collective-permute-start.8
  13.6 1.4 collective-permute-start.6
  14.9 0.7 collective-permute-start.7
  15.6 1.2 add_add_fusion
  16.8 0.7 collective-permute-start.15
  17.5 0.7 collective-permute-start.13
  18.2 0.7 collective-permute-start.14
  18.9 1.1 add_select_fusion.2
  20.1 0.7 collective-permute-start.16
  20.8 0.7 collective-permute-start.17
  21.5 0.1 add_select_fusion.1
  21.6 0.7 collective-permute-start.18
  22.3 1.3 collective-permute-start.19
  23.6 29.6 %collective-permute-done.19 = f32[168,512]{1,0:T(8,128)S(1)} collective-permute-done((f32[168,512]{1,0:T(8,128)S(1)}, f32[168,512]{1,0:T(8,128)S(1)}, u32[]{:S(2)}, u32[]{:S(2)}) %collective-permute-start.19) | collective-permute-done | bytes 344096 | tf_op jit(solution)/shard_map/ppermute | solution.py:357
  53.2 0.1 add_select_fusion
  53.3 2.0 %collective-permute-start.27 = (f32[1,40,512]{2,1,0:T(8,128)S(1)}, f32[1,40,512]{2,1,0:T(8,128)S(1)}, u32[]{:S(2)}, u32[]{:S(2)}) collective-permute-start(f32[1,40,512]{2,1,0:T(8,128)S(1)} %slice_bitcast_fusion), channel_id=1, source_target_pairs={{0,3},{1,2},{2,1},{3,0},{4,7},{5,6},{6,5},{7,4},{8,11},{9,10},{10,... | collective-permute-start | bytes 245768 | tf_op jit(solution)/shard_map/ppermute | solution.py:357
  55.3 0.9 collective-permute-start.28
  56.2 1.3 collective-permute-start.29
  57.5 4.5 %collective-permute-start.20 = (f32[128,512]{1,0:T(8,128)S(1)}, f32[128,512]{1,0:T(8,128)}, u32[]{:S(2)}, u32[]{:S(2)}) collective-permute-start(f32[128,512]{1,0:T(8,128)S(1)} %slice.38), channel_id=1, source_target_pairs={{0,192},{64,128},{128,64},{192,0},{1,193},{65,129},{129,65},{193,1... | collective-permute-start | bytes 786440 | tf_op jit(solution)/shard_map/ppermute | solution.py:357
  62.0 2.8 %collective-permute-start.21 = (f32[128,512]{1,0:T(8,128)S(1)}, f32[128,512]{1,0:T(8,128)}, u32[]{:S(2)}, u32[]{:S(2)}) collective-permute-start(f32[128,512]{1,0:T(8,128)S(1)} %slice.38), channel_id=1, source_target_pairs={{0,128},{64,192},{128,0},{192,64},{1,129},{65,193},{129,1},{193,65... | collective-permute-start | bytes 786440 | tf_op jit(solution)/shard_map/ppermute | solution.py:357
  64.9 2.2 %collective-permute-start.31 = (f32[1,4,40,512]{3,2,1,0:T(8,128)S(1)}, f32[1,4,40,512]{3,2,1,0:T(8,128)S(1)}, u32[]{:S(2)}, u32[]{:S(2)}) collective-permute-start(f32[1,4,40,512]{3,2,1,0:T(8,128)S(1)} %maximum_bitcast_fusion), channel_id=1, source_target_pairs={{0,128},{64,192},{128,0},{192,64},{1,129},{65,193},{129,1},{193,65... | collective-permute-start | bytes 983048 | tf_op jit(solution)/shard_map/ppermute | solution.py:357
  67.2 2.5 %collective-permute-start.30 = (f32[1,4,40,512]{3,2,1,0:T(8,128)S(1)}, f32[1,4,40,512]{3,2,1,0:T(8,128)S(1)}, u32[]{:S(2)}, u32[]{:S(2)}) collective-permute-start(f32[1,4,40,512]{3,2,1,0:T(8,128)S(1)} %maximum_bitcast_fusion), channel_id=1, source_target_pairs={{0,192},{64,128},{128,64},{192,0},{1,193},{65,129},{129,65},{193,1... | collective-permute-start | bytes 983048 | tf_op jit(solution)/shard_map/ppermute | solution.py:357
  69.7 6.3 %collective-permute-done.20 = f32[128,512]{1,0:T(8,128)} collective-permute-done((f32[128,512]{1,0:T(8,128)S(1)}, f32[128,512]{1,0:T(8,128)}, u32[]{:S(2)}, u32[]{:S(2)}) %collective-permute-start.20) | collective-permute-done | bytes 262176 | tf_op jit(solution)/shard_map/ppermute | solution.py:357
  76.0 2.8 %collective-permute-start.32 = (f32[1,4,40,512]{3,2,1,0:T(8,128)S(1)}, f32[1,4,40,512]{3,2,1,0:T(8,128)S(1)}, u32[]{:S(2)}, u32[]{:S(2)}) collective-permute-start(f32[1,4,40,512]{3,2,1,0:T(8,128)S(1)} %maximum_bitcast_fusion), channel_id=1, source_target_pairs={{0,64},{64,0},{128,192},{192,128},{1,65},{65,1},{129,193},{193,129... | collective-permute-start | bytes 983048 | tf_op jit(solution)/shard_map/ppermute | solution.py:357
  78.8 1.0 fusion
  79.8 0.6 collective-permute-start.1
  80.4 1.7 %collective-permute-start.2 = (f32[256,512]{1,0:T(8,128)}, f32[256,512]{1,0:T(8,128)S(1)}, u32[]{:S(2)}, u32[]{:S(2)}) collective-permute-start(f32[256,512]{1,0:T(8,128)} %get-tuple-element.31), channel_id=1, source_target_pairs={{0,3},{1,2},{2,1},{3,0},{4,7},{5,6},{6,5},{7,4},{8,11},{9,10},{10,... | collective-permute-start | bytes 1572872 | tf_op jit(solution)/shard_map/ppermute | solution.py:357
  82.1 1.2 broadcast_select_fusion.15
  83.3 1.6 %collective-permute-done.31 = f32[1,4,40,512]{3,2,1,0:T(8,128)S(1)} collective-permute-done((f32[1,4,40,512]{3,2,1,0:T(8,128)S(1)}, f32[1,4,40,512]{3,2,1,0:T(8,128)S(1)}, u32[]{:S(2)}, u32[]{:S(2)}) %collective-permute-start.31) | collective-permute-done | bytes 327712 | tf_op jit(solution)/shard_map/ppermute | solution.py:357
  84.9 0.2 collective-permute-start
  85.1 0.4 collective-permute-done.30
  85.5 1.4 collective-permute-done.32
  86.9 0.1 broadcast_select_fusion.4
  87.0 0.2 broadcast_select_fusion.7
  87.2 0.1 pad_maximum_fusion.own
  87.3 0.1 collective-permute-start.33
  87.4 0.1 pad_maximum_fusion.1.own
  87.5 0.0 copy-start.3
  87.5 0.8 collective-permute-start.23
  88.2 13.4 %collective-permute-done.p1a = f32[256,512]{1,0:T(8,128)S(1)} collective-permute-done((f32[256,512]{1,0:T(8,128)}, f32[256,512]{1,0:T(8,128)S(1)}, u32[]{:S(2)}, u32[]{:S(2)}) %collective-permute-start) | collective-permute-done | bytes 524320 | tf_op jit(solution)/shard_map/ppermute | solution.py:357
  101.7 2.6 %collective-permute-start.3 = (f32[256,512]{1,0:T(8,128)}, f32[256,512]{1,0:T(8,128)S(1)}, u32[]{:S(2)}, u32[]{:S(2)}) collective-permute-start(f32[256,512]{1,0:T(8,128)} %get-tuple-element.32), channel_id=1, source_target_pairs={{0,3},{1,2},{2,1},{3,0},{4,7},{5,6},{6,5},{7,4},{8,11},{9,10},{10,... | collective-permute-start | bytes 1572872 | tf_op jit(solution)/shard_map/ppermute | solution.py:357
  104.3 0.2 collective-permute-start.4
  104.5 0.6 collective-permute-start.5
  105.2 7.1 %collective-permute-done.3.p3b = f32[256,512]{1,0:T(8,128)S(1)} collective-permute-done((f32[256,512]{1,0:T(8,128)}, f32[256,512]{1,0:T(8,128)S(1)}, u32[]{:S(2)}, u32[]{:S(2)}) %collective-permute-start.3) | collective-permute-done | bytes 524320 | tf_op jit(solution)/shard_map/ppermute | solution.py:357
  112.3 0.4 split_rows.1
  112.6 5.0 %collective-permute-done.4.far1 = f32[256,512]{1,0:T(8,128)S(1)} collective-permute-done((f32[256,512]{1,0:T(8,128)S(1)}, f32[256,512]{1,0:T(8,128)S(1)}, u32[]{:S(2)}, u32[]{:S(2)}) %collective-permute-start.4) | collective-permute-done | bytes 524320 | tf_op jit(solution)/shard_map/ppermute | solution.py:357
  117.7 10.4 %collective-permute-done.5.far3 = f32[256,512]{1,0:T(8,128)S(1)} collective-permute-done((f32[256,512]{1,0:T(8,128)S(1)}, f32[256,512]{1,0:T(8,128)S(1)}, u32[]{:S(2)}, u32[]{:S(2)}) %collective-permute-start.5) | collective-permute-done | bytes 524320 | tf_op jit(solution)/shard_map/ppermute | solution.py:357
  128.1 2.5 %update_part.1.u0 = f32[512,256]{1,0:T(8,128)S(1)} custom-call(s32[3]{0:T(128)S(1)} %pad_add_fusion.where_ref, bf16[512,1536]{1,0:T(8,128)(2,1)S(1)} %get-tuple-element.13.ph, bf16[512,1536]{1,0:T(8,128)(2,1)S(1)} %get-tuple-element.14.pl_, f32[256,512]{1,0:T(8,128)S(1)} %collective-permute-done.4.far1, f32[256,512]{1,0:T(8,128)S(1)} %collective-permute-done.5.far3, ...), custom_call_target="tpu_custom_call" | custom-call | flops 1000000000 | bytes 4194304 | tf_op jit(solution)/shard_map/update_part/pallas_call | solution.py:291
  130.5 0.8 collective-permute-start.24
  131.3 4.5 %collective-permute-start.25 = (f32[512,256]{1,0:T(8,128)S(1)}, f32[512,256]{1,0:T(8,128)S(1)}, u32[]{:S(2)}, u32[]{:S(2)}) collective-permute-start(f32[512,256]{1,0:T(8,128)S(1)} %update_part.1.u0), channel_id=1, source_target_pairs={{0,2},{1,3},{2,0},{3,1},{4,6},{5,7},{6,4},{7,5},{8,10},{9,11},{10,... | collective-permute-start | bytes 1572872 | tf_op jit(solution)/shard_map/ppermute | solution.py:357
  135.8 10.5 %factor.1 = (f32[2,512,512]{2,1,0:T(8,128)S(1)}, f32[512,512]{1,0:T(8,128)S(1)}) custom-call(s32[3]{0:T(128)S(1)} %pad_add_fusion.where_ref, f32[4,4,40,512]{3,2,1,0:T(8,128)S(1)} %pad_maximum_fusion.own, f32[4,4,40,512]{3,2,1,0:T(8,128)S(1)} %collective-permute-done.33.other), custom_call_target="tpu_custom_call" | custom-call | flops 5000000000 | bytes 8388608 | tf_op jit(solution)/shard_map/factor/pallas_call | solution.py:232
  146.3 2.3 %collective-permute-done.25.u2 = f32[512,256]{1,0:T(8,128)S(1)} collective-permute-done((f32[512,256]{1,0:T(8,128)S(1)}, f32[512,256]{1,0:T(8,128)S(1)}, u32[]{:S(2)}, u32[]{:S(2)}) %collective-permute-start.25) | collective-permute-done | bytes 524320 | tf_op jit(solution)/shard_map/ppermute | solution.py:357
  148.6 3.1 %collective-permute-done.26.u3 = f32[512,256]{1,0:T(8,128)S(1)} collective-permute-done((f32[512,256]{1,0:T(8,128)S(1)}, f32[512,256]{1,0:T(8,128)S(1)}, u32[]{:S(2)}, u32[]{:S(2)}) %collective-permute-start.26) | collective-permute-done | bytes 524320 | tf_op jit(solution)/shard_map/ppermute | solution.py:357
  151.8 4.8 %solve.1 = f32[512,1024]{1,0:T(8,128)} custom-call(s32[3]{0:T(128)S(1)} %pad_add_fusion.where_ref, f32[512,256]{1,0:T(8,128)S(1)} %update_part.1.u0, f32[512,256]{1,0:T(8,128)S(1)} %collective-permute-done.24.u1, f32[512,256]{1,0:T(8,128)S(1)} %collective-permute-done.25.u2, f32[512,256]{1,0:T(8,128)S(1)} %collective-permute-done.26.u3, ...), custom_call_target="tpu_custom_call" | custom-call | flops 1000000000 | bytes 4194304 | tf_op jit(solution)/shard_map/solve/pallas_call | solution.py:333
  (36 shorter events, 0.2 us)
Async XLA Ops:
  0.0 2.9 %collective-permute-start.9 = (f32[512,512]{1,0:T(8,128)}, f32[512,512]{1,0:T(8,128)S(1)}, u32[]{:S(2)}, u32[]{:S(2)}) collective-permute-start(f32[512,512]{1,0:T(8,128)} %own.1), channel_id=1, source_target_pairs={{0,4},{4,0},{1,5},{5,1},{2,6},{6,2},{3,7},{7,3},{8,12},{12,8},{9,1... | collective-permute-start | bytes 3145736 | tf_op jit(solution)/shard_map/ppermute | solution.py:357
  2.9 1.2 copy-start
  4.1 1.6 %copy-start.2 = (f32[512,1024]{1,0:T(8,128)S(1)}, f32[512,1024]{1,0:T(8,128)}, u32[]{:S(2)}) copy-start(f32[512,1024]{1,0:T(8,128)} %a_ref.3) | copy-start | bytes 6291460
  5.7 5.7 %copy-start.1 = (f32[512,512]{1,0:T(8,128)S(1)}, f32[512,512]{1,0:T(8,128)}, u32[]{:S(2)}) copy-start(f32[512,512]{1,0:T(8,128)} %own.1) | copy-start | bytes 3145732
  7.9 7.0 %collective-permute-start.12 = (f32[160,512]{1,0:T(8,128)S(1)}, f32[160,512]{1,0:T(8,128)S(1)}, u32[]{:S(2)}, u32[]{:S(2)}) collective-permute-start(f32[160,512]{1,0:T(8,128)S(1)} %get-tuple-element.18), channel_id=1, source_target_pairs={{0,3},{1,2},{2,1},{3,0},{4,7},{5,6},{6,5},{7,4}} | collective-permute-start | bytes 983048 | tf_op jit(solution)/shard_map/ppermute | solution.py:357
  8.6 7.0 %collective-permute-start.11 = (f32[160,512]{1,0:T(8,128)S(1)}, f32[160,512]{1,0:T(8,128)}, u32[]{:S(2)}, u32[]{:S(2)}) collective-permute-start(f32[160,512]{1,0:T(8,128)S(1)} %get-tuple-element.17), channel_id=1, source_target_pairs={{0,2},{1,3},{2,0},{3,1},{4,6},{5,7},{6,4},{7,5}} | collective-permute-start | bytes 983048 | tf_op jit(solution)/shard_map/ppermute | solution.py:357
  10.0 5.6 %collective-permute-start.10 = (f32[160,512]{1,0:T(8,128)S(1)}, f32[160,512]{1,0:T(8,128)}, u32[]{:S(2)}, u32[]{:S(2)}) collective-permute-start(f32[160,512]{1,0:T(8,128)S(1)} %get-tuple-element.16), channel_id=1, source_target_pairs={{0,1},{1,0},{2,3},{3,2},{4,5},{5,4},{6,7},{7,6}} | collective-permute-start | bytes 983048 | tf_op jit(solution)/shard_map/ppermute | solution.py:357
  12.2 6.0 %collective-permute-start.8 = (f32[128,512]{1,0:T(8,128)}, f32[128,512]{1,0:T(8,128)}, u32[]{:S(2)}, u32[]{:S(2)}) collective-permute-start(f32[128,512]{1,0:T(8,128)} %get-tuple-element.29), channel_id=1, source_target_pairs={{0,195},{1,194},{2,193},{3,192},{4,199},{5,198},{6,197},{7,196}} | collective-permute-start | bytes 786440 | tf_op jit(solution)/shard_map/ppermute | solution.py:357
  13.6 5.3 %collective-permute-start.6 = (f32[128,512]{1,0:T(8,128)}, f32[128,512]{1,0:T(8,128)}, u32[]{:S(2)}, u32[]{:S(2)}) collective-permute-start(f32[128,512]{1,0:T(8,128)} %get-tuple-element.30), channel_id=1, source_target_pairs={{0,65},{1,64},{2,67},{3,66},{4,69},{5,68},{6,71},{7,70}} | collective-permute-start | bytes 786440 | tf_op jit(solution)/shard_map/ppermute | solution.py:357
  14.9 4.0 %collective-permute-start.7 = (f32[128,512]{1,0:T(8,128)S(1)}, f32[128,512]{1,0:T(8,128)S(1)}, u32[]{:S(2)}, u32[]{:S(2)}) collective-permute-start(f32[128,512]{1,0:T(8,128)S(1)} %get-tuple-element.28), channel_id=1, source_target_pairs={{0,130},{1,131},{2,128},{3,129},{4,134},{5,135},{6,132},{7,133}} | collective-permute-start | bytes 786440 | tf_op jit(solution)/shard_map/ppermute | solution.py:357
  16.8 3.2 %collective-permute-start.15 = (f32[40,512]{1,0:T(8,128)S(1)}, f32[40,512]{1,0:T(8,128)S(1)}, u32[]{:S(2)}, u32[]{:S(2)}) collective-permute-start(f32[40,512]{1,0:T(8,128)S(1)} %get-tuple-element.38), channel_id=1, source_target_pairs={{0,192},{1,193},{2,194},{3,195},{4,196},{5,197},{6,198},{7,199}} | collective-permute-start | bytes 245768 | tf_op jit(solution)/shard_map/ppermute | solution.py:357
  17.5 2.5 %collective-permute-start.13 = (f32[40,512]{1,0:T(8,128)S(1)}, f32[40,512]{1,0:T(8,128)S(1)}, u32[]{:S(2)}, u32[]{:S(2)}) collective-permute-start(f32[40,512]{1,0:T(8,128)S(1)} %get-tuple-element.39), channel_id=1, source_target_pairs={{0,64},{1,65},{2,66},{3,67},{4,68},{5,69},{6,70},{7,71}} | collective-permute-start | bytes 245768 | tf_op jit(solution)/shard_map/ppermute | solution.py:357
  18.2 1.8 %collective-permute-start.14 = (f32[40,512]{1,0:T(8,128)S(1)}, f32[40,512]{1,0:T(8,128)S(1)}, u32[]{:S(2)}, u32[]{:S(2)}) collective-permute-start(f32[40,512]{1,0:T(8,128)S(1)} %get-tuple-element.37), channel_id=1, source_target_pairs={{0,128},{1,129},{2,130},{3,131},{4,132},{5,133},{6,134},{7,135}} | collective-permute-start | bytes 245768 | tf_op jit(solution)/shard_map/ppermute | solution.py:357
  20.1 1.4 collective-permute-start.16
  20.8 0.7 collective-permute-start.17
  21.6 2.0 %collective-permute-start.18 = (f32[168,512]{1,0:T(8,128)S(1)}, f32[168,512]{1,0:T(8,128)S(1)}, u32[]{:S(2)}, u32[]{:S(2)}) collective-permute-start(f32[168,512]{1,0:T(8,128)S(1)} %add_select_fusion.1), channel_id=1, source_target_pairs={{0,8},{24,32},{40,48},{1,9},{25,33},{41,49},{2,10},{26,34},{42,50}... | collective-permute-start | bytes 1032200 | tf_op jit(solution)/shard_map/ppermute | solution.py:357
  22.3 30.9 %collective-permute-start.19 = (f32[168,512]{1,0:T(8,128)S(1)}, f32[168,512]{1,0:T(8,128)S(1)}, u32[]{:S(2)}, u32[]{:S(2)}) collective-permute-start(f32[168,512]{1,0:T(8,128)S(1)} %add_select_fusion.1), channel_id=1, source_target_pairs={{0,56},{24,16},{1,57},{25,17},{2,58},{26,18},{3,59},{27,19},{4,60}... | collective-permute-start | bytes 1032200 | tf_op jit(solution)/shard_map/ppermute | solution.py:357
  53.3 11.5 %collective-permute-start.27 = (f32[1,40,512]{2,1,0:T(8,128)S(1)}, f32[1,40,512]{2,1,0:T(8,128)S(1)}, u32[]{:S(2)}, u32[]{:S(2)}) collective-permute-start(f32[1,40,512]{2,1,0:T(8,128)S(1)} %slice_bitcast_fusion), channel_id=1, source_target_pairs={{0,3},{1,2},{2,1},{3,0},{4,7},{5,6},{6,5},{7,4},{8,11},{9,10},{10,... | collective-permute-start | bytes 245768 | tf_op jit(solution)/shard_map/ppermute | solution.py:357
  55.3 9.5 %collective-permute-start.28 = (f32[1,40,512]{2,1,0:T(8,128)S(1)}, f32[1,40,512]{2,1,0:T(8,128)S(1)}, u32[]{:S(2)}, u32[]{:S(2)}) collective-permute-start(f32[1,40,512]{2,1,0:T(8,128)S(1)} %slice_bitcast_fusion), channel_id=1, source_target_pairs={{0,2},{1,3},{2,0},{3,1},{4,6},{5,7},{6,4},{7,5},{8,10},{9,11},{10,... | collective-permute-start | bytes 245768 | tf_op jit(solution)/shard_map/ppermute | solution.py:357
  56.2 8.6 %collective-permute-start.29 = (f32[1,40,512]{2,1,0:T(8,128)S(1)}, f32[1,40,512]{2,1,0:T(8,128)S(1)}, u32[]{:S(2)}, u32[]{:S(2)}) collective-permute-start(f32[1,40,512]{2,1,0:T(8,128)S(1)} %slice_bitcast_fusion), channel_id=1, source_target_pairs={{0,1},{1,0},{2,3},{3,2},{4,5},{5,4},{6,7},{7,6},{8,9},{9,8},{10,11... | collective-permute-start | bytes 245768 | tf_op jit(solution)/shard_map/ppermute | solution.py:357
  57.5 18.5 %collective-permute-start.20 = (f32[128,512]{1,0:T(8,128)S(1)}, f32[128,512]{1,0:T(8,128)}, u32[]{:S(2)}, u32[]{:S(2)}) collective-permute-start(f32[128,512]{1,0:T(8,128)S(1)} %slice.38), channel_id=1, source_target_pairs={{0,192},{64,128},{128,64},{192,0},{1,193},{65,129},{129,65},{193,1... | collective-permute-start | bytes 786440 | tf_op jit(solution)/shard_map/ppermute | solution.py:357
  62.0 17.8 %collective-permute-start.21 = (f32[128,512]{1,0:T(8,128)S(1)}, f32[128,512]{1,0:T(8,128)}, u32[]{:S(2)}, u32[]{:S(2)}) collective-permute-start(f32[128,512]{1,0:T(8,128)S(1)} %slice.38), channel_id=1, source_target_pairs={{0,128},{64,192},{128,0},{192,64},{1,129},{65,193},{129,1},{193,65... | collective-permute-start | bytes 786440 | tf_op jit(solution)/shard_map/ppermute | solution.py:357
  64.8 15.5 %collective-permute-start.22 = (f32[128,512]{1,0:T(8,128)S(1)}, f32[128,512]{1,0:T(8,128)}, u32[]{:S(2)}, u32[]{:S(2)}) collective-permute-start(f32[128,512]{1,0:T(8,128)S(1)} %slice.38), channel_id=1, source_target_pairs={{0,64},{64,0},{128,192},{192,128},{1,65},{65,1},{129,193},{193,129... | collective-permute-start | bytes 786440 | tf_op jit(solution)/shard_map/ppermute | solution.py:357
  64.9 19.9 %collective-permute-start.31 = (f32[1,4,40,512]{3,2,1,0:T(8,128)S(1)}, f32[1,4,40,512]{3,2,1,0:T(8,128)S(1)}, u32[]{:S(2)}, u32[]{:S(2)}) collective-permute-start(f32[1,4,40,512]{3,2,1,0:T(8,128)S(1)} %maximum_bitcast_fusion), channel_id=1, source_target_pairs={{0,128},{64,192},{128,0},{192,64},{1,129},{65,193},{129,1},{193,65... | collective-permute-start | bytes 983048 | tf_op jit(solution)/shard_map/ppermute | solution.py:357
  67.2 18.3 %collective-permute-start.30 = (f32[1,4,40,512]{3,2,1,0:T(8,128)S(1)}, f32[1,4,40,512]{3,2,1,0:T(8,128)S(1)}, u32[]{:S(2)}, u32[]{:S(2)}) collective-permute-start(f32[1,4,40,512]{3,2,1,0:T(8,128)S(1)} %maximum_bitcast_fusion), channel_id=1, source_target_pairs={{0,192},{64,128},{128,64},{192,0},{1,193},{65,129},{129,65},{193,1... | collective-permute-start | bytes 983048 | tf_op jit(solution)/shard_map/ppermute | solution.py:357
  76.0 10.9 %collective-permute-start.32 = (f32[1,4,40,512]{3,2,1,0:T(8,128)S(1)}, f32[1,4,40,512]{3,2,1,0:T(8,128)S(1)}, u32[]{:S(2)}, u32[]{:S(2)}) collective-permute-start(f32[1,4,40,512]{3,2,1,0:T(8,128)S(1)} %maximum_bitcast_fusion), channel_id=1, source_target_pairs={{0,64},{64,0},{128,192},{192,128},{1,65},{65,1},{129,193},{193,129... | collective-permute-start | bytes 983048 | tf_op jit(solution)/shard_map/ppermute | solution.py:357
  79.8 24.7 %collective-permute-start.1 = (f32[256,512]{1,0:T(8,128)}, f32[256,512]{1,0:T(8,128)S(1)}, u32[]{:S(2)}, u32[]{:S(2)}) collective-permute-start(f32[256,512]{1,0:T(8,128)} %get-tuple-element.31), channel_id=1, source_target_pairs={{0,1},{1,0},{2,3},{3,2},{4,5},{5,4},{6,7},{7,6},{8,9},{9,8},{10,11... | collective-permute-start | bytes 1572872 | tf_op jit(solution)/shard_map/ppermute | solution.py:357
  80.4 23.9 %collective-permute-start.2 = (f32[256,512]{1,0:T(8,128)}, f32[256,512]{1,0:T(8,128)S(1)}, u32[]{:S(2)}, u32[]{:S(2)}) collective-permute-start(f32[256,512]{1,0:T(8,128)} %get-tuple-element.31), channel_id=1, source_target_pairs={{0,3},{1,2},{2,1},{3,0},{4,7},{5,6},{6,5},{7,4},{8,11},{9,10},{10,... | collective-permute-start | bytes 1572872 | tf_op jit(solution)/shard_map/ppermute | solution.py:357
  84.9 16.8 %collective-permute-start = (f32[256,512]{1,0:T(8,128)}, f32[256,512]{1,0:T(8,128)S(1)}, u32[]{:S(2)}, u32[]{:S(2)}) collective-permute-start(f32[256,512]{1,0:T(8,128)} %get-tuple-element.32), channel_id=1, source_target_pairs={{0,1},{1,0},{2,3},{3,2},{4,5},{5,4},{6,7},{7,6},{8,9},{9,8},{10,11... | collective-permute-start | bytes 1572872 | tf_op jit(solution)/shard_map/ppermute | solution.py:357
  87.3 48.5 %collective-permute-start.33 = (f32[4,4,40,512]{3,2,1,0:T(8,128)S(1)}, f32[4,4,40,512]{3,2,1,0:T(8,128)S(1)}, u32[]{:S(2)}, u32[]{:S(2)}) collective-permute-start(f32[4,4,40,512]{3,2,1,0:T(8,128)S(1)} %pad_maximum_fusion.own), channel_id=1, source_target_pairs={{0,4},{4,0},{1,5},{5,1},{2,6},{6,2},{3,7},{7,3},{8,12},{12,8},{9,1... | collective-permute-start | bytes 3932168 | tf_op jit(solution)/shard_map/ppermute | solution.py:357
  87.5 40.6 %copy-start.3 = (f32[512,1024]{1,0:T(8,128)S(1)}, f32[512,1024]{1,0:T(8,128)}, u32[]{:S(2)}) copy-start(f32[512,1024]{1,0:T(8,128)} %a_ref.3) | copy-start | bytes 6291460
  87.5 40.6 %collective-permute-start.23 = (f32[512,512]{1,0:T(8,128)S(1)}, f32[512,512]{1,0:T(8,128)S(1)}, u32[]{:S(2)}, u32[]{:S(2)}) collective-permute-start(f32[512,512]{1,0:T(8,128)S(1)} %pad_maximum_fusion.1.own), channel_id=1, source_target_pairs={{0,4},{4,0},{1,5},{5,1},{2,6},{6,2},{3,7},{7,3},{8,12},{12,8},{9,1... | collective-permute-start | bytes 3145736 | tf_op jit(solution)/shard_map/ppermute | solution.py:357
  101.7 10.6 %collective-permute-start.3 = (f32[256,512]{1,0:T(8,128)}, f32[256,512]{1,0:T(8,128)S(1)}, u32[]{:S(2)}, u32[]{:S(2)}) collective-permute-start(f32[256,512]{1,0:T(8,128)} %get-tuple-element.32), channel_id=1, source_target_pairs={{0,3},{1,2},{2,1},{3,0},{4,7},{5,6},{6,5},{7,4},{8,11},{9,10},{10,... | collective-permute-start | bytes 1572872 | tf_op jit(solution)/shard_map/ppermute | solution.py:357
  104.3 13.4 %collective-permute-start.4 = (f32[256,512]{1,0:T(8,128)S(1)}, f32[256,512]{1,0:T(8,128)S(1)}, u32[]{:S(2)}, u32[]{:S(2)}) collective-permute-start(f32[256,512]{1,0:T(8,128)S(1)} %collective-permute-done.2.p3a), channel_id=1, source_target_pairs={{0,1},{1,0},{2,3},{3,2},{4,5},{5,4},{6,7},{7,6},{8,9},{9,8},{10,11... | collective-permute-start | bytes 1572872 | tf_op jit(solution)/shard_map/ppermute | solution.py:357
  104.5 23.5 %collective-permute-start.5 = (f32[256,512]{1,0:T(8,128)S(1)}, f32[256,512]{1,0:T(8,128)S(1)}, u32[]{:S(2)}, u32[]{:S(2)}) collective-permute-start(f32[256,512]{1,0:T(8,128)S(1)} %collective-permute-done.p1a), channel_id=1, source_target_pairs={{0,3},{1,2},{2,1},{3,0},{4,7},{5,6},{6,5},{7,4},{8,11},{9,10},{10,... | collective-permute-start | bytes 1572872 | tf_op jit(solution)/shard_map/ppermute | solution.py:357
  130.5 15.8 %collective-permute-start.24 = (f32[512,256]{1,0:T(8,128)S(1)}, f32[512,256]{1,0:T(8,128)S(1)}, u32[]{:S(2)}, u32[]{:S(2)}) collective-permute-start(f32[512,256]{1,0:T(8,128)S(1)} %update_part.1.u0), channel_id=1, source_target_pairs={{0,1},{1,0},{2,3},{3,2},{4,5},{5,4},{6,7},{7,6},{8,9},{9,8},{10,11... | collective-permute-start | bytes 1572872 | tf_op jit(solution)/shard_map/ppermute | solution.py:357
  131.3 17.4 %collective-permute-start.25 = (f32[512,256]{1,0:T(8,128)S(1)}, f32[512,256]{1,0:T(8,128)S(1)}, u32[]{:S(2)}, u32[]{:S(2)}) collective-permute-start(f32[512,256]{1,0:T(8,128)S(1)} %update_part.1.u0), channel_id=1, source_target_pairs={{0,2},{1,3},{2,0},{3,1},{4,6},{5,7},{6,4},{7,5},{8,10},{9,11},{10,... | collective-permute-start | bytes 1572872 | tf_op jit(solution)/shard_map/ppermute | solution.py:357
  135.8 16.0 %collective-permute-start.26 = (f32[512,256]{1,0:T(8,128)S(1)}, f32[512,256]{1,0:T(8,128)S(1)}, u32[]{:S(2)}, u32[]{:S(2)}) collective-permute-start(f32[512,256]{1,0:T(8,128)S(1)} %update_part.1.u0), channel_id=1, source_target_pairs={{0,3},{1,2},{2,1},{3,0},{4,7},{5,6},{6,5},{7,4},{8,11},{9,10},{10,... | collective-permute-start | bytes 1572872 | tf_op jit(solution)/shard_map/ppermute | solution.py:357
